TPU v7x, 32 devices: a whole 2x2x4 slice. The times are simulated.
32 devices in a mesh: rep: 4 (over x, y), dp: 8 (over z, core).
Axes of the slice: x: 2, y: 2, z: 4, core: 2. Of those that a mesh axis runs over, the one named last changes fastest.
Arguments:
- x: bfloat16 [32, 2048, 1024], P(('rep', 'dp')), parts along dimension 0
- dy: bfloat16 [32, 2048, 1024], P(('rep', 'dp')), parts along dimension 0
- w_gate: bfloat16 [2, 1024, 4096], replicated
- w_up: bfloat16 [2, 1024, 4096], replicated
- w_down: bfloat16 [2, 4096, 1024], replicated
- m_w_gate: float32 [2, 1024, 4096], replicated
- m_w_up: float32 [2, 1024, 4096], replicated
- m_w_down: float32 [2, 4096, 1024], replicated
- v_w_gate: float32 [2, 1024, 4096], replicated
- v_w_up: float32 [2, 1024, 4096], replicated
- v_w_down: float32 [2, 4096, 1024], replicated
Outputs:
- output 1: bfloat16 [8, 1024, 4096], P('rep'), parts along dimension 0
- output 2: bfloat16 [8, 1024, 4096], P('rep'), parts along dimension 0
- output 3: bfloat16 [8, 4096, 1024], P('rep'), parts along dimension 0
- output 4: float32 [8, 1024, 4096], P('rep'), parts along dimension 0
- output 5: float32 [8, 1024, 4096], P('rep'), parts along dimension 0
- output 6: float32 [8, 4096, 1024], P('rep'), parts along dimension 0
- output 7: float32 [8, 1024, 4096], P('rep'), parts along dimension 0
- output 8: float32 [8, 1024, 4096], P('rep'), parts along dimension 0
- output 9: float32 [8, 4096, 1024], P('rep'), parts along dimension 0
There are 4 independent parts. A program takes and returns all parts, laid end to end along the dimension named above; an argument that names none is the same for every part.
All inputs are finite; a program needn't handle non-finite values.
Results may differ from a plain program's by a relative error of at most 0.022.
Values are sent between devices in bfloat16 or wider.
A program may use at most 2.75 GiB of HBM per device.

v0:
```python
import jax
import jax.numpy as jnp
from jax import lax
from jax.sharding import PartitionSpec as P

NAMES = ("w_gate", "w_up", "w_down")


def matmul(a, w):
    return jnp.dot(a, w, preferred_element_type=jnp.float32).astype(jnp.bfloat16)


def normed(h):
    wide = h.astype(jnp.float32)
    scale = lax.rsqrt(jnp.mean(wide**2, -1, keepdims=True) + 1e-6)
    return (wide * scale).astype(jnp.bfloat16)


def layer(h, w):
    a = normed(h)
    gate = jnp.dot(a, w["w_gate"], preferred_element_type=jnp.float32)
    up = jnp.dot(a, w["w_up"], preferred_element_type=jnp.float32)
    return h + matmul((jax.nn.silu(gate) * up).astype(jnp.bfloat16), w["w_down"])


def adamw(w, m, v, g):
    m = 0.9 * m + 0.1 * g
    v = 0.95 * v + 0.05 * g * g
    step = m * lax.rsqrt(v + 1e-8) + 0.1 * w
    return (w - 0.02 * step).astype(jnp.bfloat16), m, v


def clipped(gradients, sum_of_squares, count):
    factor = jnp.minimum(1.0, 0.5 * lax.rsqrt(sum_of_squares / count + 1e-30))
    return [g * factor for g in gradients]


def solution(mesh):
    def step(x, dy, *arrays):
        weights, m, v = (arrays[i : i + 3] for i in (0, 3, 6))
        layers = weights[0].shape[0]
        h, kept = x[0], []
        for number in range(layers):
            kept.append(h)
            h = layer(h, {name: w[number] for name, w in zip(NAMES, weights, strict=True)})
        by_h, summed = dy[0], [None] * layers
        for number in reversed(range(layers)):
            _, back = jax.vjp(lambda w, h: layer(h, w), {name: w[number] for name, w in zip(NAMES, weights, strict=True)}, kept[number])
            by_w, by_h = back(by_h)
            summed[number] = [lax.psum(by_w[name], "dp") for name in NAMES]
        gradients = [jnp.stack([summed[number][i] for number in range(layers)]).astype(jnp.float32) for i in range(3)]
        gradients = clipped(gradients, sum(jnp.sum(g * g) for g in gradients), sum(g.size for g in gradients))
        new = [adamw(w.astype(jnp.float32), m, v, g) for w, m, v, g in zip(weights, m, v, gradients, strict=True)]
        return tuple(one[which] for which in range(3) for one in new)

    return jax.shard_map(
        step,
        mesh=mesh,
        in_specs=(P(("rep", "dp"), None, None),) * 2 + (P(None, None, None),) * 9,
        out_specs=(P("rep", None, None),) * 9,
        check_vma=False,
    )
```

profile of v0, /device:TPU:0, one launch (start us, length us, event | category | flops | bytes accessed | tf_op | source)
XLA Modules:
  0.0 1636.0 jit_solution(11464796666830762889)
XLA Ops:
  7.2 0.0 all-reduce.3.cloned.1.call-start
  7.2 6.6 copy.20
  13.8 3.1 fusion.36
  16.9 0.0 copy-start.8
  16.9 6.5 copy.21
  23.4 0.0 copy-start.5
  23.4 24.5 %convolution_convert_fusion.1 = bf16[2048,4096]{1,0:T(8,128)(2,1)} fusion(bf16[2,4096,1024]{2,1,0:T(8,128)(2,1)} %param.15, bf16[1,2048,1024]{2,1,0:T(8,128)(2,1)} %param.12), kind=kOutput, calls=%fused_computation.64 | convolution fusion | flops 17188257792 | bytes 29360128 | tf_op jit(solution)/shard_map/transpose(jvp())/dot_general | solution.py:10
  47.9 0.0 copy-done.5
  47.9 23.6 %fusion.56 = f32[2048,4096]{1,0:T(8,128)} fusion(bf16[2,1024,4096]{2,1,0:T(8,128)(2,1)} %param.13, bf16[1,2048,1024]{2,1,0:T(8,128)(2,1)S(1)} %copy-done.5, f32[2048]{0:T(1024)S(1)} %add_rsqrt_fusion), kind=kOutput, calls=%fused_computation.92 | convolution fusion | flops 17186160640 | bytes 46145536 | tf_op jit(solution)/shard_map/dot_general | solution.py:21
  71.5 0.0 copy-done.8
  71.5 38.6 %multiply_convert_fusion.1 = (bf16[2048,4096]{1,0:T(8,128)(2,1)}, f32[2048,4096]{1,0:T(8,128)}) fusion(f32[2048,4096]{1,0:T(8,128)} %fusion.56, bf16[2,1024,4096]{2,1,0:T(8,128)(2,1)} %param.14, bf16[1,2048,1024]{2,1,0:T(8,128)(2,1)} %param.11, f32[2048]{0:T(1024)S(1)} %add_rsqrt_fusion), kind=kOutput, calls=%fused_computation.53 | convolution fusion | flops 17236492288 | bytes 96477184 | tf_op jit(solution)/shard_map/dot_general | solution.py:22
  110.1 23.5 %fusion.40 = (f32[2048]{0:T(1024)S(1)}, bf16[2048,1024]{0,1:T(8,128)(2,1)S(1)}) fusion(bf16[2048,4096]{1,0:T(8,128)(2,1)} %get-tuple-element.24, bf16[2,4096,1024]{2,1,0:T(8,128)(2,1)} %param.15, bf16[1,2048,1024]{1,2,0:T(8,128)(2,1)} %copy.20), kind=kOutput, calls=%fused_computation.76 | convolution fusion | flops 17190352896 | bytes 33562624 | tf_op jit(solution)/shard_map/dot_general | solution.py:10
  133.7 0.0 copy-start.6
  133.7 0.0 copy-start.3
  133.7 0.6 copy-done.6
  134.3 1.4 copy-done.3
  135.6 23.6 %fusion.43 = f32[2048,4096]{1,0:T(8,128)} fusion(bf16[2,1024,4096]{2,1,0:T(8,128)(2,1)} %param.14, bf16[2048,1024]{0,1:T(8,128)(2,1)S(1)} %get-tuple-element.27, f32[2048]{0:T(1024)S(1)} %fusion.86), kind=kOutput, calls=%fused_computation.79 | convolution fusion | flops 17186160640 | bytes 46145536 | tf_op jit(solution)/shard_map/jvp()/dot_general | solution.py:22
  159.2 46.6 %fusion.20 = (bf16[2048,4096]{1,0:T(8,128)(2,1)}, f32[2048,4096]{1,0:T(8,128)}) fusion(f32[2048,4096]{1,0:T(8,128)} %fusion.43, bf16[2048,4096]{1,0:T(8,128)(2,1)} %convolution_convert_fusion.1, bf16[2,1024,4096]{2,1,0:T(8,128)(2,1)} %param.13, bf16[2048,1024]{0,1:T(8,128)(2,1)} %copy-done.3, f32[2048]{0:T(1024)S(1)} %fusion.86), kind=kOutput, calls=%fused_computation.41 | convolution fusion | flops 17286823936 | bytes 113254400 | tf_op jit(solution)/shard_map/jvp()/dot_general | solution.py:21
  205.8 27.2 %fusion.33 = bf16[2048,1024]{0,1:T(8,128)(2,1)} fusion(bf16[2048,4096]{1,0:T(8,128)(2,1)} %convolution_convert_fusion.1, bf16[2,1024,4096]{2,1,0:T(8,128)(2,1)} %param.14, f32[2048,4096]{1,0:T(8,128)} %get-tuple-element.29), kind=kOutput, calls=%fused_computation.57 | convolution fusion | flops 17230200832 | bytes 62914560 | tf_op jit(solution)/shard_map/transpose(jvp())/dot_general | solution.py:22
  233.0 26.7 %convert_bitcast_fusion.2 = bf16[1,1024,4096]{2,1,0:T(8,128)(2,1)} fusion(bf16[2048,4096]{1,0:T(8,128)(2,1)} %convolution_convert_fusion.1, bf16[2048,1024]{0,1:T(8,128)(2,1)} %copy-done.3, f32[2048]{0:T(1024)S(1)} %fusion.86, f32[2048,4096]{1,0:T(8,128)} %get-tuple-element.29), kind=kOutput, calls=%fused_computation.96 | convolution fusion | flops 17240686592 | bytes 62922752 | tf_op jit(solution)/shard_map/transpose(jvp())/dot_general | solution.py:22
  259.6 0.0 copy-start.4
  259.6 30.9 %convert_bitcast_fusion = bf16[1,4096,1024]{2,1,0:T(8,128)(2,1)} fusion(f32[2048,4096]{1,0:T(8,128)} %fusion.43, bf16[1,2048,1024]{2,1,0:T(8,128)(2,1)} %param.12, f32[2048,4096]{1,0:T(8,128)} %get-tuple-element.29), kind=kOutput, calls=%fused_computation.94 | convolution fusion | flops 17234395136 | bytes 79691776 | tf_op jit(solution)/shard_map/transpose(jvp())/dot_general | solution.py:10
  290.5 0.0 copy-done.4
  290.5 21.6 %convert_bitcast_fusion.4 = bf16[1,1024,4096]{2,1,0:T(8,128)(2,1)} fusion(bf16[2048,4096]{1,0:T(8,128)(2,1)} %get-tuple-element.28, bf16[2048,1024]{0,1:T(8,128)(2,1)S(1)} %copy-done.4, f32[2048]{0:T(1024)S(1)} %fusion.86), kind=kOutput, calls=%fused_computation.98 | convolution fusion | flops 17186160640 | bytes 29368320 | tf_op jit(solution)/shard_map/transpose(jvp())/dot_general | solution.py:21
  312.2 0.0 copy-start.7
  312.2 0.0 copy-start.1
  312.2 25.4 %fusion.42 = (f32[2048]{0:T(1024)S(1)}, bf16[2048,1024]{0,1:T(8,128)(2,1)}) fusion(bf16[2048,1024]{0,1:T(8,128)(2,1)S(1)} %copy-done.4, bf16[2048,1024]{0,1:T(8,128)(2,1)} %fusion.33, bf16[2048,4096]{1,0:T(8,128)(2,1)} %get-tuple-element.28, bf16[2,1024,4096]{2,1,0:T(8,128)(2,1)} %param.13), kind=kOutput, calls=%fused_computation.78 | convolution fusion | flops 17190352896 | bytes 37756928 | tf_op jit(solution)/shard_map/transpose(jvp())/dot_general | solution.py:21
  337.6 0.0 copy-done.7
  337.6 0.0 copy-done.1
  337.6 6.0 fusion.71
  343.6 25.0 %convolution_convert_fusion = bf16[2048,4096]{1,0:T(8,128)(2,1)} fusion(bf16[2048,1024]{0,1:T(8,128)(2,1)} %fusion.71, bf16[2,4096,1024]{2,1,0:T(8,128)(2,1)} %param.15), kind=kOutput, calls=%fused_computation.63 | convolution fusion | flops 17188257792 | bytes 29360128 | tf_op jit(solution)/shard_map/transpose(jvp())/dot_general | solution.py:10
  368.6 0.0 copy-start.2
  368.6 0.0 copy-start.9
  368.6 24.4 %convert_bitcast_fusion.1 = bf16[1,4096,1024]{2,1,0:T(8,128)(2,1)} fusion(bf16[2048,4096]{1,0:T(8,128)(2,1)} %get-tuple-element.24, bf16[2048,1024]{0,1:T(8,128)(2,1)} %fusion.71), kind=kOutput, calls=%fused_computation.95 | convolution fusion | flops 17184063488 | bytes 29360128 | tf_op jit(solution)/shard_map/transpose(jvp())/dot_general | solution.py:10
  393.0 0.0 copy-done.2
  393.0 0.0 copy-done.9
  393.0 25.5 %convert_bitcast_fusion.3 = bf16[1,1024,4096]{2,1,0:T(8,128)(2,1)} fusion(bf16[2048,4096]{1,0:T(8,128)(2,1)} %convolution_convert_fusion, f32[2048,4096]{1,0:T(8,128)} %fusion.56, bf16[1,2048,1024]{1,2,0:T(8,128)(2,1)S(1)} %copy-done.2, f32[2048]{0:T(1024)S(1)} %copy-done.9), kind=kOutput, calls=%fused_computation.97 | convolution fusion | flops 17240686592 | bytes 62922752 | tf_op jit(solution)/shard_map/transpose(jvp())/dot_general | solution.py:22
  418.5 37.1 %convert_bitcast_fusion.5 = bf16[1,1024,4096]{2,1,0:T(8,128)(2,1)} fusion(f32[2048,4096]{1,0:T(8,128)} %fusion.56, f32[2048,4096]{1,0:T(8,128)} %get-tuple-element.25, bf16[2048,4096]{1,0:T(8,128)(2,1)} %convolution_convert_fusion, bf16[1,2048,1024]{1,2,0:T(8,128)(2,1)} %copy.20, f32[2048]{0:T(1024)S(1)} %copy-done.9), kind=kOutput, calls=%fused_computation.99 | convolution fusion | flops 17282629632 | bytes 96477184 | tf_op jit(solution)/shard_map/transpose(jvp())/dot_general | solution.py:21
  455.6 0.0 all-reduce.3.cloned.1.call-update
  455.6 965.2 %all-reduce.3.cloned.1.call-done = (bf16[1,1024,4096]{2,1,0:T(8,128)(2,1)}, bf16[1,1024,4096]{2,1,0:T(8,128)(2,1)}, bf16[1,1024,4096]{2,1,0:T(8,128)(2,1)}, bf16...) async-done(((bf16[1,1024,4096]{2,1,0:T(8,128)(2,1)}, bf16[1,1024,4096]{2,1,0:T(8,128)(2,1)}, ...) | async-done | bytes 50331664 | tf_op jit(solution)/shard_map/psum | solution.py:50
  1420.8 0.0 slice-start
  1420.8 0.0 copy-start
  1420.8 0.0 slice-start.1
  1420.8 11.5 fusion.10
  1432.3 0.0 slice-done
  1432.3 0.0 copy-done
  1432.3 0.0 slice-done.1
  1432.3 9.3 fusion.11
  1442.9 10.9 fusion.12
  1454.5 58.0 %fusion.18 = (bf16[2,4096,1024]{2,1,0:T(8,128)(2,1)}, f32[2,4096,1024]{2,1,0:T(8,128)}, f32[2,4096,1024]{2,1,0:T(8,128)}) fusion(bf16[2,4096,1024]{2,1,0:T(8,128)(2,1)} %param.15, f32[]{:T(128)S(6)} %min_shard_map.3, bf16[1,4096,1024]{2,1,0:T(8,128)(2,1)} %get-tuple-element.13, bf16[1,4096,1024]{2,1,0:T(8,128)(2,1)} %get-tuple-element.14, ...), kind=kLoop, calls=%fused_computation.39 | loop fusion | flops 167772160 | bytes 184549376 | tf_op jit(solution)/shard_map/convert_element_type | solution.py:30
  1512.4 116.3 %fusion.8 = (bf16[2,1024,4096]{2,1,0:T(8,128)(2,1)}, f32[2,1024,4096]{2,1,0:T(8,128)}, f32[2,1024,4096]{2,1,0:T(8,128)}, bf16[2,1024,4096]{2,1,0:T(8,128)(2,1)},...) fusion(bf16[2,1024,4096]{2,1,0:T(8,128)(2,1)} %param.13, f32[]{:T(128)S(6)} %min_shard_map.3, ...), kind=kLoop, calls=%fused_computation.29 | loop fusion | flops 335544320 | bytes 369098752 | tf_op jit(solution)/shard_map/convert_element_type | solution.py:30
  (4 shorter events, 0.0 us)
Async XLA Ops:
  7.2 1413.6 %all-reduce.3.cloned.1.call-start = ((), (), s32[]{:S(2)}) async-start(), calls=%async_computation | async-start | bytes 100663296 | tf_op jit(solution)/shard_map/psum | solution.py:50
  16.9 54.6 %copy-start.8 = (f32[2048]{0:T(1024)}, f32[2048]{0:T(1024)S(1)}, u32[]{:S(2)}) copy-start(f32[2048]{0:T(1024)S(1)} %add_rsqrt_fusion) | copy-start | bytes 24580
  23.4 24.5 %copy-start.5 = (bf16[1,2048,1024]{2,1,0:T(8,128)(2,1)S(1)}, bf16[1,2048,1024]{2,1,0:T(8,128)(2,1)}, u32[]{:S(2)}) copy-start(bf16[1,2048,1024]{2,1,0:T(8,128)(2,1)} %param.11) | copy-start | bytes 12582916
  133.7 0.6 copy-start.6
  133.7 1.9 copy-start.3
  259.6 30.9 %copy-start.4 = (bf16[2048,1024]{0,1:T(8,128)(2,1)S(1)}, bf16[2048,1024]{0,1:T(8,128)(2,1)}, u32[]{:S(2)}) copy-start(bf16[2048,1024]{0,1:T(8,128)(2,1)} %copy-done.3) | copy-start | bytes 12582916
  312.2 25.4 %copy-start.7 = (f32[2048]{0:T(1024)S(1)}, f32[2048]{0:T(1024)}, u32[]{:S(2)}) copy-start(f32[2048]{0:T(1024)} %copy-done.6) | copy-start | bytes 24580
  312.2 25.4 %copy-start.1 = (bf16[1,2048,1024]{1,2,0:T(8,128)(2,1)S(1)}, bf16[1,2048,1024]{1,2,0:T(8,128)(2,1)}, u32[]{:S(2)}) copy-start(bf16[1,2048,1024]{1,2,0:T(8,128)(2,1)} %copy.21) | copy-start | bytes 12582916
  368.6 24.4 %copy-start.2 = (bf16[1,2048,1024]{1,2,0:T(8,128)(2,1)S(1)}, bf16[1,2048,1024]{1,2,0:T(8,128)(2,1)}, u32[]{:S(2)}) copy-start(bf16[1,2048,1024]{1,2,0:T(8,128)(2,1)} %copy.20) | copy-start | bytes 12582916
  368.6 24.4 %copy-start.9 = (f32[2048]{0:T(1024)S(1)}, f32[2048]{0:T(1024)}, u32[]{:S(2)}) copy-start(f32[2048]{0:T(1024)} %copy-done.8) | copy-start | bytes 24580
  1420.8 11.5 slice-start
  1420.8 11.5 copy-start
  1420.8 11.5 slice-start.1
Sparse Core Ops, SparseCore 0:
  455.8 964.9 all-reduce.2
where the time goes:
time: 1640 us
  waiting for transfers between devices  965 us (59%)
  matrix products  424 us (26%)
  other arithmetic  215 us (13%)
  between operations  16.6 us (1%)
    psum x1, waiting for transfers between devices, step(): summed[number] = [lax.psum(by_w[name], 'dp') for name in NAMES]  965 us
    convert_element_type x2, other arithmetic, adamw(): return ((w - 0.02 * step).astype(jnp.bfloat16), m, v)  174 us
    dot_general x5, matrix products, layer(): gate = jnp.dot(a, w['w_gate'], preferred_element_type=jnp.float32)  154 us
    dot_general x5, matrix products, layer(): up = jnp.dot(a, w['w_up'], preferred_element_type=jnp.float32)  142 us
    dot_general x5, matrix products, matmul(): jnp.dot(a, w, preferred_element_type=jnp.float32).astype(jnp.bfloat16)  128 us
  transfers between devices with their start and end apart: 1, of which 1 were waited for; matrix products, arithmetic and copies ran while one was open for 0% of the time, Pallas kernels for 0%

commit v1 on v0

v1 whole, which is shorter than its diff:
```python
import functools

import jax
import jax.numpy as jnp
from jax import lax
from jax.experimental import pallas as pl
from jax.experimental.pallas import tpu as pltpu
from jax.sharding import PartitionSpec as P

MESH = pl.DeviceIdType.MESH
CHIPS = 4
PARTS = 8
F32, BF16 = jnp.float32, jnp.bfloat16


def dot(a, b):
    return jnp.dot(a, b, preferred_element_type=F32)


def dot_nt(a, b):
    return lax.dot_general(a, b, (((1,), (1,)), ((), ())), preferred_element_type=F32)


def inverse_size(wide):
    return lax.rsqrt(jnp.mean(wide * wide, -1, keepdims=True) + 1e-6)


def gradients_kernel(
    sizes,
    x_ref, dy_ref, wg_ref, wu_ref, wd_ref,
    g_ref, own_ref, pair_ref, chain_ref, ssq_ref, h_ref,
    a, at, up, upt, acc, wgu, wd, hid, dgu, gb, st, out, ssq,
    w_sem, io_sem, pair_send, own_sem, pair_recv, ld_sem, chain_send, chain_recv, fin_sem, pass_send, pass_recv, mate_send, mate_recv, ssq_send, ssq_recv,
):
    T, D, FS, RT, RD = sizes
    NS = 2 * PARTS
    half, quarter = D // 2, D // 4
    dp = lax.axis_index("dp")
    z, c = dp // 2, dp % 2
    mate = dp + 1 - 2 * c
    last = CHIPS - 1

    barrier = pltpu.get_barrier_semaphore()
    for k in range(1, 2 * CHIPS):
        pl.semaphore_signal(barrier, inc=1, device_id={"dp": (dp + k) % (2 * CHIPS)}, device_id_type=MESH)

    def weight_copies(w):
        layer = jnp.where((w >= PARTS) & (w < 2 * PARTS), 1, 0)
        columns = pl.ds(pl.multiple_of((w % PARTS) * FS, FS), FS)
        slot = w % 2
        return (
            pltpu.make_async_copy(wg_ref.at[layer, :, columns], wgu.at[slot, :, pl.ds(0, FS)], w_sem.at[slot, 0]),
            pltpu.make_async_copy(wu_ref.at[layer, :, columns], wgu.at[slot, :, pl.ds(FS, FS)], w_sem.at[slot, 1]),
            pltpu.make_async_copy(wd_ref.at[layer, columns, :], wd.at[slot], w_sem.at[slot, 2]),
        )

    def fetch(w):
        for copy in weight_copies(w):
            copy.start()

    def fetched(w):
        for copy in weight_copies(w):
            copy.wait()

    def rows_of(r, size):
        return pl.ds(pl.multiple_of(r * size, size), size)

    def over_rows(total, size, body):
        lax.fori_loop(0, total // size, lambda r, _: (body(rows_of(r, size)), 0)[1], 0)

    fetch(0)
    load_x = pltpu.make_async_copy(x_ref.at[0], a, io_sem.at[0])
    load_x.start()
    load_x2 = pltpu.make_async_copy(x_ref.at[0], up, io_sem.at[1])
    load_x2.start()
    ssq[...] = jnp.zeros_like(ssq)
    load_x.wait()

    def norm_in_place(rows):
        wide = a[rows, :].astype(F32)
        a[rows, :] = (wide * inverse_size(wide)).astype(BF16)

    over_rows(T, RD, norm_in_place)

    def forward(j, _):
        slot = j % 2
        fetched(j)
        fetch(j + 1)

        def tile(rows):
            gu = dot(a[rows, :], wgu[slot])
            gate, lift = gu[:, :FS], gu[:, FS:]
            hidden = (gate * jax.nn.sigmoid(gate) * lift).astype(BF16)
            acc[rows, :] = jnp.where(j > 0, acc[rows, :], 0.0) + dot(hidden, wd[slot])

        over_rows(T, RT, tile)
        return 0

    lax.fori_loop(0, PARTS, forward, 0)

    load_x2.wait()

    def close_forward(rows):
        h = up[rows, :].astype(F32) + acc[rows, :].astype(BF16).astype(F32)
        h = h.astype(BF16)
        up[rows, :] = h
        wide = h.astype(F32)
        a[rows, :] = (wide * inverse_size(wide)).astype(BF16)
        acc[rows, :] = jnp.zeros((RD, D), F32)

    over_rows(T, RD, close_forward)
    save_h = pltpu.make_async_copy(up, h_ref, io_sem.at[0])
    save_h.start()

    def turn(source, target):
        def tile(rows):
            target[:, rows] = source[rows, :].T

        over_rows(T, RD, tile)

    turn(a, at)
    save_h.wait()
    load_dy = pltpu.make_async_copy(dy_ref.at[0], up, io_sem.at[1])
    load_dy.start()
    load_dy.wait()
    turn(up, upt)

    pl.semaphore_wait(barrier, 2 * CHIPS - 1)

    def cross_layers():
        load_h = pltpu.make_async_copy(h_ref, dgu, io_sem.at[0])
        load_h.start()
        again = pltpu.make_async_copy(x_ref.at[0], a, io_sem.at[1])
        again.start()
        load_h.wait()

        def tile(rows):
            wide = dgu[rows, :].astype(F32)
            scale = inverse_size(wide)
            da = acc[rows, :].astype(BF16).astype(F32)
            along = jnp.sum(da * wide, -1, keepdims=True) * (1.0 / D)
            dh = (scale * da - wide * (scale * scale * scale * along)).astype(BF16)
            up[rows, :] = (up[rows, :].astype(F32) + dh.astype(F32)).astype(BF16)

        over_rows(T, RD, tile)
        again.wait()
        over_rows(T, RD, norm_in_place)
        turn(a, at)
        turn(up, upt)

    def mine(rows_half):
        return pl.ds(pl.multiple_of(rows_half * half, half), half)

    def pair_copy(i):
        return pltpu.make_async_remote_copy(
            src_ref=gb.at[i % 2, :, mine(1 - c), :], dst_ref=pair_ref.at[i], send_sem=pair_send.at[i % 2], recv_sem=pair_recv.at[i],
            device_id={"dp": mate}, device_id_type=MESH,
        )

    def own_copy(i):
        return pltpu.make_async_copy(gb.at[i % 2, :, mine(c), :], own_ref.at[i], own_sem.at[i % 2])

    class Way:
        def __init__(self, d):
            self.d = d
            self.place = z if d == 0 else last - z
            self.step = 2 if d == 0 else -2
            self.small = pl.ds(d * quarter, quarter)
            self.rows = pl.ds(pl.multiple_of((2 * c + d) * quarter, quarter), quarter)

        def loads(self, i):
            d = self.d
            return (
                pltpu.make_async_copy(own_ref.at[i, :, self.small, :], st.at[d, 0], ld_sem.at[d, 0]),
                pltpu.make_async_copy(pair_ref.at[i, :, self.small, :], st.at[d, 1], ld_sem.at[d, 1]),
                pltpu.make_async_copy(chain_ref.at[d, i], st.at[d, 2], ld_sem.at[d, 2]),
            )

        def hop(self, i):
            d = self.d
            return pltpu.make_async_remote_copy(
                src_ref=out.at[d, i % 2], dst_ref=chain_ref.at[d, i], send_sem=chain_send.at[d, i % 2], recv_sem=chain_recv.at[d, i],
                device_id={"dp": (dp + self.step) % (2 * CHIPS)}, device_id_type=MESH,
            )

        def keep(self, i):
            return pltpu.make_async_copy(out.at[self.d, i % 2], g_ref.at[i, :, self.rows, :], fin_sem.at[i % 2])

        def spread(self, i):
            return pltpu.make_async_remote_copy(
                src_ref=g_ref.at[i, :, self.rows, :], dst_ref=g_ref.at[i, :, self.rows, :], send_sem=pass_send.at[self.d, i], recv_sem=pass_recv.at[self.d, i],
                device_id={"dp": (dp - self.step + 2 * CHIPS) % (2 * CHIPS)}, device_id_type=MESH,
            )

        def share(self, i):
            return pltpu.make_async_remote_copy(
                src_ref=g_ref.at[i, :, self.rows, :], dst_ref=g_ref.at[i, :, self.rows, :], send_sem=mate_send.at[self.d, i], recv_sem=mate_recv.at[self.d, i],
                device_id={"dp": mate}, device_id_type=MESH,
            )

    ways = (Way(0), Way(1))

    def inside(i):
        return (i >= 0) & (i < NS)

    def start_hops(t):
        @pl.when(inside(t - 1))
        def _():
            pair_copy(t - 1).wait()
            own_copy(t - 1).wait()

        for way in ways:
            i = t - 1 - way.place

            @pl.when(inside(i))
            def _():
                own, pair, chain = way.loads(i)
                own.start()
                pair.start()

                @pl.when(way.place > 0)
                def _():
                    way.hop(i).wait_recv()
                    chain.start()

    def finish_hops(t):
        for way in ways:
            d = way.d
            i = t - 1 - way.place

            @pl.when(inside(i))
            def _():
                own, pair, chain = way.loads(i)
                own.wait()
                pair.wait()

                @pl.when((way.place < last) & (i >= 2))
                def _():
                    way.hop(i - 2).wait_send()

                def piece(total, p):
                    wide = st[d, 0, p].astype(F32) + st[d, 1, p].astype(F32)
                    if total:
                        wide += st[d, 2, p].astype(F32)
                    out[d, i % 2, p] = wide.astype(BF16)

                @pl.when(way.place == 0)
                def _():
                    lax.fori_loop(0, 3, lambda p, _: (piece(False, p), 0)[1], 0)

                @pl.when(way.place > 0)
                def _():
                    chain.wait()
                    lax.fori_loop(0, 3, lambda p, _: (piece(True, p), 0)[1], 0)

                @pl.when(way.place < last)
                def _():
                    way.hop(i).start()

                @pl.when(way.place == last)
                def _():
                    way.keep(i).start()

                    def add(p, _):
                        wide = out[d, i % 2, p].astype(F32)
                        ssq[...] += jnp.sum((wide * wide).reshape(quarter // 8, 8, FS), 0)
                        return 0

                    lax.fori_loop(0, 3, add, 0)
                    way.keep(i).wait()

    def spread_sums(t):
        for way in ways:
            i = t - 1 - last - (last - way.place)

            @pl.when(inside(i))
            def _():
                @pl.when(way.place < last)
                def _():
                    way.spread(i).wait_recv()

                @pl.when(way.place > 0)
                def _():
                    way.spread(i).start()

                way.share(i).start()

    def backward(t, _):
        w = PARTS + t
        slot = w % 2
        computing = t < NS

        @pl.when(computing)
        def _():
            @pl.when(t == PARTS)
            def _():
                cross_layers()

            fetched(w)

            @pl.when(t < NS - 1)
            def _():
                fetch(w + 1)

            def tile(rows):
                gu = dot(a[rows, :], wgu[slot])
                dh = dot_nt(up[rows, :], wd[slot]).astype(BF16).astype(F32)
                gate, lift = gu[:, :FS], gu[:, FS:]
                s = jax.nn.sigmoid(gate)
                silu = gate * s
                hid[rows, :] = (silu * lift).astype(BF16)
                dgu[rows, :FS] = (dh * lift * (s + silu * (1.0 - s))).astype(BF16)
                dgu[rows, FS:] = (dh * silu).astype(BF16)

            over_rows(T, RT, tile)

        start_hops(t)

        @pl.when(computing)
        def _():
            def tile(k, _):
                rows = mine(jnp.where(k == 0, 1 - c, c))
                gb[t % 2, 2, rows, :] = dot(upt[rows, :], hid[...]).astype(BF16)
                return 0

            lax.fori_loop(0, 2, tile, 0)

        finish_hops(t)

        @pl.when(computing)
        def _():
            def tile(k, _):
                rows = mine(jnp.where(k == 0, 1 - c, c))
                both = dot(at[rows, :], dgu[...]).astype(BF16)
                gb[t % 2, 0, rows, :] = both[:, :FS]
                gb[t % 2, 1, rows, :] = both[:, FS:]
                return 0

            lax.fori_loop(0, 2, tile, 0)
            pair_copy(t).start()
            own_copy(t).start()

        spread_sums(t)

        @pl.when(t < PARTS)
        def _():
            def tile(rows):
                acc[rows, :] += dot_nt(dgu[rows, :], wgu[slot])

            over_rows(T, RT, tile)

        return 0

    lax.fori_loop(0, NS + 2 * CHIPS - 1, backward, 0)

    for at_end in range(2):
        way = ways[1 - at_end]
        for core in range(2):
            slot = 2 * at_end + core
            holder = 2 * last * at_end + core

            def to(k, slot=slot):
                return pltpu.make_async_remote_copy(
                    src_ref=ssq, dst_ref=ssq_ref.at[slot], send_sem=ssq_send.at[k], recv_sem=ssq_recv.at[slot],
                    device_id={"dp": (dp + k) % (2 * CHIPS)}, device_id_type=MESH,
                )

            local = pltpu.make_async_copy(ssq, ssq_ref.at[slot], io_sem.at[0])

            @pl.when(dp == holder)
            def _():
                local.start()
                for k in range(1, 2 * CHIPS):
                    to(k).start()
                local.wait()
                for k in range(1, 2 * CHIPS):
                    to(k).wait_send()

            @pl.when(dp != holder)
            def _():
                to(0).wait_recv()

    for way in ways:

        @pl.when(way.place < last)
        def _():
            way.hop(NS - 2).wait_send()
            way.hop(NS - 1).wait_send()

        def close(i, _):
            @pl.when(way.place > 0)
            def _():
                way.spread(i).wait_send()

            way.share(i).wait()
            return 0

        lax.fori_loop(0, NS, close, 0)


def gradients(x, dy, w_gate, w_up, w_down):
    _, T, D = x.shape
    F = w_gate.shape[2]
    FS = F // PARTS
    RT, RD = min(512, T), min(256, T)
    NS = 2 * PARTS
    anywhere = pl.BlockSpec(memory_space=pl.ANY)
    dma = pltpu.SemaphoreType.DMA
    return pl.pallas_call(
        functools.partial(gradients_kernel, (T, D, FS, RT, RD)),
        out_shape=(
            jax.ShapeDtypeStruct((NS, 3, D, FS), BF16),
            jax.ShapeDtypeStruct((NS, 3, D // 2, FS), BF16),
            jax.ShapeDtypeStruct((NS, 3, D // 2, FS), BF16),
            jax.ShapeDtypeStruct((2, NS, 3, D // 4, FS), BF16),
            jax.ShapeDtypeStruct((4, 8, FS), F32),
            jax.ShapeDtypeStruct((T, D), BF16),
        ),
        in_specs=[anywhere] * 5,
        out_specs=(anywhere,) * 6,
        scratch_shapes=[
            pltpu.VMEM((T, D), BF16),
            pltpu.VMEM((D, T), BF16),
            pltpu.VMEM((T, D), BF16),
            pltpu.VMEM((D, T), BF16),
            pltpu.VMEM((T, D), F32),
            pltpu.VMEM((2, D, 2 * FS), BF16),
            pltpu.VMEM((2, FS, D), BF16),
            pltpu.VMEM((T, FS), BF16),
            pltpu.VMEM((T, 2 * FS), BF16),
            pltpu.VMEM((2, 3, D, FS), BF16),
            pltpu.VMEM((2, 3, 3, D // 4, FS), BF16),
            pltpu.VMEM((2, 2, 3, D // 4, FS), BF16),
            pltpu.VMEM((8, FS), F32),
            dma((2, 3)),
            dma((2,)),
            dma((2,)),
            dma((2,)),
            dma((NS,)),
            dma((2, 3)),
            dma((2, 2)),
            dma((2, NS)),
            dma((2,)),
            dma((2, NS)),
            dma((2, NS)),
            dma((2, NS)),
            dma((2, NS)),
            dma((2 * CHIPS,)),
            dma((4,)),
        ],
        compiler_params=pltpu.CompilerParams(collective_id=0, has_side_effects=True, vmem_limit_bytes=66_000_000),
        name="gradients",
    )(x, dy, w_gate, w_up, w_down)


def adamw_kernel(count, ssq_ref, g_ref, *refs):
    ins, outs = refs[:9], refs[9:]
    factor = jnp.minimum(1.0, 0.5 * lax.rsqrt(jnp.sum(ssq_ref[...]) / count + 1e-30))
    for k in range(3):
        w_ref, m_ref, v_ref = ins[k::3]
        g = g_ref[0, k].astype(F32)
        if k == 2:
            g = g.T
        g = g * factor
        m = 0.9 * m_ref[0] + 0.1 * g
        v = 0.95 * v_ref[0] + 0.05 * g * g
        w = w_ref[0].astype(F32)
        outs[k][0] = (w - 0.02 * (m * lax.rsqrt(v + 1e-8) + 0.1 * w)).astype(BF16)
        outs[3 + k][0] = m
        outs[6 + k][0] = v


def adamw(ssq, g, arrays):
    NS, _, D, FS = g.shape
    rows = min(256, D)

    def across(i, r):
        return 1 - i // PARTS, r, i % PARTS

    def down(i, r):
        return 1 - i // PARTS, i % PARTS, r

    specs = [pl.BlockSpec((1, rows, FS), across), pl.BlockSpec((1, rows, FS), across), pl.BlockSpec((1, FS, rows), down)] * 3
    count = 3 * g.shape[0] * D * FS
    return pl.pallas_call(
        functools.partial(adamw_kernel, float(count)),
        grid=(NS, D // rows),
        in_specs=[pl.BlockSpec(ssq.shape, lambda i, r: (0, 0, 0)), pl.BlockSpec((1, 3, rows, FS), lambda i, r: (i, 0, r, 0))] + specs,
        out_specs=specs,
        out_shape=[jax.ShapeDtypeStruct(a.shape, a.dtype) for a in arrays],
        compiler_params=pltpu.CompilerParams(dimension_semantics=("arbitrary", "arbitrary"), vmem_limit_bytes=50_000_000),
        name="adamw",
    )(ssq, g, *arrays)


def solution(mesh):
    def step(x, dy, *arrays):
        g, *_, ssq, _ = gradients(x, dy, *arrays[:3])
        return tuple(adamw(ssq, g, arrays))

    return jax.shard_map(
        step,
        mesh=mesh,
        in_specs=(P(("rep", "dp"), None, None),) * 2 + (P(None, None, None),) * 9,
        out_specs=(P("rep", None, None),) * 9,
        check_vma=False,
    )
```

time: 1640 us -> 924 us (0.56)
  waiting for transfers between devices: 965 us -> 0 us
  Pallas kernels: 0 us -> 922 us
  matrix products: 424 us -> 0 us
  other arithmetic: 215 us -> 0 us
    psum x1 -> x0, waiting for transfers between devices: 965 us -> none  [step(): summed[number] = [lax.psum(by_w[name], 'dp') for name in NAMES]]
    pallas_call x0 -> x2, Pallas kernels: none -> 922 us  [the longest x1 730 us: gradients(): pl.pallas_call(functools.partial(gradients_kernel, (T, D, FS, RT, RD)), o...]
    dot_general x15 -> x0, matrix products: 424 us -> none  [the longest x5 154 us: layer(): gate = jnp.dot(a, w['w_gate'], preferred_element_type=jnp.float32)]
    convert_element_type x2 -> x0, other arithmetic: 174 us -> none  [adamw(): return ((w - 0.02 * step).astype(jnp.bfloat16), m, v)]
    reduce_sum x4 -> x0, other arithmetic: 34.7 us -> none  [the longest x3 31.6 us: step(): jnp.sum(g * g)]
  transfers between devices with their start and end apart: 1 -> 0, of which waited for: 1 -> 0; matrix products, arithmetic and copies ran while one was open for 0% -> 0% of each run, Pallas kernels for 0% -> 0%
where the time goes in v1:
time: 924 us
  Pallas kernels  922 us (100%)
    pallas_call x1, Pallas kernels, gradients(): pl.pallas_call(functools.partial(gradients_kernel, (T, D, FS, RT, RD)), o...  730 us
    pallas_call x1, Pallas kernels, adamw(): pl.pallas_call(functools.partial(adamw_kernel, float(count)), grid=(NS, D...  192 us

profile of v1, /device:TPU:0, one launch (start us, length us, event | category | flops | bytes accessed | tf_op | source)
XLA Modules:
  0.0 923.9 jit_solution(10263488688528438449)
XLA Ops:
  0.6 730.2 %gradients.1 = (bf16[16,3,1024,512]{3,2,1,0:T(8,128)(2,1)}, bf16[16,3,512,512]{3,2,1,0:T(8,128)(2,1)}, bf16[16,3,512,512]{3,2,1,0:T(8,128)(2,1)}, bf16[2,16,3,25...) custom-call(bf16[1,2048,1024]{2,1,0:T(8,128)(2,1)} %x_ref.1, ...), custom_call_target="tpu_custom_call" | custom-call | tf_op jit(solution)/shard_map/gradients/pallas_call | solution.py:409
  730.9 0.0 copy-start
  730.9 0.8 copy-done
  731.7 192.1 %adamw.1 = (bf16[2,1024,4096]{2,1,0:T(8,128)(2,1)}, bf16[2,1024,4096]{2,1,0:T(8,128)(2,1)}, bf16[2,4096,1024]{2,1,0:T(8,128)(2,1)}, f32[2,1024,4096]{2,1,0:T(8,1...) custom-call(f32[4,8,512]{2,1,0:T(8,128)S(1)} %copy-done, ...), custom_call_target="tpu_custom_call" | custom-call | tf_op jit(solution)/shard_map/adamw/pallas_call | solution.py:485
Async XLA Ops:
  730.9 0.8 copy-start

commit v2 on v1

v2 whole, which is shorter than its diff:
```python
import functools

import jax
import jax.numpy as jnp
from jax import lax
from jax.experimental import pallas as pl
from jax.experimental.pallas import tpu as pltpu
from jax.sharding import PartitionSpec as P


MESH = pl.DeviceIdType.MESH
CHIPS = 4
PARTS = 8
NS = 2 * PARTS
WHOLE = 4
LAG = 3
SLOTS = 4
F32, BF16 = jnp.float32, jnp.bfloat16


def dot(a, b):
    return jnp.dot(a, b, preferred_element_type=F32)


def dot_nt(a, b):
    return lax.dot_general(a, b, (((1,), (1,)), ((), ())), preferred_element_type=F32)


def inverse_size(wide):
    return lax.rsqrt(jnp.mean(wide * wide, -1, keepdims=True) + 1e-6)


def gradients_kernel(
    sizes,
    x_ref, dy_ref, wg_ref, wu_ref, wd_ref,
    g_ref, own_ref, pair_ref, chain_ref, ssq_ref, h_ref,
    a, at, up, upt, acc, wgu, wd, hid, dgu, gb, st, out, ssq,
    w_sem, io_sem, pair_send, own_sem, pair_recv, ld_sem, chain_send, chain_recv, keep_sem, pass_send, pass_recv, mate_send, mate_recv, ssq_send, ssq_recv,
):
    T, D, FS, RT, RD = sizes
    UNITS = 3 * NS
    half, quarter = D // 2, D // 4
    dp = lax.axis_index("dp")
    z, c = dp // 2, dp % 2
    mate = dp + 1 - 2 * c
    last = CHIPS - 1

    barrier = pltpu.get_barrier_semaphore()
    for k in range(1, 2 * CHIPS):
        pl.semaphore_signal(barrier, inc=1, device_id={"dp": (dp + k) % (2 * CHIPS)}, device_id_type=MESH)

    def weight_copies(w):
        layer = jnp.where((w >= PARTS) & (w < 2 * PARTS), 1, 0)
        columns = pl.ds(pl.multiple_of((w % PARTS) * FS, FS), FS)
        slot = w % 2
        return (
            pltpu.make_async_copy(wg_ref.at[layer, :, columns], wgu.at[slot, :, pl.ds(0, FS)], w_sem.at[slot, 0]),
            pltpu.make_async_copy(wu_ref.at[layer, :, columns], wgu.at[slot, :, pl.ds(FS, FS)], w_sem.at[slot, 1]),
            pltpu.make_async_copy(wd_ref.at[layer, columns, :], wd.at[slot], w_sem.at[slot, 2]),
        )

    def fetch(w):
        for copy in weight_copies(w):
            copy.start()

    def fetched(w):
        for copy in weight_copies(w):
            copy.wait()

    def rows_of(r, size):
        return pl.ds(pl.multiple_of(r * size, size), size)

    def repeat(n, body):
        lax.fori_loop(0, n, lambda r, _: (body(r), 0)[1], 0)

    def over_rows(total, size, body):
        repeat(total // size, lambda r: body(rows_of(r, size)))

    load_x = pltpu.make_async_copy(x_ref.at[0], a, io_sem.at[0])
    load_x.start()
    fetch(0)
    load_again = pltpu.make_async_copy(x_ref.at[0], dgu, io_sem.at[1])
    load_again.start()
    load_dy = pltpu.make_async_copy(dy_ref.at[0], up, io_sem.at[2])
    load_dy.start()
    ssq[...] = jnp.zeros_like(ssq)
    load_x.wait()

    def norm_in_place(rows):
        wide = a[rows, :].astype(F32)
        a[rows, :] = (wide * inverse_size(wide)).astype(BF16)

    over_rows(T, RD, norm_in_place)

    def forward(j):
        slot = j % 2
        fetched(j)
        fetch(j + 1)

        def tile(rows):
            gu = dot(a[rows, :], wgu[slot])
            gate, lift = gu[:, :FS], gu[:, FS:]
            hidden = (gate * jax.nn.sigmoid(gate) * lift).astype(BF16)
            acc[rows, :] = jnp.where(j > 0, acc[rows, :], 0.0) + dot(hidden, wd[slot])

        over_rows(T, RT, tile)

    repeat(PARTS, forward)

    load_again.wait()

    def close_forward(rows):
        h = dgu[rows, :].astype(F32) + acc[rows, :].astype(BF16).astype(F32)
        h = h.astype(BF16)
        dgu[rows, :] = h
        wide = h.astype(F32)
        a[rows, :] = (wide * inverse_size(wide)).astype(BF16)
        acc[rows, :] = jnp.zeros((RD, D), F32)

    over_rows(T, RD, close_forward)
    save_h = pltpu.make_async_copy(dgu, h_ref, io_sem.at[0])
    save_h.start()

    def turn(source, target):
        def tile(rows):
            target[:, rows] = source[rows, :].T

        over_rows(T, RD, tile)

    load_dy.wait()
    turn(a, at)
    turn(up, upt)
    save_h.wait()
    pl.semaphore_wait(barrier, 2 * CHIPS - 1)

    reload_x = pltpu.make_async_copy(x_ref.at[0], a, io_sem.at[1])

    def cross_layers():
        load_h = pltpu.make_async_copy(h_ref, dgu, io_sem.at[0])
        load_h.start()
        reload_x.wait()
        over_rows(T, RD, norm_in_place)
        turn(a, at)
        load_h.wait()

        def tile(rows):
            wide = dgu[rows, :].astype(F32)
            scale = inverse_size(wide)
            da = acc[rows, :].astype(BF16).astype(F32)
            along = jnp.sum(da * wide, -1, keepdims=True) * (1.0 / D)
            dh = (scale * da - wide * (scale * scale * scale * along)).astype(BF16)
            up[rows, :] = (up[rows, :].astype(F32) + dh.astype(F32)).astype(BF16)

        over_rows(T, RD, tile)
        turn(up, upt)

    def half_of(core):
        return pl.ds(pl.multiple_of(core * half, half), half)

    def pair_copy(n):
        i, p = n // 3, n % 3
        return pltpu.make_async_remote_copy(
            src_ref=gb.at[i % 2, p, half_of(1 - c), :], dst_ref=pair_ref.at[i, p], send_sem=pair_send.at[i % 2, p], recv_sem=pair_recv.at[i, p],
            device_id={"dp": mate}, device_id_type=MESH,
        )

    def own_copy(n):
        i, p = n // 3, n % 3
        return pltpu.make_async_copy(gb.at[i % 2, p, half_of(c), :], own_ref.at[i, p], own_sem.at[i % 2, p])

    class Way:
        def __init__(self, d):
            self.d = d
            self.place = z if d == 0 else last - z
            self.step = 2 if d == 0 else -2
            self.small = pl.ds(d * quarter, quarter)
            self.rows = pl.ds(pl.multiple_of((2 * c + d) * quarter, quarter), quarter)

        def loads(self, n):
            d, i, p = self.d, n // 3, n % 3
            return (
                pltpu.make_async_copy(own_ref.at[i, p, self.small, :], st.at[d, 0], ld_sem.at[d, 0]),
                pltpu.make_async_copy(pair_ref.at[i, p, self.small, :], st.at[d, 1], ld_sem.at[d, 1]),
                pltpu.make_async_copy(chain_ref.at[d, i, p], st.at[d, 2], ld_sem.at[d, 2]),
            )

        def hop(self, n):
            d, i, p = self.d, n // 3, n % 3
            return pltpu.make_async_remote_copy(
                src_ref=out.at[d, n % SLOTS], dst_ref=chain_ref.at[d, i, p], send_sem=chain_send.at[d, n % SLOTS], recv_sem=chain_recv.at[d, i, p],
                device_id={"dp": (dp + self.step) % (2 * CHIPS)}, device_id_type=MESH,
            )

        def keep(self, n):
            return pltpu.make_async_copy(out.at[self.d, n % SLOTS], g_ref.at[n // 3, n % 3, self.rows, :], keep_sem.at[n % SLOTS])

        def spread(self, n):
            d, i, p = self.d, n // 3, n % 3
            return pltpu.make_async_remote_copy(
                src_ref=g_ref.at[i, p, self.rows, :], dst_ref=g_ref.at[i, p, self.rows, :], send_sem=pass_send.at[d, i, p], recv_sem=pass_recv.at[d, i, p],
                device_id={"dp": (dp - self.step + 2 * CHIPS) % (2 * CHIPS)}, device_id_type=MESH,
            )

        def share(self, n):
            d, i, p = self.d, n // 3, n % 3
            return pltpu.make_async_remote_copy(
                src_ref=g_ref.at[i, p, self.rows, :], dst_ref=g_ref.at[i, p, self.rows, :], send_sem=mate_send.at[d, i, p], recv_sem=mate_recv.at[d, i, p],
                device_id={"dp": mate}, device_id_type=MESH,
            )

        def reaches(self, n, place):
            return last - place <= WHOLE + last - 1 - n // 3

        def holds(self, n):
            return (self.place == last) | self.reaches(n, self.place)

        def passes(self, n):
            return (self.place > 0) & self.reaches(n, self.place - 1)

    ways = (Way(0), Way(1))

    def inside(n):
        return (n >= 0) & (n < UNITS)

    def start_tick(k):
        @pl.when(inside(k - 2))
        def _():
            own_copy(k - 2).wait()
            pair_copy(k - 2).wait_recv()

        for way in ways:
            n = k - 2 - LAG * way.place

            @pl.when(inside(n))
            def _(way=way, n=n):
                own, pair, chain = way.loads(n)
                own.start()
                pair.start()

                @pl.when(way.place > 0)
                def _():
                    way.hop(n).wait_recv()
                    chain.start()

    def finish_tick(k):
        for way in ways:
            d = way.d
            n = k - 2 - LAG * way.place

            @pl.when(inside(n))
            def _(way=way, d=d, n=n):
                own, pair, chain = way.loads(n)
                own.wait()
                pair.wait()

                @pl.when((way.place < last) & (n >= SLOTS))
                def _():
                    way.hop(n - SLOTS).wait_send()

                def add(so_far):
                    wide = st[d, 0].astype(F32) + st[d, 1].astype(F32)
                    if so_far:
                        wide += st[d, 2].astype(F32)
                    rounded = wide.astype(BF16)
                    out[d, n % SLOTS] = rounded
                    return rounded.astype(F32)

                @pl.when(way.place == 0)
                def _():
                    add(False)
                    way.hop(n).start()

                @pl.when((way.place > 0) & (way.place < last))
                def _():
                    chain.wait()
                    add(True)
                    way.hop(n).start()

                @pl.when(way.place == last)
                def _():
                    chain.wait()
                    total = add(True)
                    way.keep(n).start()
                    ssq[...] += jnp.sum((total * total).reshape(quarter // 8, 8, FS), 0)

        for way in ways:
            n = k - 3 - LAG * (2 * last - way.place)

            @pl.when(inside(n))
            def _(way=way, n=n):
                @pl.when(way.place == last)
                def _():
                    way.keep(n).wait()

                @pl.when((way.place < last) & way.holds(n))
                def _():
                    way.spread(n).wait_recv()

                @pl.when(way.passes(n))
                def _():
                    way.spread(n).start()

                @pl.when(way.holds(n))
                def _():
                    way.share(n).start()

    def backward(t):
        w = PARTS + t
        slot = w % 2

        @pl.when(t == PARTS)
        def _():
            cross_layers()

        fetched(w)

        @pl.when(t < NS - 1)
        def _():
            fetch(w + 1)

        def hidden_half(k):
            start_tick(3 * t + k)

            def tile(r):
                rows = rows_of(k * (T // RT // 2) + r, RT)
                gu = dot(a[rows, :], wgu[slot])
                dh = dot_nt(up[rows, :], wd[slot]).astype(BF16).astype(F32)
                gate, lift = gu[:, :FS], gu[:, FS:]
                s = jax.nn.sigmoid(gate)
                silu = gate * s
                hid[rows, :] = (silu * lift).astype(BF16)
                dgu[rows, :FS] = (dh * lift * (s + silu * (1.0 - s))).astype(BF16)
                dgu[rows, FS:] = (dh * silu).astype(BF16)

            repeat(T // RT // 2, tile)
            finish_tick(3 * t + k)

        repeat(2, hidden_half)

        @pl.when(t == PARTS - 1)
        def _():
            reload_x.start()

        @pl.when(t >= 2)
        def _():
            for p in range(3):
                pair_copy(3 * (t - 2) + p).wait_send()

        def down_half(k):
            rows = half_of(jnp.where(k == 0, 1 - c, c))
            gb[t % 2, 0, rows, :] = dot(upt[rows, :], hid[...]).astype(BF16)

            @pl.when(k == 0)
            def _():
                pair_copy(3 * t).start()

            @pl.when(k == 1)
            def _():
                own_copy(3 * t).start()

        repeat(2, down_half)

        def both_half(k):
            @pl.when(k == 1)
            def _():
                start_tick(3 * t + 2)

            rows = half_of(jnp.where(k == 0, 1 - c, c))
            both = dot(at[rows, :], dgu[...]).astype(BF16)
            gb[t % 2, 1, rows, :] = both[:, :FS]
            gb[t % 2, 2, rows, :] = both[:, FS:]

            @pl.when(k == 0)
            def _():
                pair_copy(3 * t + 1).start()
                pair_copy(3 * t + 2).start()

            @pl.when(k == 1)
            def _():
                own_copy(3 * t + 1).start()
                own_copy(3 * t + 2).start()
                finish_tick(3 * t + 2)

        repeat(2, both_half)

        @pl.when(t < PARTS)
        def _():
            def tile(rows):
                acc[rows, :] += dot_nt(dgu[rows, :], wgu[slot])

            over_rows(T, RT, tile)

    repeat(NS, backward)

    def drain(k):
        start_tick(UNITS + k)
        finish_tick(UNITS + k)

    ticks = max(UNITS + 2 + LAG * last + 1, 3 * (WHOLE + last - 1) + 2 + LAG * 2 * last + 1)
    repeat(ticks - UNITS, drain)

    for at_end in range(2):
        for core in range(2):
            slot = 2 * at_end + core
            holder = 2 * last * at_end + core

            def to(k, slot=slot):
                return pltpu.make_async_remote_copy(
                    src_ref=ssq, dst_ref=ssq_ref.at[slot], send_sem=ssq_send.at[k], recv_sem=ssq_recv.at[slot],
                    device_id={"dp": (dp + k) % (2 * CHIPS)}, device_id_type=MESH,
                )

            local = pltpu.make_async_copy(ssq, ssq_ref.at[slot], io_sem.at[0])

            @pl.when(dp == holder)
            def _(to=to, local=local):
                local.start()
                for k in range(1, 2 * CHIPS):
                    to(k).start()
                local.wait()
                for k in range(1, 2 * CHIPS):
                    to(k).wait_send()

    for slot in range(4):
        holder = 2 * last * (slot // 2) + slot % 2

        @pl.when(dp != holder)
        def _(slot=slot):
            pltpu.make_async_remote_copy(
                src_ref=ssq, dst_ref=ssq_ref.at[slot], send_sem=ssq_send.at[0], recv_sem=ssq_recv.at[slot],
                device_id={"dp": dp}, device_id_type=MESH,
            ).wait_recv()

    for p in range(3):
        pair_copy(3 * (NS - 2) + p).wait_send()
        pair_copy(3 * (NS - 1) + p).wait_send()

    for way in ways:

        @pl.when(way.place < last)
        def _(way=way):
            repeat(SLOTS, lambda k: way.hop(UNITS - SLOTS + k).wait_send())

        def close(n, way=way):
            @pl.when(way.passes(n))
            def _():
                way.spread(n).wait_send()

            @pl.when(way.holds(n))
            def _():
                way.share(n).wait()

        repeat(UNITS, close)


def gradients(x, dy, w_gate, w_up, w_down):
    _, T, D = x.shape
    F = w_gate.shape[2]
    FS = F // PARTS
    RT, RD = min(512, T // 2), min(256, T)
    anywhere = pl.BlockSpec(memory_space=pl.ANY)
    dma = pltpu.SemaphoreType.DMA
    return pl.pallas_call(
        functools.partial(gradients_kernel, (T, D, FS, RT, RD)),
        out_shape=(
            jax.ShapeDtypeStruct((NS, 3, D, FS), BF16),
            jax.ShapeDtypeStruct((NS, 3, D // 2, FS), BF16),
            jax.ShapeDtypeStruct((NS, 3, D // 2, FS), BF16),
            jax.ShapeDtypeStruct((2, NS, 3, D // 4, FS), BF16),
            jax.ShapeDtypeStruct((4, 8, FS), F32),
            jax.ShapeDtypeStruct((T, D), BF16),
        ),
        in_specs=[anywhere] * 5,
        out_specs=(anywhere,) * 6,
        scratch_shapes=[
            pltpu.VMEM((T, D), BF16),
            pltpu.VMEM((D, T), BF16),
            pltpu.VMEM((T, D), BF16),
            pltpu.VMEM((D, T), BF16),
            pltpu.VMEM((T, D), F32),
            pltpu.VMEM((2, D, 2 * FS), BF16),
            pltpu.VMEM((2, FS, D), BF16),
            pltpu.VMEM((T, FS), BF16),
            pltpu.VMEM((T, 2 * FS), BF16),
            pltpu.VMEM((2, 3, D, FS), BF16),
            pltpu.VMEM((2, 3, D // 4, FS), BF16),
            pltpu.VMEM((2, SLOTS, D // 4, FS), BF16),
            pltpu.VMEM((8, FS), F32),
            dma((2, 3)),
            dma((3,)),
            dma((2, 3)),
            dma((2, 3)),
            dma((NS, 3)),
            dma((2, 3)),
            dma((2, SLOTS)),
            dma((2, NS, 3)),
            dma((SLOTS,)),
            dma((2, WHOLE + CHIPS, 3)),
            dma((2, WHOLE + CHIPS, 3)),
            dma((2, NS, 3)),
            dma((2, NS, 3)),
            dma((2 * CHIPS,)),
            dma((4,)),
        ],
        compiler_params=pltpu.CompilerParams(collective_id=0, has_side_effects=True, vmem_limit_bytes=66_000_000),
        name="gradients",
    )(x, dy, w_gate, w_up, w_down)


def adamw_kernel(count, work, split, n_in, *refs):
    ssq_ref, g_ref = refs[:2]
    back = refs[2 : 2 + n_in]
    ins = refs[2 + n_in : 11 + n_in]
    outs, gv, sem = refs[-11:-2], refs[-2], refs[-1]
    quarter, FS = gv.shape[2:]
    dp = lax.axis_index("dp")
    z, c = dp // 2, dp % 2
    step = pl.program_id(0)

    def here(k, source):
        return pltpu.make_async_copy(source, gv.at[k], sem.at[k])

    @pl.when(step == 0)
    def _():
        for k, (i, q, came) in enumerate(work):
            whole = g_ref.at[i, :, pl.ds(q * quarter, quarter), :]
            place = z if q % 2 == 0 else CHIPS - 1 - z
            for p in range(CHIPS):
                if came[p] is None:

                    @pl.when(place == p)
                    def _(k=k, whole=whole):
                        here(k, whole).start()

                else:
                    for core in range(2):

                        @pl.when((place == p) & (c == core))
                        def _(k=k, at=came[p][0 if core == q // 2 else 1]):
                            here(k, back[at].at[0]).start()

    k, sub = step // split, step % split

    @pl.when(sub == 0)
    def _():
        here(k, g_ref.at[0, :, pl.ds(0, quarter), :]).wait()

    factor = jnp.minimum(1.0, 0.5 * lax.rsqrt(jnp.sum(ssq_ref[...]) / count + 1e-30))
    some = quarter // split

    def update(number, rows, g):
        w_ref, m_ref, v_ref = ins[number::3]
        g = g * factor
        m = 0.9 * m_ref[0, rows, :] + 0.1 * g
        v = 0.95 * v_ref[0, rows, :] + 0.05 * g * g
        w = w_ref[0, rows, :].astype(F32)
        outs[number][0, rows, :] = (w - 0.02 * (m * lax.rsqrt(v + 1e-8) + 0.1 * w)).astype(BF16)
        outs[3 + number][0, rows, :] = m
        outs[6 + number][0, rows, :] = v

    def across(r, _):
        few = some // 4
        rows = pl.ds(pl.multiple_of(r * few, few), few)
        there = pl.ds(pl.multiple_of(sub * some + r * few, few), few)
        update(0, rows, gv[k, 1, there, :].astype(F32))
        update(1, rows, gv[k, 2, there, :].astype(F32))
        return 0

    lax.fori_loop(0, 4, across, 0)

    def down(r, _):
        few = FS // 4
        rows = pl.ds(pl.multiple_of(r * few, few), few)
        update(2, rows, gv[k, 0, pl.ds(pl.multiple_of(sub * some, some), some), rows].astype(F32).T)
        return 0

    lax.fori_loop(0, 4, down, 0)


def adamw(ssq, g, arrays, results, listed, back):
    _, _, D, FS = g.shape
    quarter = D // 4
    split = 2 if quarter % 256 == 0 else 1
    some = quarter // split
    first, base = listed[0][:2], listed[-1][0]
    alone = 4 * first[0] + first[1]
    rest = 4 * base + 4 - len(listed)

    def number(s):
        k = s // split
        if all(4 * i + q == alone + at for at, (i, q, _) in enumerate(listed)):
            return alone + k
        return jnp.where(k == 0, alone, rest + k)

    def across(s):
        n = number(s)
        return 1 - n // 4 // PARTS, n % 4 * split + s % split, n // 4 % PARTS

    def down(s):
        n = number(s)
        return 1 - n // 4 // PARTS, n // 4 % PARTS, n % 4 * split + s % split

    specs = [pl.BlockSpec((1, some, FS), across), pl.BlockSpec((1, some, FS), across), pl.BlockSpec((1, FS, some), down)] * 3
    anywhere = pl.BlockSpec(memory_space=pl.ANY)
    count = 3 * g.shape[0] * D * FS
    size = 3 * len(listed) * quarter * FS
    ins = [ssq, g, *back, *arrays, *(results or ())]
    return pl.pallas_call(
        functools.partial(adamw_kernel, float(count), listed, split, len(back)),
        grid=(len(listed) * split,),
        in_specs=[pl.BlockSpec(ssq.shape, lambda s: (0, 0, 0))] + [anywhere] * (1 + len(back)) + specs + [anywhere] * (9 if results else 0),
        out_specs=specs,
        out_shape=[jax.ShapeDtypeStruct(a.shape, a.dtype) for a in arrays],
        input_output_aliases={len(ins) - 9 + k: k for k in range(9)} if results else {},
        scratch_shapes=[pltpu.VMEM((len(listed), 3, quarter, FS), BF16), pltpu.SemaphoreType.DMA((len(listed),))],
        compiler_params=pltpu.CompilerParams(dimension_semantics=("arbitrary",), vmem_limit_bytes=66_000_000),
        cost_estimate=pl.CostEstimate(flops=COST * size, bytes_accessed=22 * size, transcendentals=size),
        name="adamw",
    )(*ins)


COST = 16


def finish(g, ssq, arrays):
    _, _, D, FS = g.shape
    quarter = D // 4
    last = CHIPS - 1
    dp = lax.axis_index("dp")
    z, c = dp // 2, dp % 2
    stages = NS - WHOLE
    ready = [(i, q, (None,) * CHIPS) for i in range(WHOLE) for q in range(4)]
    back, results = [], None
    index = {}

    def kept(i, d, g=g):
        return lax.dynamic_slice(g, (jnp.asarray(i, jnp.int32), jnp.int32(0), (2 * c + d) * quarter, jnp.int32(0)), (1, 3, quarter, FS))

    def units(u):
        came = []
        for d in range(2):
            came.append(tuple(index[u - p, d] if p < last and u >= p else None for p in range(CHIPS)))
        return [(WHOLE + u, q, came[q % 2]) for q in range(4)]

    def update(results, listed):
        used = sorted({at for _, _, came in listed for pair in came if pair for at in pair})
        where = {at: k for k, at in enumerate(used)}
        listed = [(i, q, tuple(pair and tuple(where[at] for at in pair) for pair in came)) for i, q, came in listed]
        return adamw(ssq, g, arrays, results, listed, [back[at] for at in used])

    newest, pending = [None, None], []
    extra = 4 * WHOLE - 2 * 5
    for s in range(stages + 2):
        for at, swaps in pending:
            back[at + 1] = lax.ppermute(back[at], "dp", swaps)
        pending = []
        at_hand = g
        if s > 0:
            at_hand, *newest = lax.optimization_barrier((g, *newest))
        for d in range(2 if s < stages else 0):
            place = z if d == 0 else last - z
            if s == 0:
                sent = kept(WHOLE + place - 1, d)
            elif s + last - 1 < stages:
                sent = jnp.where(place == last, kept(WHOLE + s + last - 1, d, at_hand), newest[d])
            else:
                sent = newest[d]
            moves = []
            for p in range(1, CHIPS):
                if s + p - 1 < stages:
                    for core in range(2):
                        source, target = (p, p - 1) if d == 0 else (last - p, last - p + 1)
                        moves.append((2 * source + core, 2 * target + core))
            newest[d] = lax.ppermute(sent, "dp", moves)
            index[s, d] = (len(back), len(back) + 1)
            pending.append((len(back), [(to, to + 1 - 2 * (to % 2)) for _, to in moves]))
            back += [newest[d], None]
        many = 5 if s < 2 else 1 if s - 2 < extra else 0
        listed, ready = ready[:many], ready[many:]
        if s >= 2:
            listed = listed + units(s - 2)
        results = update(results, listed)
    return results


def solution(mesh):
    def step(x, dy, *arrays):
        g, *_, ssq, _ = gradients(x, dy, *arrays[:3])
        return tuple(finish(g, ssq, arrays))

    return jax.shard_map(
        step,
        mesh=mesh,
        in_specs=(P(("rep", "dp"), None, None),) * 2 + (P(None, None, None),) * 9,
        out_specs=(P("rep", None, None),) * 9,
        check_vma=False,
    )
```

time: 924 us -> 1080 us (1.17)
  waiting for transfers between devices: 0 us -> 153 us
  Pallas kernels: 922 us -> 789 us
  starting transfers between devices: 0 us -> 111 us
  other arithmetic: 0 us -> 18.9 us
    pallas_call x1, Pallas kernels: 730 us -> 520 us  [gradients(): pl.pallas_call(functools.partial(gradients_kernel, (T, D, FS, RT, RD)), o...]
    ppermute x0 -> x48, waiting for transfers between devices: none -> 153 us  [the longest x24 153 us: finish(): newest[d] = lax.ppermute(sent, 'dp', moves)]
    ppermute x0 -> x48, starting transfers between devices: none -> 111 us  [the longest x24 73.3 us: finish(): newest[d] = lax.ppermute(sent, 'dp', moves)]
    pallas_call x1 -> x14, Pallas kernels: 192 us -> 269 us  [adamw(): pl.pallas_call(functools.partial(adamw_kernel, float(count), listed, spli...]
    select_n x0 -> x9, other arithmetic: none -> 18.9 us  [finish(): jnp.where(place == last, kept(WHOLE + s + last - 1, d, at_hand), newest[d])]
  transfers between devices with their start and end apart: 0 -> 48, of which waited for: 0 -> 21; matrix products, arithmetic and copies ran while one was open for 0% -> 0% of each run, Pallas kernels for 0% -> 23%
where the time goes in v2:
time: 1080 us
  Pallas kernels  789 us (73%)
  waiting for transfers between devices  153 us (14%)
  starting transfers between devices  111 us (10%)
  other arithmetic  18.9 us (2%)
    pallas_call x1, Pallas kernels, gradients(): pl.pallas_call(functools.partial(gradients_kernel, (T, D, FS, RT, RD)), o...  520 us
    pallas_call x14, Pallas kernels, adamw(): pl.pallas_call(functools.partial(adamw_kernel, float(count), listed, spli...  269 us
    ppermute x24, waiting for transfers between devices, finish(): newest[d] = lax.ppermute(sent, 'dp', moves)  153 us
    ppermute x24, starting transfers between devices, finish(): newest[d] = lax.ppermute(sent, 'dp', moves)  73.3 us
    ppermute x24, starting transfers between devices, finish(): back[at + 1] = lax.ppermute(back[at], 'dp', swaps)  37.7 us
  transfers between devices with their start and end apart: 48, of which 21 were waited for; matrix products, arithmetic and copies ran while one was open for 0% of the time, Pallas kernels for 23%

profile of v2, /device:TPU:0, one launch (start us, length us, event | category | flops | bytes accessed | tf_op | source)
XLA Modules:
  0.0 1075.6 jit_solution(4083724742163085860)
XLA Ops:
  0.7 519.9 %gradients.1 = (bf16[16,3,1024,512]{3,2,1,0:T(8,128)(2,1)}, bf16[16,3,512,512]{3,2,1,0:T(8,128)(2,1)}, bf16[16,3,512,512]{3,2,1,0:T(8,128)(2,1)}, bf16[2,16,3,25...) custom-call(bf16[1,2048,1024]{2,1,0:T(8,128)(2,1)} %x_ref.1, ...), custom_call_target="tpu_custom_call" | custom-call | tf_op jit(solution)/shard_map/gradients/pallas_call | solution.py:463
  523.4 4.6 collective-permute-start.1
  528.0 15.5 %collective-permute-done.refs_2_ = bf16[1,3,256,512]{3,2,1,0:T(8,128)(2,1)S(1)} collective-permute-done((bf16[1,3,256,512]{3,2,1,0:T(8,128)(2,1)S(1)}, bf16[1,3,256,512]{3,2,1,0:T(8,128)(2,1)S(1)}, u32[]{:S(2)}, u32[]{:S(2)}) %collective-permute-start) | collective-permute-done | bytes 786464 | tf_op jit(solution)/shard_map/ppermute | solution.py:674
  544.7 2.1 dynamic-slice_select_fusion.16
  548.1 5.1 collective-permute-start.3
  553.2 14.7 %collective-permute-done.2.refs_6_.refs_2_ = bf16[1,3,256,512]{3,2,1,0:T(8,128)(2,1)S(1)} collective-permute-done((bf16[1,3,256,512]{3,2,1,0:T(8,128)(2,1)S(1)}, bf16[1,3,256,512]{3,2,1,0:T(8,128)(2,1)S(1)}, u32[]{:S(2)}, u32[]{:S(2)}) %collective-permute-start.2) | collective-permute-done | bytes 786464 | tf_op jit(solution)/shard_map/ppermute | solution.py:674
  569.0 2.1 dynamic-slice_select_fusion.14
  572.5 5.1 collective-permute-start.5
  577.5 13.8 %collective-permute-done.4.refs_10_.refs_6_.refs_2_ = bf16[1,3,256,512]{3,2,1,0:T(8,128)(2,1)S(1)} collective-permute-done((bf16[1,3,256,512]{3,2,1,0:T(8,128)(2,1)S(1)}, bf16[1,3,256,512]{3,2,1,0:T(8,128)(2,1)S(1)}, u32[]{:S(2)}, u32[]{:S(2)}) %collective-permute-start.4) | collective-permute-done | bytes 786464 | tf_op jit(solution)/shard_map/ppermute | solution.py:674
  592.6 2.1 dynamic-slice_select_fusion.12
  596.0 5.1 collective-permute-start.7
  601.1 13.0 %collective-permute-done.6.refs_10_.refs_6_.refs_2_ = bf16[1,3,256,512]{3,2,1,0:T(8,128)(2,1)S(1)} collective-permute-done((bf16[1,3,256,512]{3,2,1,0:T(8,128)(2,1)S(1)}, bf16[1,3,256,512]{3,2,1,0:T(8,128)(2,1)S(1)}, u32[]{:S(2)}, u32[]{:S(2)}) %collective-permute-start.6) | collective-permute-done | bytes 786464 | tf_op jit(solution)/shard_map/ppermute | solution.py:674
  615.2 2.1 dynamic-slice_select_fusion.10
  618.7 5.1 collective-permute-start.9
  623.8 12.1 %collective-permute-done.8.refs_10_.refs_6_.refs_2_ = bf16[1,3,256,512]{3,2,1,0:T(8,128)(2,1)S(1)} collective-permute-done((bf16[1,3,256,512]{3,2,1,0:T(8,128)(2,1)S(1)}, bf16[1,3,256,512]{3,2,1,0:T(8,128)(2,1)S(1)}, u32[]{:S(2)}, u32[]{:S(2)}) %collective-permute-start.8) | collective-permute-done | bytes 786464 | tf_op jit(solution)/shard_map/ppermute | solution.py:674
  637.1 2.1 dynamic-slice_select_fusion.8
  640.5 5.1 collective-permute-start.11
  645.6 11.3 %collective-permute-done.10.refs_10_.refs_6_.refs_2_ = bf16[1,3,256,512]{3,2,1,0:T(8,128)(2,1)S(1)} collective-permute-done((bf16[1,3,256,512]{3,2,1,0:T(8,128)(2,1)S(1)}, bf16[1,3,256,512]{3,2,1,0:T(8,128)(2,1)S(1)}, u32[]{:S(2)}, u32[]{:S(2)}) %collective-permute-start.10) | collective-permute-done | bytes 786464 | tf_op jit(solution)/shard_map/ppermute | solution.py:674
  658.0 2.1 dynamic-slice_select_fusion.6
  661.5 5.1 collective-permute-start.13
  666.5 10.4 collective-permute-done.12.refs_10_.refs_6_.refs_2_
  678.1 2.1 dynamic-slice_select_fusion.4
  681.6 5.1 collective-permute-start.15
  686.7 9.6 collective-permute-done.14.refs_10_.refs_6_.refs_2_
  697.4 2.1 dynamic-slice_select_fusion.2
  700.8 5.1 collective-permute-start.17
  705.9 1.9 collective-permute-start.46
  707.8 1.6 collective-permute-start.47
  709.4 2.4 collective-permute-start.44
  711.8 2.8 collective-permute-done.16.refs_10_.refs_6_.refs_2_
  715.8 1.9 collective-permute-start.42
  718.5 2.4 collective-permute-start.40
  721.6 1.9 dynamic-slice_select_fusion
  723.5 1.9 collective-permute-start.38
  726.8 9.3 collective-permute-start.20
  736.8 1.9 collective-permute-start.36
  739.7 11.3 %collective-permute-done.18.refs_10_.refs_6_.refs_2_ = bf16[1,3,256,512]{3,2,1,0:T(8,128)(2,1)S(1)} collective-permute-done((bf16[1,3,256,512]{3,2,1,0:T(8,128)(2,1)S(1)}, bf16[1,3,256,512]{3,2,1,0:T(8,128)(2,1)S(1)}, u32[]{:S(2)}, u32[]{:S(2)}) %collective-permute-start.18) | collective-permute-done | bytes 786464 | tf_op jit(solution)/shard_map/ppermute | solution.py:674
  751.0 1.9 collective-permute-start.34
  752.9 1.6 collective-permute-start.35
  755.8 1.6 collective-permute-start.24
  757.4 2.4 collective-permute-start.32
  760.6 1.9 collective-permute-start.30
  762.5 14.4 %collective-permute-done.22.refs_10_.refs_6_ = bf16[1,3,256,512]{3,2,1,0:T(8,128)(2,1)} collective-permute-done((bf16[1,3,256,512]{3,2,1,0:T(8,128)(2,1)S(1)}, bf16[1,3,256,512]{3,2,1,0:T(8,128)(2,1)}, u32[]{:S(2)}, u32[]{:S(2)}) %collective-permute-start.22) | collective-permute-done | bytes 786464 | tf_op jit(solution)/shard_map/ppermute | solution.py:674
  777.6 1.9 collective-permute-start.19
  781.1 1.6 collective-permute-start.28
  782.7 1.6 collective-permute-start.21
  784.3 2.4 collective-permute-start.23
  786.7 1.6 collective-permute-start.25
  788.3 14.4 %collective-permute-done.26.refs_10_ = bf16[1,3,256,512]{3,2,1,0:T(8,128)(2,1)} collective-permute-done((bf16[1,3,256,512]{3,2,1,0:T(8,128)(2,1)}, bf16[1,3,256,512]{3,2,1,0:T(8,128)(2,1)}, u32[]{:S(2)}, u32[]{:S(2)}) %collective-permute-start.26) | collective-permute-done | bytes 786464 | tf_op jit(solution)/shard_map/ppermute | solution.py:674
  802.7 1.9 collective-permute-start.27
  806.3 20.6 %adamw.14 = (bf16[2,1024,4096]{2,1,0:T(8,128)(2,1)}, bf16[2,1024,4096]{2,1,0:T(8,128)(2,1)}, bf16[2,4096,1024]{2,1,0:T(8,128)(2,1)}, f32[2,1024,4096]{2,1,0:T(8,...) custom-call(f32[4,8,512]{2,1,0:T(8,128)} %get-tuple-element.159.refs, ...), custom_call_target="tpu_custom_call" | custom-call | flops 31457280 | bytes 43253760 | tf_op jit(solution)/shard_map/adamw/pallas_call | solution.py:608
  827.0 20.6 %adamw.15 = (bf16[2,1024,4096]{2,1,0:T(8,128)(2,1)}, bf16[2,1024,4096]{2,1,0:T(8,128)(2,1)}, bf16[2,4096,1024]{2,1,0:T(8,128)(2,1)}, f32[2,1024,4096]{2,1,0:T(8,...) custom-call(f32[4,8,512]{2,1,0:T(8,128)} %get-tuple-element.159.refs, ...), custom_call_target="tpu_custom_call", output_to_operand_aliasing={{0}: (11, {}), {1}: (12, {}), {2}: (13, {}), {3}: (14, {}),... | custom-call | flops 31457280 | bytes 43253760 | tf_op jit(solution)/shard_map/adamw/pallas_call | solution.py:608
  847.6 20.8 %adamw.16 = (bf16[2,1024,4096]{2,1,0:T(8,128)(2,1)}, bf16[2,1024,4096]{2,1,0:T(8,128)(2,1)}, bf16[2,4096,1024]{2,1,0:T(8,128)(2,1)}, f32[2,1024,4096]{2,1,0:T(8,...) custom-call(f32[4,8,512]{2,1,0:T(8,128)} %get-tuple-element.159.refs, ...), custom_call_target="tpu_custom_call", output_to_operand_aliasing={{0}: (15, {}), {1}: (16, {}), {2}: (17, {}), {3}: (18, {}),... | custom-call | flops 31457280 | bytes 43253760 | tf_op jit(solution)/shard_map/adamw/pallas_call | solution.py:608
  868.4 20.8 %adamw.17 = (bf16[2,1024,4096]{2,1,0:T(8,128)(2,1)}, bf16[2,1024,4096]{2,1,0:T(8,128)(2,1)}, bf16[2,4096,1024]{2,1,0:T(8,128)(2,1)}, f32[2,1024,4096]{2,1,0:T(8,...) custom-call(f32[4,8,512]{2,1,0:T(8,128)} %get-tuple-element.159.refs, ...), custom_call_target="tpu_custom_call", output_to_operand_aliasing={{0}: (19, {}), {1}: (20, {}), {2}: (21, {}), {3}: (22, {}),... | custom-call | flops 31457280 | bytes 43253760 | tf_op jit(solution)/shard_map/adamw/pallas_call | solution.py:608
  889.2 20.7 %adamw.18 = (bf16[2,1024,4096]{2,1,0:T(8,128)(2,1)}, bf16[2,1024,4096]{2,1,0:T(8,128)(2,1)}, bf16[2,4096,1024]{2,1,0:T(8,128)(2,1)}, f32[2,1024,4096]{2,1,0:T(8,...) custom-call(f32[4,8,512]{2,1,0:T(8,128)} %get-tuple-element.159.refs, ...), custom_call_target="tpu_custom_call", output_to_operand_aliasing={{0}: (23, {}), {1}: (24, {}), {2}: (25, {}), {3}: (26, {}),... | custom-call | flops 31457280 | bytes 43253760 | tf_op jit(solution)/shard_map/adamw/pallas_call | solution.py:608
  909.9 20.7 %adamw.19 = (bf16[2,1024,4096]{2,1,0:T(8,128)(2,1)}, bf16[2,1024,4096]{2,1,0:T(8,128)(2,1)}, bf16[2,4096,1024]{2,1,0:T(8,128)(2,1)}, f32[2,1024,4096]{2,1,0:T(8,...) custom-call(f32[4,8,512]{2,1,0:T(8,128)} %get-tuple-element.159.refs, ...), custom_call_target="tpu_custom_call", output_to_operand_aliasing={{0}: (23, {}), {1}: (24, {}), {2}: (25, {}), {3}: (26, {}),... | custom-call | flops 31457280 | bytes 43253760 | tf_op jit(solution)/shard_map/adamw/pallas_call | solution.py:608
  930.7 20.7 %adamw.20 = (bf16[2,1024,4096]{2,1,0:T(8,128)(2,1)}, bf16[2,1024,4096]{2,1,0:T(8,128)(2,1)}, bf16[2,4096,1024]{2,1,0:T(8,128)(2,1)}, f32[2,1024,4096]{2,1,0:T(8,...) custom-call(f32[4,8,512]{2,1,0:T(8,128)} %get-tuple-element.159.refs, ...), custom_call_target="tpu_custom_call", output_to_operand_aliasing={{0}: (23, {}), {1}: (24, {}), {2}: (25, {}), {3}: (26, {}),... | custom-call | flops 31457280 | bytes 43253760 | tf_op jit(solution)/shard_map/adamw/pallas_call | solution.py:608
  951.4 20.7 %adamw.21 = (bf16[2,1024,4096]{2,1,0:T(8,128)(2,1)}, bf16[2,1024,4096]{2,1,0:T(8,128)(2,1)}, bf16[2,4096,1024]{2,1,0:T(8,128)(2,1)}, f32[2,1024,4096]{2,1,0:T(8,...) custom-call(f32[4,8,512]{2,1,0:T(8,128)} %get-tuple-element.159.refs, ...), custom_call_target="tpu_custom_call", output_to_operand_aliasing={{0}: (23, {}), {1}: (24, {}), {2}: (25, {}), {3}: (26, {}),... | custom-call | flops 31457280 | bytes 43253760 | tf_op jit(solution)/shard_map/adamw/pallas_call | solution.py:608
  972.1 17.2 %adamw.22 = (bf16[2,1024,4096]{2,1,0:T(8,128)(2,1)}, bf16[2,1024,4096]{2,1,0:T(8,128)(2,1)}, bf16[2,4096,1024]{2,1,0:T(8,128)(2,1)}, f32[2,1024,4096]{2,1,0:T(8,...) custom-call(f32[4,8,512]{2,1,0:T(8,128)} %get-tuple-element.159.refs, ...), custom_call_target="tpu_custom_call", output_to_operand_aliasing={{0}: (23, {}), {1}: (24, {}), {2}: (25, {}), {3}: (26, {}),... | custom-call | flops 25165824 | bytes 34603008 | tf_op jit(solution)/shard_map/adamw/pallas_call | solution.py:608
  989.3 17.2 %adamw.23 = (bf16[2,1024,4096]{2,1,0:T(8,128)(2,1)}, bf16[2,1024,4096]{2,1,0:T(8,128)(2,1)}, bf16[2,4096,1024]{2,1,0:T(8,128)(2,1)}, f32[2,1024,4096]{2,1,0:T(8,...) custom-call(f32[4,8,512]{2,1,0:T(8,128)} %get-tuple-element.159.refs, ...), custom_call_target="tpu_custom_call", output_to_operand_aliasing={{0}: (23, {}), {1}: (24, {}), {2}: (25, {}), {3}: (26, {}),... | custom-call | flops 25165824 | bytes 34603008 | tf_op jit(solution)/shard_map/adamw/pallas_call | solution.py:608
  1006.6 17.2 %adamw.24 = (bf16[2,1024,4096]{2,1,0:T(8,128)(2,1)}, bf16[2,1024,4096]{2,1,0:T(8,128)(2,1)}, bf16[2,4096,1024]{2,1,0:T(8,128)(2,1)}, f32[2,1024,4096]{2,1,0:T(8,...) custom-call(f32[4,8,512]{2,1,0:T(8,128)} %get-tuple-element.159.refs, ...), custom_call_target="tpu_custom_call", output_to_operand_aliasing={{0}: (23, {}), {1}: (24, {}), {2}: (25, {}), {3}: (26, {}),... | custom-call | flops 25165824 | bytes 34603008 | tf_op jit(solution)/shard_map/adamw/pallas_call | solution.py:608
  1023.8 17.2 %adamw.25 = (bf16[2,1024,4096]{2,1,0:T(8,128)(2,1)}, bf16[2,1024,4096]{2,1,0:T(8,128)(2,1)}, bf16[2,4096,1024]{2,1,0:T(8,128)(2,1)}, f32[2,1024,4096]{2,1,0:T(8,...) custom-call(f32[4,8,512]{2,1,0:T(8,128)} %get-tuple-element.159.refs, ...), custom_call_target="tpu_custom_call", output_to_operand_aliasing={{0}: (23, {}), {1}: (24, {}), {2}: (25, {}), {3}: (26, {}),... | custom-call | flops 25165824 | bytes 34603008 | tf_op jit(solution)/shard_map/adamw/pallas_call | solution.py:608
  1041.0 17.2 %adamw.26 = (bf16[2,1024,4096]{2,1,0:T(8,128)(2,1)}, bf16[2,1024,4096]{2,1,0:T(8,128)(2,1)}, bf16[2,4096,1024]{2,1,0:T(8,128)(2,1)}, f32[2,1024,4096]{2,1,0:T(8,...) custom-call(f32[4,8,512]{2,1,0:T(8,128)} %get-tuple-element.159.refs, ...), custom_call_target="tpu_custom_call", output_to_operand_aliasing={{0}: (23, {}), {1}: (24, {}), {2}: (25, {}), {3}: (26, {}),... | custom-call | flops 25165824 | bytes 34603008 | tf_op jit(solution)/shard_map/adamw/pallas_call | solution.py:608
  1058.2 17.2 %adamw.27 = (bf16[2,1024,4096]{2,1,0:T(8,128)(2,1)}, bf16[2,1024,4096]{2,1,0:T(8,128)(2,1)}, bf16[2,4096,1024]{2,1,0:T(8,128)(2,1)}, f32[2,1024,4096]{2,1,0:T(8,...) custom-call(f32[4,8,512]{2,1,0:T(8,128)} %get-tuple-element.159.refs, ...), custom_call_target="tpu_custom_call", output_to_operand_aliasing={{0}: (23, {}), {1}: (24, {}), {2}: (25, {}), {3}: (26, {}),... | custom-call | flops 25165824 | bytes 34603008 | tf_op jit(solution)/shard_map/adamw/pallas_call | solution.py:608
  (125 shorter events, 34.0 us)
Async XLA Ops:
  522.1 21.5 %collective-permute-start = (bf16[1,3,256,512]{3,2,1,0:T(8,128)(2,1)S(1)}, bf16[1,3,256,512]{3,2,1,0:T(8,128)(2,1)S(1)}, u32[]{:S(2)}, u32[]{:S(2)}) collective-permute-start(bf16[1,3,256,512]{3,2,1,0:T(8,128)(2,1)S(1)} %get-tuple-element.328), channel_id=1, source_target_pairs={{2,0},{3,1},{4,2},{5,3},{6,4},{7,5},{10,8},{11,9},{12,10},{13,11},... | collective-permute-start | bytes 2359304 | tf_op jit(solution)/shard_map/ppermute | solution.py:674
  523.4 21.3 %collective-permute-start.1 = (bf16[1,3,256,512]{3,2,1,0:T(8,128)(2,1)S(1)}, bf16[1,3,256,512]{3,2,1,0:T(8,128)(2,1)S(1)}, u32[]{:S(2)}, u32[]{:S(2)}) collective-permute-start(bf16[1,3,256,512]{3,2,1,0:T(8,128)(2,1)S(1)} %get-tuple-element.327), channel_id=1, source_target_pairs={{4,6},{5,7},{2,4},{3,5},{0,2},{1,3},{12,14},{13,15},{10,12},{11,13... | collective-permute-start | bytes 2359304 | tf_op jit(solution)/shard_map/ppermute | solution.py:674
  543.5 262.7 %copy-start.13 = (bf16[1,3,256,512]{3,2,1,0:T(8,128)(2,1)}, bf16[1,3,256,512]{3,2,1,0:T(8,128)(2,1)S(1)}, u32[]{:S(2)}) copy-start(bf16[1,3,256,512]{3,2,1,0:T(8,128)(2,1)S(1)} %collective-permute-done.refs_2_) | copy-start | bytes 2359300
  544.7 261.5 %copy-start.16 = (bf16[1,3,256,512]{3,2,1,0:T(8,128)(2,1)}, bf16[1,3,256,512]{3,2,1,0:T(8,128)(2,1)S(1)}, u32[]{:S(2)}) copy-start(bf16[1,3,256,512]{3,2,1,0:T(8,128)(2,1)S(1)} %collective-permute-done.1.refs_4_) | copy-start | bytes 2359300
  546.8 21.1 %collective-permute-start.2 = (bf16[1,3,256,512]{3,2,1,0:T(8,128)(2,1)S(1)}, bf16[1,3,256,512]{3,2,1,0:T(8,128)(2,1)S(1)}, u32[]{:S(2)}, u32[]{:S(2)}) collective-permute-start(bf16[1,3,256,512]{3,2,1,0:T(8,128)(2,1)S(1)} %get-tuple-element.326), channel_id=1, source_target_pairs={{2,0},{3,1},{4,2},{5,3},{6,4},{7,5},{10,8},{11,9},{12,10},{13,11},... | collective-permute-start | bytes 2359304 | tf_op jit(solution)/shard_map/ppermute | solution.py:674
  548.1 20.9 %collective-permute-start.3 = (bf16[1,3,256,512]{3,2,1,0:T(8,128)(2,1)S(1)}, bf16[1,3,256,512]{3,2,1,0:T(8,128)(2,1)S(1)}, u32[]{:S(2)}, u32[]{:S(2)}) collective-permute-start(bf16[1,3,256,512]{3,2,1,0:T(8,128)(2,1)S(1)} %get-tuple-element.325), channel_id=1, source_target_pairs={{4,6},{5,7},{2,4},{3,5},{0,2},{1,3},{12,14},{13,15},{10,12},{11,13... | collective-permute-start | bytes 2359304 | tf_op jit(solution)/shard_map/ppermute | solution.py:674
  567.9 238.3 %copy-start.14 = (bf16[1,3,256,512]{3,2,1,0:T(8,128)(2,1)}, bf16[1,3,256,512]{3,2,1,0:T(8,128)(2,1)S(1)}, u32[]{:S(2)}) copy-start(bf16[1,3,256,512]{3,2,1,0:T(8,128)(2,1)S(1)} %collective-permute-done.2.refs_6_.refs_2_) | copy-start | bytes 2359300
  569.0 237.1 %copy-start.17 = (bf16[1,3,256,512]{3,2,1,0:T(8,128)(2,1)}, bf16[1,3,256,512]{3,2,1,0:T(8,128)(2,1)S(1)}, u32[]{:S(2)}) copy-start(bf16[1,3,256,512]{3,2,1,0:T(8,128)(2,1)S(1)} %collective-permute-done.3.refs_8_.refs_4_) | copy-start | bytes 2359300
  571.2 20.2 %collective-permute-start.4 = (bf16[1,3,256,512]{3,2,1,0:T(8,128)(2,1)S(1)}, bf16[1,3,256,512]{3,2,1,0:T(8,128)(2,1)S(1)}, u32[]{:S(2)}, u32[]{:S(2)}) collective-permute-start(bf16[1,3,256,512]{3,2,1,0:T(8,128)(2,1)S(1)} %get-tuple-element.324), channel_id=1, source_target_pairs={{2,0},{3,1},{4,2},{5,3},{6,4},{7,5},{10,8},{11,9},{12,10},{13,11},... | collective-permute-start | bytes 2359304 | tf_op jit(solution)/shard_map/ppermute | solution.py:674
  572.5 20.1 %collective-permute-start.5 = (bf16[1,3,256,512]{3,2,1,0:T(8,128)(2,1)S(1)}, bf16[1,3,256,512]{3,2,1,0:T(8,128)(2,1)S(1)}, u32[]{:S(2)}, u32[]{:S(2)}) collective-permute-start(bf16[1,3,256,512]{3,2,1,0:T(8,128)(2,1)S(1)} %get-tuple-element.323), channel_id=1, source_target_pairs={{4,6},{5,7},{2,4},{3,5},{0,2},{1,3},{12,14},{13,15},{10,12},{11,13... | collective-permute-start | bytes 2359304 | tf_op jit(solution)/shard_map/ppermute | solution.py:674
  591.4 214.8 %copy-start.11 = (bf16[1,3,256,512]{3,2,1,0:T(8,128)(2,1)}, bf16[1,3,256,512]{3,2,1,0:T(8,128)(2,1)S(1)}, u32[]{:S(2)}) copy-start(bf16[1,3,256,512]{3,2,1,0:T(8,128)(2,1)S(1)} %collective-permute-done.4.refs_10_.refs_6_.refs_2_) | copy-start | bytes 2359300
  592.6 213.6 %copy-start.15 = (bf16[1,3,256,512]{3,2,1,0:T(8,128)(2,1)}, bf16[1,3,256,512]{3,2,1,0:T(8,128)(2,1)S(1)}, u32[]{:S(2)}) copy-start(bf16[1,3,256,512]{3,2,1,0:T(8,128)(2,1)S(1)} %collective-permute-done.5.refs_12_.refs_8_.refs_4_) | copy-start | bytes 2359300
  594.7 19.4 %collective-permute-start.6 = (bf16[1,3,256,512]{3,2,1,0:T(8,128)(2,1)S(1)}, bf16[1,3,256,512]{3,2,1,0:T(8,128)(2,1)S(1)}, u32[]{:S(2)}, u32[]{:S(2)}) collective-permute-start(bf16[1,3,256,512]{3,2,1,0:T(8,128)(2,1)S(1)} %get-tuple-element.322), channel_id=1, source_target_pairs={{2,0},{3,1},{4,2},{5,3},{6,4},{7,5},{10,8},{11,9},{12,10},{13,11},... | collective-permute-start | bytes 2359304 | tf_op jit(solution)/shard_map/ppermute | solution.py:674
  596.0 19.2 %collective-permute-start.7 = (bf16[1,3,256,512]{3,2,1,0:T(8,128)(2,1)S(1)}, bf16[1,3,256,512]{3,2,1,0:T(8,128)(2,1)S(1)}, u32[]{:S(2)}, u32[]{:S(2)}) collective-permute-start(bf16[1,3,256,512]{3,2,1,0:T(8,128)(2,1)S(1)} %get-tuple-element.321), channel_id=1, source_target_pairs={{4,6},{5,7},{2,4},{3,5},{0,2},{1,3},{12,14},{13,15},{10,12},{11,13... | collective-permute-start | bytes 2359304 | tf_op jit(solution)/shard_map/ppermute | solution.py:674
  614.1 192.1 %copy-start.9 = (bf16[1,3,256,512]{3,2,1,0:T(8,128)(2,1)}, bf16[1,3,256,512]{3,2,1,0:T(8,128)(2,1)S(1)}, u32[]{:S(2)}) copy-start(bf16[1,3,256,512]{3,2,1,0:T(8,128)(2,1)S(1)} %collective-permute-done.6.refs_10_.refs_6_.refs_2_) | copy-start | bytes 2359300
  615.2 191.0 %copy-start.12 = (bf16[1,3,256,512]{3,2,1,0:T(8,128)(2,1)}, bf16[1,3,256,512]{3,2,1,0:T(8,128)(2,1)S(1)}, u32[]{:S(2)}) copy-start(bf16[1,3,256,512]{3,2,1,0:T(8,128)(2,1)S(1)} %collective-permute-done.7.refs_12_.refs_8_.refs_4_) | copy-start | bytes 2359300
  617.4 18.5 %collective-permute-start.8 = (bf16[1,3,256,512]{3,2,1,0:T(8,128)(2,1)S(1)}, bf16[1,3,256,512]{3,2,1,0:T(8,128)(2,1)S(1)}, u32[]{:S(2)}, u32[]{:S(2)}) collective-permute-start(bf16[1,3,256,512]{3,2,1,0:T(8,128)(2,1)S(1)} %get-tuple-element.320), channel_id=1, source_target_pairs={{2,0},{3,1},{4,2},{5,3},{6,4},{7,5},{10,8},{11,9},{12,10},{13,11},... | collective-permute-start | bytes 2359304 | tf_op jit(solution)/shard_map/ppermute | solution.py:674
  618.7 18.4 %collective-permute-start.9 = (bf16[1,3,256,512]{3,2,1,0:T(8,128)(2,1)S(1)}, bf16[1,3,256,512]{3,2,1,0:T(8,128)(2,1)S(1)}, u32[]{:S(2)}, u32[]{:S(2)}) collective-permute-start(bf16[1,3,256,512]{3,2,1,0:T(8,128)(2,1)S(1)} %get-tuple-element.319), channel_id=1, source_target_pairs={{4,6},{5,7},{2,4},{3,5},{0,2},{1,3},{12,14},{13,15},{10,12},{11,13... | collective-permute-start | bytes 2359304 | tf_op jit(solution)/shard_map/ppermute | solution.py:674
  635.9 168.7 %copy-start.7 = (bf16[1,3,256,512]{3,2,1,0:T(8,128)(2,1)}, bf16[1,3,256,512]{3,2,1,0:T(8,128)(2,1)S(1)}, u32[]{:S(2)}) copy-start(bf16[1,3,256,512]{3,2,1,0:T(8,128)(2,1)S(1)} %collective-permute-done.8.refs_10_.refs_6_.refs_2_) | copy-start | bytes 2359300
  637.1 169.1 %copy-start.10 = (bf16[1,3,256,512]{3,2,1,0:T(8,128)(2,1)}, bf16[1,3,256,512]{3,2,1,0:T(8,128)(2,1)S(1)}, u32[]{:S(2)}) copy-start(bf16[1,3,256,512]{3,2,1,0:T(8,128)(2,1)S(1)} %collective-permute-done.9.refs_12_.refs_8_.refs_4_) | copy-start | bytes 2359300
  639.2 17.6 %collective-permute-start.10 = (bf16[1,3,256,512]{3,2,1,0:T(8,128)(2,1)S(1)}, bf16[1,3,256,512]{3,2,1,0:T(8,128)(2,1)S(1)}, u32[]{:S(2)}, u32[]{:S(2)}) collective-permute-start(bf16[1,3,256,512]{3,2,1,0:T(8,128)(2,1)S(1)} %get-tuple-element.318), channel_id=1, source_target_pairs={{2,0},{3,1},{4,2},{5,3},{6,4},{7,5},{10,8},{11,9},{12,10},{13,11},... | collective-permute-start | bytes 2359304 | tf_op jit(solution)/shard_map/ppermute | solution.py:674
  640.5 17.5 %collective-permute-start.11 = (bf16[1,3,256,512]{3,2,1,0:T(8,128)(2,1)S(1)}, bf16[1,3,256,512]{3,2,1,0:T(8,128)(2,1)S(1)}, u32[]{:S(2)}, u32[]{:S(2)}) collective-permute-start(bf16[1,3,256,512]{3,2,1,0:T(8,128)(2,1)S(1)} %get-tuple-element.317), channel_id=1, source_target_pairs={{4,6},{5,7},{2,4},{3,5},{0,2},{1,3},{12,14},{13,15},{10,12},{11,13... | collective-permute-start | bytes 2359304 | tf_op jit(solution)/shard_map/ppermute | solution.py:674
  656.9 131.4 %copy-start.5 = (bf16[1,3,256,512]{3,2,1,0:T(8,128)(2,1)}, bf16[1,3,256,512]{3,2,1,0:T(8,128)(2,1)S(1)}, u32[]{:S(2)}) copy-start(bf16[1,3,256,512]{3,2,1,0:T(8,128)(2,1)S(1)} %collective-permute-done.10.refs_10_.refs_6_.refs_2_) | copy-start | bytes 2359300
  658.0 146.6 %copy-start.8 = (bf16[1,3,256,512]{3,2,1,0:T(8,128)(2,1)}, bf16[1,3,256,512]{3,2,1,0:T(8,128)(2,1)S(1)}, u32[]{:S(2)}) copy-start(bf16[1,3,256,512]{3,2,1,0:T(8,128)(2,1)S(1)} %collective-permute-done.11.refs_12_.refs_8_.refs_4_) | copy-start | bytes 2359300
  660.2 16.8 %collective-permute-start.12 = (bf16[1,3,256,512]{3,2,1,0:T(8,128)(2,1)S(1)}, bf16[1,3,256,512]{3,2,1,0:T(8,128)(2,1)S(1)}, u32[]{:S(2)}, u32[]{:S(2)}) collective-permute-start(bf16[1,3,256,512]{3,2,1,0:T(8,128)(2,1)S(1)} %get-tuple-element.316), channel_id=1, source_target_pairs={{2,0},{3,1},{4,2},{5,3},{6,4},{7,5},{10,8},{11,9},{12,10},{13,11},... | collective-permute-start | bytes 2359304 | tf_op jit(solution)/shard_map/ppermute | solution.py:674
  661.5 16.7 %collective-permute-start.13 = (bf16[1,3,256,512]{3,2,1,0:T(8,128)(2,1)S(1)}, bf16[1,3,256,512]{3,2,1,0:T(8,128)(2,1)S(1)}, u32[]{:S(2)}, u32[]{:S(2)}) collective-permute-start(bf16[1,3,256,512]{3,2,1,0:T(8,128)(2,1)S(1)} %get-tuple-element.315), channel_id=1, source_target_pairs={{4,6},{5,7},{2,4},{3,5},{0,2},{1,3},{12,14},{13,15},{10,12},{11,13... | collective-permute-start | bytes 2359304 | tf_op jit(solution)/shard_map/ppermute | solution.py:674
  677.0 109.7 %copy-start.4 = (bf16[1,3,256,512]{3,2,1,0:T(8,128)(2,1)}, bf16[1,3,256,512]{3,2,1,0:T(8,128)(2,1)S(1)}, u32[]{:S(2)}) copy-start(bf16[1,3,256,512]{3,2,1,0:T(8,128)(2,1)S(1)} %collective-permute-done.12.refs_10_.refs_6_.refs_2_) | copy-start | bytes 2359300
  678.1 124.5 %copy-start.6 = (bf16[1,3,256,512]{3,2,1,0:T(8,128)(2,1)}, bf16[1,3,256,512]{3,2,1,0:T(8,128)(2,1)S(1)}, u32[]{:S(2)}) copy-start(bf16[1,3,256,512]{3,2,1,0:T(8,128)(2,1)S(1)} %collective-permute-done.13.refs_12_.refs_8_.refs_4_) | copy-start | bytes 2359300
  680.3 15.9 %collective-permute-start.14 = (bf16[1,3,256,512]{3,2,1,0:T(8,128)(2,1)S(1)}, bf16[1,3,256,512]{3,2,1,0:T(8,128)(2,1)S(1)}, u32[]{:S(2)}, u32[]{:S(2)}) collective-permute-start(bf16[1,3,256,512]{3,2,1,0:T(8,128)(2,1)S(1)} %get-tuple-element.314), channel_id=1, source_target_pairs={{2,0},{3,1},{4,2},{5,3},{6,4},{7,5},{10,8},{11,9},{12,10},{13,11},... | collective-permute-start | bytes 2359304 | tf_op jit(solution)/shard_map/ppermute | solution.py:674
  681.6 15.8 %collective-permute-start.15 = (bf16[1,3,256,512]{3,2,1,0:T(8,128)(2,1)S(1)}, bf16[1,3,256,512]{3,2,1,0:T(8,128)(2,1)S(1)}, u32[]{:S(2)}, u32[]{:S(2)}) collective-permute-start(bf16[1,3,256,512]{3,2,1,0:T(8,128)(2,1)S(1)} %get-tuple-element.313), channel_id=1, source_target_pairs={{4,6},{5,7},{2,4},{3,5},{0,2},{1,3},{12,14},{13,15},{10,12},{11,13... | collective-permute-start | bytes 2359304 | tf_op jit(solution)/shard_map/ppermute | solution.py:674
  696.2 88.1 %copy-start.2 = (bf16[1,3,256,512]{3,2,1,0:T(8,128)(2,1)}, bf16[1,3,256,512]{3,2,1,0:T(8,128)(2,1)S(1)}, u32[]{:S(2)}) copy-start(bf16[1,3,256,512]{3,2,1,0:T(8,128)(2,1)S(1)} %collective-permute-done.14.refs_10_.refs_6_.refs_2_) | copy-start | bytes 2359300
  697.4 89.3 %copy-start.3 = (bf16[1,3,256,512]{3,2,1,0:T(8,128)(2,1)}, bf16[1,3,256,512]{3,2,1,0:T(8,128)(2,1)S(1)}, u32[]{:S(2)}) copy-start(bf16[1,3,256,512]{3,2,1,0:T(8,128)(2,1)S(1)} %collective-permute-done.15.refs_12_.refs_8_.refs_4_) | copy-start | bytes 2359300
  699.5 15.1 %collective-permute-start.16 = (bf16[1,3,256,512]{3,2,1,0:T(8,128)(2,1)S(1)}, bf16[1,3,256,512]{3,2,1,0:T(8,128)(2,1)S(1)}, u32[]{:S(2)}, u32[]{:S(2)}) collective-permute-start(bf16[1,3,256,512]{3,2,1,0:T(8,128)(2,1)S(1)} %get-tuple-element.312), channel_id=1, source_target_pairs={{2,0},{3,1},{4,2},{5,3},{6,4},{7,5},{10,8},{11,9},{12,10},{13,11},... | collective-permute-start | bytes 2359304 | tf_op jit(solution)/shard_map/ppermute | solution.py:674
  700.8 15.0 %collective-permute-start.17 = (bf16[1,3,256,512]{3,2,1,0:T(8,128)(2,1)S(1)}, bf16[1,3,256,512]{3,2,1,0:T(8,128)(2,1)S(1)}, u32[]{:S(2)}, u32[]{:S(2)}) collective-permute-start(bf16[1,3,256,512]{3,2,1,0:T(8,128)(2,1)S(1)} %get-tuple-element.311), channel_id=1, source_target_pairs={{4,6},{5,7},{2,4},{3,5},{0,2},{1,3},{12,14},{13,15},{10,12},{11,13... | collective-permute-start | bytes 2359304 | tf_op jit(solution)/shard_map/ppermute | solution.py:674
  705.9 11.8 %collective-permute-start.46 = (bf16[1,3,256,512]{3,2,1,0:T(8,128)(2,1)S(1)}, bf16[1,3,256,512]{3,2,1,0:T(8,128)(2,1)}, u32[]{:S(2)}, u32[]{:S(2)}) collective-permute-start(bf16[1,3,256,512]{3,2,1,0:T(8,128)(2,1)S(1)} %collective-permute-done.refs_2_), channel_id=1, source_target_pairs={{0,1},{1,0},{2,3},{3,2},{4,5},{5,4},{8,9},{9,8},{10,11},{11,10},{1... | collective-permute-start | bytes 2359304 | tf_op jit(solution)/shard_map/ppermute | solution.py:655
  707.8 10.6 collective-permute-start.47
  709.4 11.5 %collective-permute-start.44 = (bf16[1,3,256,512]{3,2,1,0:T(8,128)(2,1)S(1)}, bf16[1,3,256,512]{3,2,1,0:T(8,128)(2,1)}, u32[]{:S(2)}, u32[]{:S(2)}) collective-permute-start(bf16[1,3,256,512]{3,2,1,0:T(8,128)(2,1)S(1)} %collective-permute-done.2.refs_6_.refs_2_), channel_id=1, source_target_pairs={{0,1},{1,0},{2,3},{3,2},{4,5},{5,4},{8,9},{9,8},{10,11},{11,10},{1... | collective-permute-start | bytes 2359304 | tf_op jit(solution)/shard_map/ppermute | solution.py:655
  714.6 8.9 collective-permute-start.45
  715.8 9.6 collective-permute-start.42
  717.7 9.0 collective-permute-start.43
  718.5 17.6 %collective-permute-start.40 = (bf16[1,3,256,512]{3,2,1,0:T(8,128)(2,1)S(1)}, bf16[1,3,256,512]{3,2,1,0:T(8,128)(2,1)S(1)}, u32[]{:S(2)}, u32[]{:S(2)}) collective-permute-start(bf16[1,3,256,512]{3,2,1,0:T(8,128)(2,1)S(1)} %collective-permute-done.6.refs_10_.refs_6_.refs_2_), channel_id=1, source_target_pairs={{0,1},{1,0},{2,3},{3,2},{4,5},{5,4},{8,9},{9,8},{10,11},{11,10},{1... | collective-permute-start | bytes 2359304 | tf_op jit(solution)/shard_map/ppermute | solution.py:655
  720.9 15.9 %collective-permute-start.41 = (bf16[1,3,256,512]{3,2,1,0:T(8,128)(2,1)S(1)}, bf16[1,3,256,512]{3,2,1,0:T(8,128)(2,1)S(1)}, u32[]{:S(2)}, u32[]{:S(2)}) collective-permute-start(bf16[1,3,256,512]{3,2,1,0:T(8,128)(2,1)S(1)} %collective-permute-done.7.refs_12_.refs_8_.refs_4_), channel_id=1, source_target_pairs={{6,7},{7,6},{4,5},{5,4},{2,3},{3,2},{14,15},{15,14},{12,13},{13,12... | collective-permute-start | bytes 2359304 | tf_op jit(solution)/shard_map/ppermute | solution.py:655
  723.5 15.3 %collective-permute-start.38 = (bf16[1,3,256,512]{3,2,1,0:T(8,128)(2,1)S(1)}, bf16[1,3,256,512]{3,2,1,0:T(8,128)(2,1)S(1)}, u32[]{:S(2)}, u32[]{:S(2)}) collective-permute-start(bf16[1,3,256,512]{3,2,1,0:T(8,128)(2,1)S(1)} %collective-permute-done.8.refs_10_.refs_6_.refs_2_), channel_id=1, source_target_pairs={{0,1},{1,0},{2,3},{3,2},{4,5},{5,4},{8,9},{9,8},{10,11},{11,10},{1... | collective-permute-start | bytes 2359304 | tf_op jit(solution)/shard_map/ppermute | solution.py:655
  725.4 25.5 %collective-permute-start.18 = (bf16[1,3,256,512]{3,2,1,0:T(8,128)(2,1)S(1)}, bf16[1,3,256,512]{3,2,1,0:T(8,128)(2,1)S(1)}, u32[]{:S(2)}, u32[]{:S(2)}) collective-permute-start(bf16[1,3,256,512]{3,2,1,0:T(8,128)(2,1)S(1)} %get-tuple-element.310), channel_id=1, source_target_pairs={{2,0},{3,1},{4,2},{5,3},{6,4},{7,5},{10,8},{11,9},{12,10},{13,11},... | collective-permute-start | bytes 2359304 | tf_op jit(solution)/shard_map/ppermute | solution.py:674
  726.8 26.1 %collective-permute-start.20 = (bf16[1,3,256,512]{3,2,1,0:T(8,128)(2,1)S(1)}, bf16[1,3,256,512]{3,2,1,0:T(8,128)(2,1)}, u32[]{:S(2)}, u32[]{:S(2)}) collective-permute-start(bf16[1,3,256,512]{3,2,1,0:T(8,128)(2,1)S(1)} %get-tuple-element.309), channel_id=1, source_target_pairs={{4,6},{5,7},{2,4},{3,5},{0,2},{1,3},{12,14},{13,15},{10,12},{11,13... | collective-permute-start | bytes 2359304 | tf_op jit(solution)/shard_map/ppermute | solution.py:674
  736.1 18.4 %collective-permute-start.39 = (bf16[1,3,256,512]{3,2,1,0:T(8,128)(2,1)S(1)}, bf16[1,3,256,512]{3,2,1,0:T(8,128)(2,1)S(1)}, u32[]{:S(2)}, u32[]{:S(2)}) collective-permute-start(bf16[1,3,256,512]{3,2,1,0:T(8,128)(2,1)S(1)} %collective-permute-done.9.refs_12_.refs_8_.refs_4_), channel_id=1, source_target_pairs={{6,7},{7,6},{4,5},{5,4},{2,3},{3,2},{14,15},{15,14},{12,13},{13,12... | collective-permute-start | bytes 2359304 | tf_op jit(solution)/shard_map/ppermute | solution.py:655
  736.8 19.0 %collective-permute-start.36 = (bf16[1,3,256,512]{3,2,1,0:T(8,128)(2,1)S(1)}, bf16[1,3,256,512]{3,2,1,0:T(8,128)(2,1)S(1)}, u32[]{:S(2)}, u32[]{:S(2)}) collective-permute-start(bf16[1,3,256,512]{3,2,1,0:T(8,128)(2,1)S(1)} %collective-permute-done.10.refs_10_.refs_6_.refs_2_), channel_id=1, source_target_pairs={{0,1},{1,0},{2,3},{3,2},{4,5},{5,4},{8,9},{9,8},{10,11},{11,10},{1... | collective-permute-start | bytes 2359304 | tf_op jit(solution)/shard_map/ppermute | solution.py:655
  738.8 18.6 %collective-permute-start.37 = (bf16[1,3,256,512]{3,2,1,0:T(8,128)(2,1)S(1)}, bf16[1,3,256,512]{3,2,1,0:T(8,128)(2,1)S(1)}, u32[]{:S(2)}, u32[]{:S(2)}) collective-permute-start(bf16[1,3,256,512]{3,2,1,0:T(8,128)(2,1)S(1)} %collective-permute-done.11.refs_12_.refs_8_.refs_4_), channel_id=1, source_target_pairs={{6,7},{7,6},{4,5},{5,4},{2,3},{3,2},{14,15},{15,14},{12,13},{13,12... | collective-permute-start | bytes 2359304 | tf_op jit(solution)/shard_map/ppermute | solution.py:655
  751.0 8.8 collective-permute-start.34
  752.9 7.7 collective-permute-start.35
  754.5 22.4 %collective-permute-start.22 = (bf16[1,3,256,512]{3,2,1,0:T(8,128)(2,1)S(1)}, bf16[1,3,256,512]{3,2,1,0:T(8,128)(2,1)}, u32[]{:S(2)}, u32[]{:S(2)}) collective-permute-start(bf16[1,3,256,512]{3,2,1,0:T(8,128)(2,1)S(1)} %collective-permute-done.18.refs_10_.refs_6_.refs_2_), channel_id=1, source_target_pairs={{2,0},{3,1},{4,2},{5,3},{10,8},{11,9},{12,10},{13,11},{18,16},{19,... | collective-permute-start | bytes 2359304 | tf_op jit(solution)/shard_map/ppermute | solution.py:674
  755.8 21.8 %collective-permute-start.24 = (bf16[1,3,256,512]{3,2,1,0:T(8,128)(2,1)}, bf16[1,3,256,512]{3,2,1,0:T(8,128)(2,1)}, u32[]{:S(2)}, u32[]{:S(2)}) collective-permute-start(bf16[1,3,256,512]{3,2,1,0:T(8,128)(2,1)} %collective-permute-done.20.refs_12_.refs_8_.refs_4_), channel_id=1, source_target_pairs={{4,6},{5,7},{2,4},{3,5},{12,14},{13,15},{10,12},{11,13},{20,22},{2... | collective-permute-start | bytes 2359304 | tf_op jit(solution)/shard_map/ppermute | solution.py:674
  757.4 22.2 %collective-permute-start.32 = (bf16[1,3,256,512]{3,2,1,0:T(8,128)(2,1)S(1)}, bf16[1,3,256,512]{3,2,1,0:T(8,128)(2,1)S(1)}, u32[]{:S(2)}, u32[]{:S(2)}) collective-permute-start(bf16[1,3,256,512]{3,2,1,0:T(8,128)(2,1)S(1)} %collective-permute-done.14.refs_10_.refs_6_.refs_2_), channel_id=1, source_target_pairs={{0,1},{1,0},{2,3},{3,2},{4,5},{5,4},{8,9},{9,8},{10,11},{11,10},{1... | collective-permute-start | bytes 2359304 | tf_op jit(solution)/shard_map/ppermute | solution.py:655
  759.8 21.3 %collective-permute-start.33 = (bf16[1,3,256,512]{3,2,1,0:T(8,128)(2,1)S(1)}, bf16[1,3,256,512]{3,2,1,0:T(8,128)(2,1)S(1)}, u32[]{:S(2)}, u32[]{:S(2)}) collective-permute-start(bf16[1,3,256,512]{3,2,1,0:T(8,128)(2,1)S(1)} %collective-permute-done.15.refs_12_.refs_8_.refs_4_), channel_id=1, source_target_pairs={{6,7},{7,6},{4,5},{5,4},{2,3},{3,2},{14,15},{15,14},{12,13},{13,12... | collective-permute-start | bytes 2359304 | tf_op jit(solution)/shard_map/ppermute | solution.py:655
  760.6 22.1 %collective-permute-start.30 = (bf16[1,3,256,512]{3,2,1,0:T(8,128)(2,1)S(1)}, bf16[1,3,256,512]{3,2,1,0:T(8,128)(2,1)S(1)}, u32[]{:S(2)}, u32[]{:S(2)}) collective-permute-start(bf16[1,3,256,512]{3,2,1,0:T(8,128)(2,1)S(1)} %collective-permute-done.16.refs_10_.refs_6_.refs_2_), channel_id=1, source_target_pairs={{0,1},{1,0},{2,3},{3,2},{4,5},{5,4},{8,9},{9,8},{10,11},{11,10},{1... | collective-permute-start | bytes 2359304 | tf_op jit(solution)/shard_map/ppermute | solution.py:655
  776.9 7.4 collective-permute-start.31
  777.6 9.1 collective-permute-start.19
  779.6 23.1 %collective-permute-start.26 = (bf16[1,3,256,512]{3,2,1,0:T(8,128)(2,1)}, bf16[1,3,256,512]{3,2,1,0:T(8,128)(2,1)}, u32[]{:S(2)}, u32[]{:S(2)}) collective-permute-start(bf16[1,3,256,512]{3,2,1,0:T(8,128)(2,1)} %collective-permute-done.22.refs_10_.refs_6_), channel_id=1, source_target_pairs={{2,0},{3,1},{10,8},{11,9},{18,16},{19,17},{26,24},{27,25}} | collective-permute-start | bytes 2359304 | tf_op jit(solution)/shard_map/ppermute | solution.py:674
  781.1 23.5 %collective-permute-start.28 = (bf16[1,3,256,512]{3,2,1,0:T(8,128)(2,1)}, bf16[1,3,256,512]{3,2,1,0:T(8,128)(2,1)}, u32[]{:S(2)}, u32[]{:S(2)}) collective-permute-start(bf16[1,3,256,512]{3,2,1,0:T(8,128)(2,1)} %collective-permute-done.24.refs_12_.refs_8_), channel_id=1, source_target_pairs={{4,6},{5,7},{12,14},{13,15},{20,22},{21,23},{28,30},{29,31}} | collective-permute-start | bytes 2359304 | tf_op jit(solution)/shard_map/ppermute | solution.py:674
  782.7 241.1 %collective-permute-start.21 = (bf16[1,3,256,512]{3,2,1,0:T(8,128)(2,1)}, bf16[1,3,256,512]{3,2,1,0:T(8,128)(2,1)}, u32[]{:S(2)}, u32[]{:S(2)}) collective-permute-start(bf16[1,3,256,512]{3,2,1,0:T(8,128)(2,1)} %collective-permute-done.20.refs_12_.refs_8_.refs_4_), channel_id=1, source_target_pairs={{6,7},{7,6},{4,5},{5,4},{2,3},{3,2},{14,15},{15,14},{12,13},{13,12... | collective-permute-start | bytes 2359304 | tf_op jit(solution)/shard_map/ppermute | solution.py:655
  784.3 256.7 %collective-permute-start.23 = (bf16[1,3,256,512]{3,2,1,0:T(8,128)(2,1)}, bf16[1,3,256,512]{3,2,1,0:T(8,128)(2,1)}, u32[]{:S(2)}, u32[]{:S(2)}) collective-permute-start(bf16[1,3,256,512]{3,2,1,0:T(8,128)(2,1)} %collective-permute-done.22.refs_10_.refs_6_), channel_id=1, source_target_pairs={{0,1},{1,0},{2,3},{3,2},{8,9},{9,8},{10,11},{11,10},{16,17},{17,16... | collective-permute-start | bytes 2359304 | tf_op jit(solution)/shard_map/ppermute | solution.py:655
  786.7 254.3 %collective-permute-start.25 = (bf16[1,3,256,512]{3,2,1,0:T(8,128)(2,1)}, bf16[1,3,256,512]{3,2,1,0:T(8,128)(2,1)}, u32[]{:S(2)}, u32[]{:S(2)}) collective-permute-start(bf16[1,3,256,512]{3,2,1,0:T(8,128)(2,1)} %collective-permute-done.24.refs_12_.refs_8_), channel_id=1, source_target_pairs={{6,7},{7,6},{4,5},{5,4},{14,15},{15,14},{12,13},{13,12},{22,23},{2... | collective-permute-start | bytes 2359304 | tf_op jit(solution)/shard_map/ppermute | solution.py:655
  802.7 255.6 %collective-permute-start.27 = (bf16[1,3,256,512]{3,2,1,0:T(8,128)(2,1)}, bf16[1,3,256,512]{3,2,1,0:T(8,128)(2,1)}, u32[]{:S(2)}, u32[]{:S(2)}) collective-permute-start(bf16[1,3,256,512]{3,2,1,0:T(8,128)(2,1)} %collective-permute-done.26.refs_10_), channel_id=1, source_target_pairs={{0,1},{1,0},{8,9},{9,8},{16,17},{17,16},{24,25},{25,24}} | collective-permute-start | bytes 2359304 | tf_op jit(solution)/shard_map/ppermute | solution.py:655
  804.6 253.6 %collective-permute-start.29 = (bf16[1,3,256,512]{3,2,1,0:T(8,128)(2,1)}, bf16[1,3,256,512]{3,2,1,0:T(8,128)(2,1)}, u32[]{:S(2)}, u32[]{:S(2)}) collective-permute-start(bf16[1,3,256,512]{3,2,1,0:T(8,128)(2,1)} %collective-permute-done.28.refs_12_), channel_id=1, source_target_pairs={{6,7},{7,6},{14,15},{15,14},{22,23},{23,22},{30,31},{31,30}} | collective-permute-start | bytes 2359304 | tf_op jit(solution)/shard_map/ppermute | solution.py:655
  (18 other events, 699.4 us)

commit v3 on v2

--- a/solution.py
+++ b/solution.py
@@ -12,7 +12,7 @@
 CHIPS = 4
 PARTS = 8
 NS = 2 * PARTS
-WHOLE = 4
+WHOLE = 2
 LAG = 3
 SLOTS = 4
 F32, BF16 = jnp.float32, jnp.bfloat16
@@ -174,7 +174,7 @@
             self.place = z if d == 0 else last - z
             self.step = 2 if d == 0 else -2
             self.small = pl.ds(d * quarter, quarter)
-            self.rows = pl.ds(pl.multiple_of((2 * c + d) * quarter, quarter), quarter)
+            self.block = 2 * d + c
 
         def loads(self, n):
             d, i, p = self.d, n // 3, n % 3
@@ -192,19 +192,19 @@
             )
 
         def keep(self, n):
-            return pltpu.make_async_copy(out.at[self.d, n % SLOTS], g_ref.at[n // 3, n % 3, self.rows, :], keep_sem.at[n % SLOTS])
+            return pltpu.make_async_copy(out.at[self.d, n % SLOTS], g_ref.at[n // 3, n % 3, self.block], keep_sem.at[n % SLOTS])
 
         def spread(self, n):
             d, i, p = self.d, n // 3, n % 3
             return pltpu.make_async_remote_copy(
-                src_ref=g_ref.at[i, p, self.rows, :], dst_ref=g_ref.at[i, p, self.rows, :], send_sem=pass_send.at[d, i, p], recv_sem=pass_recv.at[d, i, p],
+                src_ref=g_ref.at[i, p, self.block], dst_ref=g_ref.at[i, p, self.block], send_sem=pass_send.at[d, i, p], recv_sem=pass_recv.at[d, i, p],
                 device_id={"dp": (dp - self.step + 2 * CHIPS) % (2 * CHIPS)}, device_id_type=MESH,
             )
 
         def share(self, n):
             d, i, p = self.d, n // 3, n % 3
             return pltpu.make_async_remote_copy(
-                src_ref=g_ref.at[i, p, self.rows, :], dst_ref=g_ref.at[i, p, self.rows, :], send_sem=mate_send.at[d, i, p], recv_sem=mate_recv.at[d, i, p],
+                src_ref=g_ref.at[i, p, self.block], dst_ref=g_ref.at[i, p, self.block], send_sem=mate_send.at[d, i, p], recv_sem=mate_recv.at[d, i, p],
                 device_id={"dp": mate}, device_id_type=MESH,
             )
 
@@ -463,7 +463,7 @@
     return pl.pallas_call(
         functools.partial(gradients_kernel, (T, D, FS, RT, RD)),
         out_shape=(
-            jax.ShapeDtypeStruct((NS, 3, D, FS), BF16),
+            jax.ShapeDtypeStruct((NS, 3, 4, D // 4, FS), BF16),
             jax.ShapeDtypeStruct((NS, 3, D // 2, FS), BF16),
             jax.ShapeDtypeStruct((NS, 3, D // 2, FS), BF16),
             jax.ShapeDtypeStruct((2, NS, 3, D // 4, FS), BF16),
@@ -507,179 +507,223 @@
     )(x, dy, w_gate, w_up, w_down)
 
 
-def adamw_kernel(count, work, split, n_in, *refs):
-    ssq_ref, g_ref = refs[:2]
-    back = refs[2 : 2 + n_in]
-    ins = refs[2 + n_in : 11 + n_in]
-    outs, gv, sem = refs[-11:-2], refs[-2], refs[-1]
+SUBS, DEEP = 4, 6
+
+
+def adamw_kernel(count, work, n_in, aliased, *refs):
+    refs = list(refs)
+
+    def take(n):
+        out, refs[:n] = refs[:n], []
+        return out
+
+    ssq_ref, g_ref = take(2)
+    back = take(n_in)
+    arrays = take(9)
+    take(9 if aliased else 0)
+    results = take(9)
+    bufs, outs = take(9), take(9)
+    gv, g_sem, in_sem, out_sem = take(4)
     quarter, FS = gv.shape[2:]
+    few, part = quarter // SUBS, FS // SUBS
     dp = lax.axis_index("dp")
     z, c = dp // 2, dp % 2
-    step = pl.program_id(0)
+    total = SUBS * len(work)
+    alone = 4 * work[0][0] + work[0][1]
+    rest = 4 * work[-1][0] + 4 - len(work)
+    run = all(4 * i + b == alone + at for at, (i, b, _) in enumerate(work))
 
     def here(k, source):
-        return pltpu.make_async_copy(source, gv.at[k], sem.at[k])
-
-    @pl.when(step == 0)
-    def _():
-        for k, (i, q, came) in enumerate(work):
-            whole = g_ref.at[i, :, pl.ds(q * quarter, quarter), :]
-            place = z if q % 2 == 0 else CHIPS - 1 - z
-            for p in range(CHIPS):
-                if came[p] is None:
-
-                    @pl.when(place == p)
-                    def _(k=k, whole=whole):
-                        here(k, whole).start()
-
-                else:
-                    for core in range(2):
-
-                        @pl.when((place == p) & (c == core))
-                        def _(k=k, at=came[p][0 if core == q // 2 else 1]):
-                            here(k, back[at].at[0]).start()
-
-    k, sub = step // split, step % split
-
-    @pl.when(sub == 0)
-    def _():
-        here(k, g_ref.at[0, :, pl.ds(0, quarter), :]).wait()
-
+        return pltpu.make_async_copy(source, gv.at[k], g_sem.at[k])
+
+    def fetch(k):
+        i, b, came = work[k]
+        place = z if b < 2 else CHIPS - 1 - z
+        for p in range(CHIPS):
+            if came[p] is None:
+
+                @pl.when(place == p)
+                def _():
+                    here(k, g_ref.at[i, :, b]).start()
+
+            else:
+                for core in range(2):
+
+                    @pl.when((place == p) & (c == core))
+                    def _(at=came[p][0 if core == b // 2 else 1]):
+                        here(k, back[at].at[0, :, b % 2]).start()
+
+    def blocks(n):
+        k, sub = n // SUBS, n % SUBS
+        at = alone + k if run else jnp.where(k == 0, alone, rest + k)
+        i, b = at // 4, at % 4
+        layer, hidden, q = 1 - i // PARTS, i % PARTS, b % 2 * 2 + b // 2
+        across = (layer, pl.ds(pl.multiple_of(q * quarter + sub * few, few), few), pl.ds(pl.multiple_of(hidden * FS, FS), FS))
+        down = (layer, pl.ds(pl.multiple_of(hidden * FS + sub * part, part), part), pl.ds(pl.multiple_of(q * quarter, quarter), quarter))
+        return across, across, down
+
+    def copies(n, inward):
+        slot, where = n % DEEP, blocks(n)
+        if inward:
+            return [pltpu.make_async_copy(arrays[k].at[where[k % 3]], bufs[k].at[slot], in_sem.at[slot, k]) for k in range(9)]
+        return [pltpu.make_async_copy(outs[k].at[slot], results[k].at[where[k % 3]], out_sem.at[slot, k]) for k in range(9)]
+
+    def start(n, inward):
+        for copy in copies(n, inward):
+            copy.start()
+
+    def wait(n, inward):
+        for copy in copies(n, inward):
+            copy.wait()
+
+    fetch(0)
+    for n in range(min(DEEP - 1, total)):
+        start(n, True)
+    for k in range(1, len(work)):
+        fetch(k)
     factor = jnp.minimum(1.0, 0.5 * lax.rsqrt(jnp.sum(ssq_ref[...]) / count + 1e-30))
-    some = quarter // split
-
-    def update(number, rows, g):
-        w_ref, m_ref, v_ref = ins[number::3]
-        g = g * factor
-        m = 0.9 * m_ref[0, rows, :] + 0.1 * g
-        v = 0.95 * v_ref[0, rows, :] + 0.05 * g * g
-        w = w_ref[0, rows, :].astype(F32)
-        outs[number][0, rows, :] = (w - 0.02 * (m * lax.rsqrt(v + 1e-8) + 0.1 * w)).astype(BF16)
-        outs[3 + number][0, rows, :] = m
-        outs[6 + number][0, rows, :] = v
-
-    def across(r, _):
-        few = some // 4
-        rows = pl.ds(pl.multiple_of(r * few, few), few)
-        there = pl.ds(pl.multiple_of(sub * some + r * few, few), few)
-        update(0, rows, gv[k, 1, there, :].astype(F32))
-        update(1, rows, gv[k, 2, there, :].astype(F32))
+
+    def piece(n, _):
+        k, sub, slot = n // SUBS, n % SUBS, n % DEEP
+
+        @pl.when(sub == 0)
+        def _():
+            here(k, g_ref.at[0, :, 0]).wait()
+
+        @pl.when(n + DEEP - 1 < total)
+        def _():
+            start(n + DEEP - 1, True)
+
+        wait(n, True)
+
+        @pl.when(n >= DEEP)
+        def _():
+            wait(n - DEEP, False)
+
+        def update(number, g):
+            g = g * factor
+            m = 0.9 * bufs[3 + number][slot] + 0.1 * g
+            v = 0.95 * bufs[6 + number][slot] + 0.05 * g * g
+            w = bufs[number][slot].astype(F32)
+            outs[number][slot] = (w - 0.02 * (m * lax.rsqrt(v + 1e-8) + 0.1 * w)).astype(BF16)
+            outs[3 + number][slot] = m
+            outs[6 + number][slot] = v
+
+        rows = pl.ds(pl.multiple_of(sub * few, few), few)
+        update(0, gv[k, 1, rows, :].astype(F32))
+        update(1, gv[k, 2, rows, :].astype(F32))
+        update(2, gv[k, 0, :, pl.ds(pl.multiple_of(sub * part, part), part)].astype(F32).T)
+        start(n, False)
         return 0
 
-    lax.fori_loop(0, 4, across, 0)
-
-    def down(r, _):
-        few = FS // 4
-        rows = pl.ds(pl.multiple_of(r * few, few), few)
-        update(2, rows, gv[k, 0, pl.ds(pl.multiple_of(sub * some, some), some), rows].astype(F32).T)
-        return 0
-
-    lax.fori_loop(0, 4, down, 0)
+    lax.fori_loop(0, total, piece, 0)
+    lax.fori_loop(max(total - DEEP, 0), total, lambda n, _: (wait(n, False), 0)[1], 0)
 
 
 def adamw(ssq, g, arrays, results, listed, back):
-    _, _, D, FS = g.shape
-    quarter = D // 4
-    split = 2 if quarter % 256 == 0 else 1
-    some = quarter // split
-    first, base = listed[0][:2], listed[-1][0]
-    alone = 4 * first[0] + first[1]
-    rest = 4 * base + 4 - len(listed)
-
-    def number(s):
-        k = s // split
-        if all(4 * i + q == alone + at for at, (i, q, _) in enumerate(listed)):
-            return alone + k
-        return jnp.where(k == 0, alone, rest + k)
-
-    def across(s):
-        n = number(s)
-        return 1 - n // 4 // PARTS, n % 4 * split + s % split, n // 4 % PARTS
-
-    def down(s):
-        n = number(s)
-        return 1 - n // 4 // PARTS, n // 4 % PARTS, n % 4 * split + s % split
-
-    specs = [pl.BlockSpec((1, some, FS), across), pl.BlockSpec((1, some, FS), across), pl.BlockSpec((1, FS, some), down)] * 3
+    _, _, _, quarter, FS = g.shape
     anywhere = pl.BlockSpec(memory_space=pl.ANY)
-    count = 3 * g.shape[0] * D * FS
     size = 3 * len(listed) * quarter * FS
     ins = [ssq, g, *back, *arrays, *(results or ())]
+    shapes = [(DEEP, quarter // SUBS, FS)] * 2 + [(DEEP, FS // SUBS, quarter)]
+    bufs = [pltpu.VMEM(shapes[k % 3], a.dtype) for k, a in enumerate(arrays)]
     return pl.pallas_call(
-        functools.partial(adamw_kernel, float(count), listed, split, len(back)),
-        grid=(len(listed) * split,),
-        in_specs=[pl.BlockSpec(ssq.shape, lambda s: (0, 0, 0))] + [anywhere] * (1 + len(back)) + specs + [anywhere] * (9 if results else 0),
-        out_specs=specs,
+        functools.partial(adamw_kernel, float(g.size), listed, len(back), bool(results)),
+        in_specs=[pl.BlockSpec(memory_space=pltpu.VMEM)] + [anywhere] * (len(ins) - 1),
+        out_specs=[anywhere] * 9,
         out_shape=[jax.ShapeDtypeStruct(a.shape, a.dtype) for a in arrays],
         input_output_aliases={len(ins) - 9 + k: k for k in range(9)} if results else {},
-        scratch_shapes=[pltpu.VMEM((len(listed), 3, quarter, FS), BF16), pltpu.SemaphoreType.DMA((len(listed),))],
-        compiler_params=pltpu.CompilerParams(dimension_semantics=("arbitrary",), vmem_limit_bytes=66_000_000),
-        cost_estimate=pl.CostEstimate(flops=COST * size, bytes_accessed=22 * size, transcendentals=size),
+        scratch_shapes=[
+            *bufs,
+            *bufs,
+            pltpu.VMEM((len(listed), 3, quarter, FS), BF16),
+            pltpu.SemaphoreType.DMA((len(listed),)),
+            pltpu.SemaphoreType.DMA((DEEP, 9)),
+            pltpu.SemaphoreType.DMA((DEEP, 9)),
+        ],
+        compiler_params=pltpu.CompilerParams(vmem_limit_bytes=66_000_000),
+        cost_estimate=pl.CostEstimate(flops=16 * size, bytes_accessed=22 * size, transcendentals=size),
         name="adamw",
     )(*ins)
 
 
-COST = 16
+def load_kernel(i, g_ref, _, sent_ref, buf, sem):
+    dp = lax.axis_index("dp")
+    z, c = dp // 2, dp % 2
+
+    @pl.when(z == (CHIPS - 1) * (1 - c))
+    def _():
+        pieces = buf.shape[0]
+        loads = [pltpu.make_async_copy(g_ref.at[i, p, pl.ds(2 * c, 2)], buf.at[p], sem.at[0, p]) for p in range(pieces)]
+        stores = [pltpu.make_async_copy(buf.at[p], sent_ref.at[0, p], sem.at[1, p]) for p in range(pieces)]
+        for load in loads:
+            load.start()
+        for load, store in zip(loads, stores, strict=True):
+            load.wait()
+            store.start()
+        for store in stores:
+            store.wait()
+
+
+def load(g, i, came):
+    anywhere = pl.BlockSpec(memory_space=pl.ANY)
+    return pl.pallas_call(
+        functools.partial(load_kernel, i),
+        in_specs=[anywhere, anywhere],
+        out_specs=anywhere,
+        out_shape=jax.ShapeDtypeStruct(came.shape, came.dtype),
+        input_output_aliases={1: 0},
+        scratch_shapes=[pltpu.VMEM(came.shape[1:], BF16), pltpu.SemaphoreType.DMA((2, 3))],
+        compiler_params=pltpu.CompilerParams(vmem_limit_bytes=66_000_000),
+        cost_estimate=pl.CostEstimate(flops=came.size, bytes_accessed=4 * came.size, transcendentals=0),
+        name="load",
+    )(g, came)
 
 
 def finish(g, ssq, arrays):
-    _, _, D, FS = g.shape
-    quarter = D // 4
+    _, _, _, quarter, FS = g.shape
     last = CHIPS - 1
     dp = lax.axis_index("dp")
     z, c = dp // 2, dp % 2
+    place = jnp.where(c == 0, z, last - z)
     stages = NS - WHOLE
-    ready = [(i, q, (None,) * CHIPS) for i in range(WHOLE) for q in range(4)]
-    back, results = [], None
-    index = {}
-
-    def kept(i, d, g=g):
-        return lax.dynamic_slice(g, (jnp.asarray(i, jnp.int32), jnp.int32(0), (2 * c + d) * quarter, jnp.int32(0)), (1, 3, quarter, FS))
+    ready = [(i, b, (None,) * CHIPS) for i in range(WHOLE) for b in range(4)]
+    first = min(5, 2 * WHOLE)
+    extra = 4 * WHOLE - 2 * first
+    back, index, results = [], {}, None
 
     def units(u):
-        came = []
-        for d in range(2):
-            came.append(tuple(index[u - p, d] if p < last and u >= p else None for p in range(CHIPS)))
-        return [(WHOLE + u, q, came[q % 2]) for q in range(4)]
+        came = tuple(index[u - p] if p < last and u >= p else None for p in range(CHIPS))
+        return [(WHOLE + u, b, came) for b in range(4)]
 
     def update(results, listed):
         used = sorted({at for _, _, came in listed for pair in came if pair for at in pair})
         where = {at: k for k, at in enumerate(used)}
-        listed = [(i, q, tuple(pair and tuple(where[at] for at in pair) for pair in came)) for i, q, came in listed]
+        listed = [(i, b, tuple(pair and tuple(where[at] for at in pair) for pair in came)) for i, b, came in listed]
         return adamw(ssq, g, arrays, results, listed, [back[at] for at in used])
 
-    newest, pending = [None, None], []
-    extra = 4 * WHOLE - 2 * 5
+    def device(place, core):
+        return 2 * (place if core == 0 else last - place) + core
+
+    sent = lax.dynamic_slice(g, (WHOLE + place - 1, jnp.int32(0), 2 * c, jnp.int32(0), jnp.int32(0)), (1, 3, 2, quarter, FS))
+    pending = None
     for s in range(stages + 2):
-        for at, swaps in pending:
-            back[at + 1] = lax.ppermute(back[at], "dp", swaps)
-        pending = []
-        at_hand = g
-        if s > 0:
-            at_hand, *newest = lax.optimization_barrier((g, *newest))
-        for d in range(2 if s < stages else 0):
-            place = z if d == 0 else last - z
-            if s == 0:
-                sent = kept(WHOLE + place - 1, d)
-            elif s + last - 1 < stages:
-                sent = jnp.where(place == last, kept(WHOLE + s + last - 1, d, at_hand), newest[d])
-            else:
-                sent = newest[d]
-            moves = []
-            for p in range(1, CHIPS):
-                if s + p - 1 < stages:
-                    for core in range(2):
-                        source, target = (p, p - 1) if d == 0 else (last - p, last - p + 1)
-                        moves.append((2 * source + core, 2 * target + core))
-            newest[d] = lax.ppermute(sent, "dp", moves)
-            index[s, d] = (len(back), len(back) + 1)
-            pending.append((len(back), [(to, to + 1 - 2 * (to % 2)) for _, to in moves]))
-            back += [newest[d], None]
-        many = 5 if s < 2 else 1 if s - 2 < extra else 0
+        if s < stages:
+            moves = [(device(p, core), device(p - 1, core)) for p in range(1, CHIPS) if s + p - 1 < stages for core in range(2)]
+            newest = lax.ppermute(sent, "dp", moves)
+        if pending is not None:
+            back.append(lax.ppermute(*pending))
+            pending = None
+        many = first if s < 2 else 1 if s - 2 < extra else 0
         listed, ready = ready[:many], ready[many:]
         if s >= 2:
             listed = listed + units(s - 2)
         results = update(results, listed)
+        if s < stages:
+            sent = load(g, WHOLE + s + last, newest) if s + last < stages else newest
+            index[s] = (len(back), len(back) + 1)
+            back.append(sent)
+            pending = (sent, "dp", [(to, to + 1 - 2 * (to % 2)) for _, to in moves])
     return results
 
 

time: 1080 us -> 1030 us (0.954)
  waiting for transfers between devices: 153 us -> 266 us
  Pallas kernels: 789 us -> 711 us
  starting transfers between devices: 111 us -> 52.4 us
  other arithmetic: 18.9 us -> 0 us
    ppermute x48 -> x28, waiting for transfers between devices: 153 us -> 266 us  [the longest x14 266 us: finish(): newest = lax.ppermute(sent, 'dp', moves)]
    ppermute x48 -> x28, starting transfers between devices: 111 us -> 52.4 us  [the longest x14 34.4 us: finish(): back.append(lax.ppermute(*pending))]
    pallas_call x14 -> x27, Pallas kernels: 269 us -> 225 us  [the longest x16 224 us: adamw(): pl.pallas_call(functools.partial(adamw_kernel, float(g.size), listed, len...]
    pallas_call x1, Pallas kernels: 520 us -> 486 us  [gradients(): pl.pallas_call(functools.partial(gradients_kernel, (T, D, FS, RT, RD)), o...]
    select_n x9 -> x0, other arithmetic: 18.9 us -> none  [finish(): jnp.where(place == last, kept(WHOLE + s + last - 1, d, at_hand), newest[d])]
  transfers between devices with their start and end apart: 48 -> 28, of which waited for: 21 -> 14; matrix products, arithmetic and copies ran while one was open for 0% -> 0% of each run, Pallas kernels for 23% -> 20%
where the time goes in v3:
time: 1030 us
  Pallas kernels  711 us (69%)
  waiting for transfers between devices  266 us (26%)
  starting transfers between devices  52.4 us (5%)
    pallas_call x1, Pallas kernels, gradients(): pl.pallas_call(functools.partial(gradients_kernel, (T, D, FS, RT, RD)), o...  486 us
    ppermute x14, waiting for transfers between devices, finish(): newest = lax.ppermute(sent, 'dp', moves)  266 us
    pallas_call x16, Pallas kernels, adamw(): pl.pallas_call(functools.partial(adamw_kernel, float(g.size), listed, len...  224 us
    ppermute x14, starting transfers between devices, finish(): back.append(lax.ppermute(*pending))  34.4 us
  transfers between devices with their start and end apart: 28, of which 14 were waited for; matrix products, arithmetic and copies ran while one was open for 0% of the time, Pallas kernels for 20%

profile of v3, /device:TPU:0, one launch (start us, length us, event | category | flops | bytes accessed | tf_op | source)
XLA Modules:
  0.0 1032.7 jit_solution(14587759771227087087)
XLA Ops:
  0.7 486.0 %gradients.1 = (bf16[16,3,4,256,512]{4,3,2,1,0:T(8,128)(2,1)}, bf16[16,3,512,512]{3,2,1,0:T(8,128)(2,1)}, bf16[16,3,512,512]{3,2,1,0:T(8,128)(2,1)}, bf16[2,16,3...) custom-call(bf16[1,2048,1024]{2,1,0:T(8,128)(2,1)} %x_ref.1, ...), custom_call_target="tpu_custom_call" | custom-call | tf_op jit(solution)/shard_map/gradients/pallas_call | solution.py:463
  486.7 1.5 constant_dynamic-slice_fusion
  488.3 1.3 collective-permute-start
  489.6 21.1 %collective-permute-done._ = bf16[1,3,2,256,512]{4,3,2,1,0:T(8,128)(2,1)} collective-permute-done((bf16[1,3,2,256,512]{4,3,2,1,0:T(8,128)(2,1)S(1)}, bf16[1,3,2,256,512]{4,3,2,1,0:T(8,128)(2,1)}, u32[]{:S(2)}, u32[]{:S(2)}) %collective-permute-start) | collective-permute-done | bytes 1572896 | tf_op jit(solution)/shard_map/ppermute | solution.py:713
  510.7 0.1 load.11.refs_2_
  510.7 1.3 collective-permute-start.1
  512.0 21.3 %collective-permute-done.1._ = bf16[1,3,2,256,512]{4,3,2,1,0:T(8,128)(2,1)} collective-permute-done((bf16[1,3,2,256,512]{4,3,2,1,0:T(8,128)(2,1)}, bf16[1,3,2,256,512]{4,3,2,1,0:T(8,128)(2,1)}, u32[]{:S(2)}, u32[]{:S(2)}) %collective-permute-start.1) | collective-permute-done | bytes 1572896 | tf_op jit(solution)/shard_map/ppermute | solution.py:713
  533.4 1.3 collective-permute-start.2
  534.7 21.3 %collective-permute-done.2._ = bf16[1,3,2,256,512]{4,3,2,1,0:T(8,128)(2,1)} collective-permute-done((bf16[1,3,2,256,512]{4,3,2,1,0:T(8,128)(2,1)}, bf16[1,3,2,256,512]{4,3,2,1,0:T(8,128)(2,1)}, u32[]{:S(2)}, u32[]{:S(2)}) %collective-permute-start.2) | collective-permute-done | bytes 1572896 | tf_op jit(solution)/shard_map/ppermute | solution.py:713
  556.0 0.1 load.13.refs_6_.refs_4_.refs_2_
  556.1 1.3 collective-permute-start.3
  557.4 21.3 %collective-permute-done.3._ = bf16[1,3,2,256,512]{4,3,2,1,0:T(8,128)(2,1)} collective-permute-done((bf16[1,3,2,256,512]{4,3,2,1,0:T(8,128)(2,1)}, bf16[1,3,2,256,512]{4,3,2,1,0:T(8,128)(2,1)}, u32[]{:S(2)}, u32[]{:S(2)}) %collective-permute-start.3) | collective-permute-done | bytes 1572896 | tf_op jit(solution)/shard_map/ppermute | solution.py:713
  578.7 0.1 load.14.refs_6_.refs_4_.refs_2_
  578.8 1.3 collective-permute-start.4
  580.1 21.3 %collective-permute-done.4._ = bf16[1,3,2,256,512]{4,3,2,1,0:T(8,128)(2,1)} collective-permute-done((bf16[1,3,2,256,512]{4,3,2,1,0:T(8,128)(2,1)}, bf16[1,3,2,256,512]{4,3,2,1,0:T(8,128)(2,1)}, u32[]{:S(2)}, u32[]{:S(2)}) %collective-permute-start.4) | collective-permute-done | bytes 1572896 | tf_op jit(solution)/shard_map/ppermute | solution.py:713
  601.5 1.3 collective-permute-start.5
  602.8 21.3 %collective-permute-done.5._ = bf16[1,3,2,256,512]{4,3,2,1,0:T(8,128)(2,1)} collective-permute-done((bf16[1,3,2,256,512]{4,3,2,1,0:T(8,128)(2,1)}, bf16[1,3,2,256,512]{4,3,2,1,0:T(8,128)(2,1)}, u32[]{:S(2)}, u32[]{:S(2)}) %collective-permute-start.5) | collective-permute-done | bytes 1572896 | tf_op jit(solution)/shard_map/ppermute | solution.py:713
  624.1 0.1 load.16.refs_6_.refs_4_.refs_2_
  624.2 1.3 collective-permute-start.6
  625.5 21.3 %collective-permute-done.6._ = bf16[1,3,2,256,512]{4,3,2,1,0:T(8,128)(2,1)} collective-permute-done((bf16[1,3,2,256,512]{4,3,2,1,0:T(8,128)(2,1)}, bf16[1,3,2,256,512]{4,3,2,1,0:T(8,128)(2,1)}, u32[]{:S(2)}, u32[]{:S(2)}) %collective-permute-start.6) | collective-permute-done | bytes 1572896 | tf_op jit(solution)/shard_map/ppermute | solution.py:713
  646.9 1.3 collective-permute-start.7
  648.2 21.3 %collective-permute-done.7._ = bf16[1,3,2,256,512]{4,3,2,1,0:T(8,128)(2,1)} collective-permute-done((bf16[1,3,2,256,512]{4,3,2,1,0:T(8,128)(2,1)}, bf16[1,3,2,256,512]{4,3,2,1,0:T(8,128)(2,1)}, u32[]{:S(2)}, u32[]{:S(2)}) %collective-permute-start.7) | collective-permute-done | bytes 1572896 | tf_op jit(solution)/shard_map/ppermute | solution.py:713
  669.6 1.3 collective-permute-start.8
  670.9 21.3 %collective-permute-done.8._ = bf16[1,3,2,256,512]{4,3,2,1,0:T(8,128)(2,1)} collective-permute-done((bf16[1,3,2,256,512]{4,3,2,1,0:T(8,128)(2,1)}, bf16[1,3,2,256,512]{4,3,2,1,0:T(8,128)(2,1)}, u32[]{:S(2)}, u32[]{:S(2)}) %collective-permute-start.8) | collective-permute-done | bytes 1572896 | tf_op jit(solution)/shard_map/ppermute | solution.py:713
  692.2 1.3 collective-permute-start.9
  693.5 21.3 %collective-permute-done.9._ = bf16[1,3,2,256,512]{4,3,2,1,0:T(8,128)(2,1)} collective-permute-done((bf16[1,3,2,256,512]{4,3,2,1,0:T(8,128)(2,1)}, bf16[1,3,2,256,512]{4,3,2,1,0:T(8,128)(2,1)}, u32[]{:S(2)}, u32[]{:S(2)}) %collective-permute-start.9) | collective-permute-done | bytes 1572896 | tf_op jit(solution)/shard_map/ppermute | solution.py:713
  714.9 1.3 collective-permute-start.10
  716.2 2.5 collective-permute-start.27
  718.7 18.9 %collective-permute-done.10._ = bf16[1,3,2,256,512]{4,3,2,1,0:T(8,128)(2,1)} collective-permute-done((bf16[1,3,2,256,512]{4,3,2,1,0:T(8,128)(2,1)}, bf16[1,3,2,256,512]{4,3,2,1,0:T(8,128)(2,1)}, u32[]{:S(2)}, u32[]{:S(2)}) %collective-permute-start.10) | collective-permute-done | bytes 1572896 | tf_op jit(solution)/shard_map/ppermute | solution.py:713
  737.6 1.3 collective-permute-start.11
  738.9 2.5 collective-permute-start.26
  741.4 2.5 collective-permute-start.25
  743.9 2.4 collective-permute-start.24
  746.3 2.5 collective-permute-start.23
  748.8 11.5 %collective-permute-done.11.refs_6_.refs_4_.refs_2_ = bf16[1,3,2,256,512]{4,3,2,1,0:T(8,128)(2,1)} collective-permute-done((bf16[1,3,2,256,512]{4,3,2,1,0:T(8,128)(2,1)}, bf16[1,3,2,256,512]{4,3,2,1,0:T(8,128)(2,1)}, u32[]{:S(2)}, u32[]{:S(2)}) %collective-permute-start.11) | collective-permute-done | bytes 1572896 | tf_op jit(solution)/shard_map/ppermute | solution.py:713
  760.3 1.3 collective-permute-start.13
  761.6 2.5 collective-permute-start.22
  764.1 2.4 collective-permute-start.21
  766.5 2.4 collective-permute-start.20
  768.9 2.5 collective-permute-start.19
  771.4 11.5 %collective-permute-done.13.refs_6_.refs_4_ = bf16[1,3,2,256,512]{4,3,2,1,0:T(8,128)(2,1)} collective-permute-done((bf16[1,3,2,256,512]{4,3,2,1,0:T(8,128)(2,1)}, bf16[1,3,2,256,512]{4,3,2,1,0:T(8,128)(2,1)}, u32[]{:S(2)}, u32[]{:S(2)}) %collective-permute-start.13) | collective-permute-done | bytes 1572896 | tf_op jit(solution)/shard_map/ppermute | solution.py:713
  782.9 1.3 collective-permute-start.15
  784.2 2.5 collective-permute-start.18
  786.6 2.4 collective-permute-start.17
  789.1 2.4 collective-permute-start.12
  791.5 2.5 collective-permute-start.14
  793.9 11.5 %collective-permute-done.15.refs_6_ = bf16[1,3,2,256,512]{4,3,2,1,0:T(8,128)(2,1)} collective-permute-done((bf16[1,3,2,256,512]{4,3,2,1,0:T(8,128)(2,1)}, bf16[1,3,2,256,512]{4,3,2,1,0:T(8,128)(2,1)}, u32[]{:S(2)}, u32[]{:S(2)}) %collective-permute-start.15) | collective-permute-done | bytes 1572896 | tf_op jit(solution)/shard_map/ppermute | solution.py:713
  805.5 2.4 collective-permute-start.16
  807.9 14.1 %adamw.16 = (bf16[2,1024,4096]{2,1,0:T(8,128)(2,1)}, bf16[2,1024,4096]{2,1,0:T(8,128)(2,1)}, bf16[2,4096,1024]{2,1,0:T(8,128)(2,1)}, f32[2,1024,4096]{2,1,0:T(8,...) custom-call(f32[4,8,512]{2,1,0:T(8,128)} %get-tuple-element.146.refs, ...), custom_call_target="tpu_custom_call" | custom-call | flops 25165824 | bytes 34603008 | tf_op jit(solution)/shard_map/adamw/pallas_call | solution.py:630
  822.1 14.2 %adamw.17 = (bf16[2,1024,4096]{2,1,0:T(8,128)(2,1)}, bf16[2,1024,4096]{2,1,0:T(8,128)(2,1)}, bf16[2,4096,1024]{2,1,0:T(8,128)(2,1)}, f32[2,1024,4096]{2,1,0:T(8,...) custom-call(f32[4,8,512]{2,1,0:T(8,128)} %get-tuple-element.146.refs, ...), custom_call_target="tpu_custom_call", output_to_operand_aliasing={{0}: (11, {}), {1}: (12, {}), {2}: (13, {}), {3}: (14, {}),... | custom-call | flops 25165824 | bytes 34603008 | tf_op jit(solution)/shard_map/adamw/pallas_call | solution.py:630
  836.3 14.1 %adamw.18 = (bf16[2,1024,4096]{2,1,0:T(8,128)(2,1)}, bf16[2,1024,4096]{2,1,0:T(8,128)(2,1)}, bf16[2,4096,1024]{2,1,0:T(8,128)(2,1)}, f32[2,1024,4096]{2,1,0:T(8,...) custom-call(f32[4,8,512]{2,1,0:T(8,128)} %get-tuple-element.146.refs, ...), custom_call_target="tpu_custom_call", output_to_operand_aliasing={{0}: (13, {}), {1}: (14, {}), {2}: (15, {}), {3}: (16, {}),... | custom-call | flops 25165824 | bytes 34603008 | tf_op jit(solution)/shard_map/adamw/pallas_call | solution.py:630
  850.4 14.0 %adamw.19 = (bf16[2,1024,4096]{2,1,0:T(8,128)(2,1)}, bf16[2,1024,4096]{2,1,0:T(8,128)(2,1)}, bf16[2,4096,1024]{2,1,0:T(8,128)(2,1)}, f32[2,1024,4096]{2,1,0:T(8,...) custom-call(f32[4,8,512]{2,1,0:T(8,128)} %get-tuple-element.146.refs, ...), custom_call_target="tpu_custom_call", output_to_operand_aliasing={{0}: (15, {}), {1}: (16, {}), {2}: (17, {}), {3}: (18, {}),... | custom-call | flops 25165824 | bytes 34603008 | tf_op jit(solution)/shard_map/adamw/pallas_call | solution.py:630
  864.5 14.0 %adamw.20 = (bf16[2,1024,4096]{2,1,0:T(8,128)(2,1)}, bf16[2,1024,4096]{2,1,0:T(8,128)(2,1)}, bf16[2,4096,1024]{2,1,0:T(8,128)(2,1)}, f32[2,1024,4096]{2,1,0:T(8,...) custom-call(f32[4,8,512]{2,1,0:T(8,128)} %get-tuple-element.146.refs, ...), custom_call_target="tpu_custom_call", output_to_operand_aliasing={{0}: (17, {}), {1}: (18, {}), {2}: (19, {}), {3}: (20, {}),... | custom-call | flops 25165824 | bytes 34603008 | tf_op jit(solution)/shard_map/adamw/pallas_call | solution.py:630
  878.5 14.0 %adamw.21 = (bf16[2,1024,4096]{2,1,0:T(8,128)(2,1)}, bf16[2,1024,4096]{2,1,0:T(8,128)(2,1)}, bf16[2,4096,1024]{2,1,0:T(8,128)(2,1)}, f32[2,1024,4096]{2,1,0:T(8,...) custom-call(f32[4,8,512]{2,1,0:T(8,128)} %get-tuple-element.146.refs, ...), custom_call_target="tpu_custom_call", output_to_operand_aliasing={{0}: (17, {}), {1}: (18, {}), {2}: (19, {}), {3}: (20, {}),... | custom-call | flops 25165824 | bytes 34603008 | tf_op jit(solution)/shard_map/adamw/pallas_call | solution.py:630
  892.5 14.0 %adamw.22 = (bf16[2,1024,4096]{2,1,0:T(8,128)(2,1)}, bf16[2,1024,4096]{2,1,0:T(8,128)(2,1)}, bf16[2,4096,1024]{2,1,0:T(8,128)(2,1)}, f32[2,1024,4096]{2,1,0:T(8,...) custom-call(f32[4,8,512]{2,1,0:T(8,128)} %get-tuple-element.146.refs, ...), custom_call_target="tpu_custom_call", output_to_operand_aliasing={{0}: (17, {}), {1}: (18, {}), {2}: (19, {}), {3}: (20, {}),... | custom-call | flops 25165824 | bytes 34603008 | tf_op jit(solution)/shard_map/adamw/pallas_call | solution.py:630
  906.5 14.0 %adamw.23 = (bf16[2,1024,4096]{2,1,0:T(8,128)(2,1)}, bf16[2,1024,4096]{2,1,0:T(8,128)(2,1)}, bf16[2,4096,1024]{2,1,0:T(8,128)(2,1)}, f32[2,1024,4096]{2,1,0:T(8,...) custom-call(f32[4,8,512]{2,1,0:T(8,128)} %get-tuple-element.146.refs, ...), custom_call_target="tpu_custom_call", output_to_operand_aliasing={{0}: (17, {}), {1}: (18, {}), {2}: (19, {}), {3}: (20, {}),... | custom-call | flops 25165824 | bytes 34603008 | tf_op jit(solution)/shard_map/adamw/pallas_call | solution.py:630
  920.5 14.0 %adamw.24 = (bf16[2,1024,4096]{2,1,0:T(8,128)(2,1)}, bf16[2,1024,4096]{2,1,0:T(8,128)(2,1)}, bf16[2,4096,1024]{2,1,0:T(8,128)(2,1)}, f32[2,1024,4096]{2,1,0:T(8,...) custom-call(f32[4,8,512]{2,1,0:T(8,128)} %get-tuple-element.146.refs, ...), custom_call_target="tpu_custom_call", output_to_operand_aliasing={{0}: (17, {}), {1}: (18, {}), {2}: (19, {}), {3}: (20, {}),... | custom-call | flops 25165824 | bytes 34603008 | tf_op jit(solution)/shard_map/adamw/pallas_call | solution.py:630
  934.5 14.0 %adamw.25 = (bf16[2,1024,4096]{2,1,0:T(8,128)(2,1)}, bf16[2,1024,4096]{2,1,0:T(8,128)(2,1)}, bf16[2,4096,1024]{2,1,0:T(8,128)(2,1)}, f32[2,1024,4096]{2,1,0:T(8,...) custom-call(f32[4,8,512]{2,1,0:T(8,128)} %get-tuple-element.146.refs, ...), custom_call_target="tpu_custom_call", output_to_operand_aliasing={{0}: (17, {}), {1}: (18, {}), {2}: (19, {}), {3}: (20, {}),... | custom-call | flops 25165824 | bytes 34603008 | tf_op jit(solution)/shard_map/adamw/pallas_call | solution.py:630
  948.5 14.0 %adamw.26 = (bf16[2,1024,4096]{2,1,0:T(8,128)(2,1)}, bf16[2,1024,4096]{2,1,0:T(8,128)(2,1)}, bf16[2,4096,1024]{2,1,0:T(8,128)(2,1)}, f32[2,1024,4096]{2,1,0:T(8,...) custom-call(f32[4,8,512]{2,1,0:T(8,128)} %get-tuple-element.146.refs, ...), custom_call_target="tpu_custom_call", output_to_operand_aliasing={{0}: (17, {}), {1}: (18, {}), {2}: (19, {}), {3}: (20, {}),... | custom-call | flops 25165824 | bytes 34603008 | tf_op jit(solution)/shard_map/adamw/pallas_call | solution.py:630
  962.5 14.0 %adamw.27 = (bf16[2,1024,4096]{2,1,0:T(8,128)(2,1)}, bf16[2,1024,4096]{2,1,0:T(8,128)(2,1)}, bf16[2,4096,1024]{2,1,0:T(8,128)(2,1)}, f32[2,1024,4096]{2,1,0:T(8,...) custom-call(f32[4,8,512]{2,1,0:T(8,128)} %get-tuple-element.146.refs, ...), custom_call_target="tpu_custom_call", output_to_operand_aliasing={{0}: (17, {}), {1}: (18, {}), {2}: (19, {}), {3}: (20, {}),... | custom-call | flops 25165824 | bytes 34603008 | tf_op jit(solution)/shard_map/adamw/pallas_call | solution.py:630
  976.5 14.0 %adamw.28 = (bf16[2,1024,4096]{2,1,0:T(8,128)(2,1)}, bf16[2,1024,4096]{2,1,0:T(8,128)(2,1)}, bf16[2,4096,1024]{2,1,0:T(8,128)(2,1)}, f32[2,1024,4096]{2,1,0:T(8,...) custom-call(f32[4,8,512]{2,1,0:T(8,128)} %get-tuple-element.146.refs, ...), custom_call_target="tpu_custom_call", output_to_operand_aliasing={{0}: (17, {}), {1}: (18, {}), {2}: (19, {}), {3}: (20, {}),... | custom-call | flops 25165824 | bytes 34603008 | tf_op jit(solution)/shard_map/adamw/pallas_call | solution.py:630
  990.5 14.0 %adamw.29 = (bf16[2,1024,4096]{2,1,0:T(8,128)(2,1)}, bf16[2,1024,4096]{2,1,0:T(8,128)(2,1)}, bf16[2,4096,1024]{2,1,0:T(8,128)(2,1)}, f32[2,1024,4096]{2,1,0:T(8,...) custom-call(f32[4,8,512]{2,1,0:T(8,128)} %get-tuple-element.146.refs, ...), custom_call_target="tpu_custom_call", output_to_operand_aliasing={{0}: (17, {}), {1}: (18, {}), {2}: (19, {}), {3}: (20, {}),... | custom-call | flops 25165824 | bytes 34603008 | tf_op jit(solution)/shard_map/adamw/pallas_call | solution.py:630
  1004.5 14.0 %adamw.30 = (bf16[2,1024,4096]{2,1,0:T(8,128)(2,1)}, bf16[2,1024,4096]{2,1,0:T(8,128)(2,1)}, bf16[2,4096,1024]{2,1,0:T(8,128)(2,1)}, f32[2,1024,4096]{2,1,0:T(8,...) custom-call(f32[4,8,512]{2,1,0:T(8,128)} %get-tuple-element.146.refs, ...), custom_call_target="tpu_custom_call", output_to_operand_aliasing={{0}: (17, {}), {1}: (18, {}), {2}: (19, {}), {3}: (20, {}),... | custom-call | flops 25165824 | bytes 34603008 | tf_op jit(solution)/shard_map/adamw/pallas_call | solution.py:630
  1018.5 14.0 %adamw.31 = (bf16[2,1024,4096]{2,1,0:T(8,128)(2,1)}, bf16[2,1024,4096]{2,1,0:T(8,128)(2,1)}, bf16[2,4096,1024]{2,1,0:T(8,128)(2,1)}, f32[2,1024,4096]{2,1,0:T(8,...) custom-call(f32[4,8,512]{2,1,0:T(8,128)} %get-tuple-element.146.refs, ...), custom_call_target="tpu_custom_call", output_to_operand_aliasing={{0}: (17, {}), {1}: (18, {}), {2}: (19, {}), {3}: (20, {}),... | custom-call | flops 25165824 | bytes 34603008 | tf_op jit(solution)/shard_map/adamw/pallas_call | solution.py:630
  (21 shorter events, 0.4 us)
Async XLA Ops:
  488.3 22.4 %collective-permute-start = (bf16[1,3,2,256,512]{4,3,2,1,0:T(8,128)(2,1)S(1)}, bf16[1,3,2,256,512]{4,3,2,1,0:T(8,128)(2,1)}, u32[]{:S(2)}, u32[]{:S(2)}) collective-permute-start(bf16[1,3,2,256,512]{4,3,2,1,0:T(8,128)(2,1)S(1)} %constant_dynamic-slice_fusion), channel_id=1, source_target_pairs={{2,0},{5,7},{4,2},{3,5},{6,4},{1,3},{10,8},{13,15},{12,10},{11,13}... | collective-permute-start | bytes 4718600 | tf_op jit(solution)/shard_map/ppermute | solution.py:713
  510.7 22.6 %collective-permute-start.1 = (bf16[1,3,2,256,512]{4,3,2,1,0:T(8,128)(2,1)}, bf16[1,3,2,256,512]{4,3,2,1,0:T(8,128)(2,1)}, u32[]{:S(2)}, u32[]{:S(2)}) collective-permute-start(bf16[1,3,2,256,512]{4,3,2,1,0:T(8,128)(2,1)} %load.11.refs_2_), channel_id=1, source_target_pairs={{2,0},{5,7},{4,2},{3,5},{6,4},{1,3},{10,8},{13,15},{12,10},{11,13}... | collective-permute-start | bytes 4718600 | tf_op jit(solution)/shard_map/ppermute | solution.py:713
  533.4 22.6 %collective-permute-start.2 = (bf16[1,3,2,256,512]{4,3,2,1,0:T(8,128)(2,1)}, bf16[1,3,2,256,512]{4,3,2,1,0:T(8,128)(2,1)}, u32[]{:S(2)}, u32[]{:S(2)}) collective-permute-start(bf16[1,3,2,256,512]{4,3,2,1,0:T(8,128)(2,1)} %load.12.refs_4_.refs_2_), channel_id=1, source_target_pairs={{2,0},{5,7},{4,2},{3,5},{6,4},{1,3},{10,8},{13,15},{12,10},{11,13}... | collective-permute-start | bytes 4718600 | tf_op jit(solution)/shard_map/ppermute | solution.py:713
  556.1 22.6 %collective-permute-start.3 = (bf16[1,3,2,256,512]{4,3,2,1,0:T(8,128)(2,1)}, bf16[1,3,2,256,512]{4,3,2,1,0:T(8,128)(2,1)}, u32[]{:S(2)}, u32[]{:S(2)}) collective-permute-start(bf16[1,3,2,256,512]{4,3,2,1,0:T(8,128)(2,1)} %load.13.refs_6_.refs_4_.refs_2_), channel_id=1, source_target_pairs={{2,0},{5,7},{4,2},{3,5},{6,4},{1,3},{10,8},{13,15},{12,10},{11,13}... | collective-permute-start | bytes 4718600 | tf_op jit(solution)/shard_map/ppermute | solution.py:713
  578.8 22.6 %collective-permute-start.4 = (bf16[1,3,2,256,512]{4,3,2,1,0:T(8,128)(2,1)}, bf16[1,3,2,256,512]{4,3,2,1,0:T(8,128)(2,1)}, u32[]{:S(2)}, u32[]{:S(2)}) collective-permute-start(bf16[1,3,2,256,512]{4,3,2,1,0:T(8,128)(2,1)} %load.14.refs_6_.refs_4_.refs_2_), channel_id=1, source_target_pairs={{2,0},{5,7},{4,2},{3,5},{6,4},{1,3},{10,8},{13,15},{12,10},{11,13}... | collective-permute-start | bytes 4718600 | tf_op jit(solution)/shard_map/ppermute | solution.py:713
  601.5 22.6 %collective-permute-start.5 = (bf16[1,3,2,256,512]{4,3,2,1,0:T(8,128)(2,1)}, bf16[1,3,2,256,512]{4,3,2,1,0:T(8,128)(2,1)}, u32[]{:S(2)}, u32[]{:S(2)}) collective-permute-start(bf16[1,3,2,256,512]{4,3,2,1,0:T(8,128)(2,1)} %load.15.refs_6_.refs_4_.refs_2_), channel_id=1, source_target_pairs={{2,0},{5,7},{4,2},{3,5},{6,4},{1,3},{10,8},{13,15},{12,10},{11,13}... | collective-permute-start | bytes 4718600 | tf_op jit(solution)/shard_map/ppermute | solution.py:713
  624.2 22.6 %collective-permute-start.6 = (bf16[1,3,2,256,512]{4,3,2,1,0:T(8,128)(2,1)}, bf16[1,3,2,256,512]{4,3,2,1,0:T(8,128)(2,1)}, u32[]{:S(2)}, u32[]{:S(2)}) collective-permute-start(bf16[1,3,2,256,512]{4,3,2,1,0:T(8,128)(2,1)} %load.16.refs_6_.refs_4_.refs_2_), channel_id=1, source_target_pairs={{2,0},{5,7},{4,2},{3,5},{6,4},{1,3},{10,8},{13,15},{12,10},{11,13}... | collective-permute-start | bytes 4718600 | tf_op jit(solution)/shard_map/ppermute | solution.py:713
  646.9 22.6 %collective-permute-start.7 = (bf16[1,3,2,256,512]{4,3,2,1,0:T(8,128)(2,1)}, bf16[1,3,2,256,512]{4,3,2,1,0:T(8,128)(2,1)}, u32[]{:S(2)}, u32[]{:S(2)}) collective-permute-start(bf16[1,3,2,256,512]{4,3,2,1,0:T(8,128)(2,1)} %load.17.refs_6_.refs_4_.refs_2_), channel_id=1, source_target_pairs={{2,0},{5,7},{4,2},{3,5},{6,4},{1,3},{10,8},{13,15},{12,10},{11,13}... | collective-permute-start | bytes 4718600 | tf_op jit(solution)/shard_map/ppermute | solution.py:713
  669.6 22.6 %collective-permute-start.8 = (bf16[1,3,2,256,512]{4,3,2,1,0:T(8,128)(2,1)}, bf16[1,3,2,256,512]{4,3,2,1,0:T(8,128)(2,1)}, u32[]{:S(2)}, u32[]{:S(2)}) collective-permute-start(bf16[1,3,2,256,512]{4,3,2,1,0:T(8,128)(2,1)} %load.18.refs_6_.refs_4_.refs_2_), channel_id=1, source_target_pairs={{2,0},{5,7},{4,2},{3,5},{6,4},{1,3},{10,8},{13,15},{12,10},{11,13}... | collective-permute-start | bytes 4718600 | tf_op jit(solution)/shard_map/ppermute | solution.py:713
  692.2 22.6 %collective-permute-start.9 = (bf16[1,3,2,256,512]{4,3,2,1,0:T(8,128)(2,1)}, bf16[1,3,2,256,512]{4,3,2,1,0:T(8,128)(2,1)}, u32[]{:S(2)}, u32[]{:S(2)}) collective-permute-start(bf16[1,3,2,256,512]{4,3,2,1,0:T(8,128)(2,1)} %load.19.refs_6_.refs_4_.refs_2_), channel_id=1, source_target_pairs={{2,0},{5,7},{4,2},{3,5},{6,4},{1,3},{10,8},{13,15},{12,10},{11,13}... | collective-permute-start | bytes 4718600 | tf_op jit(solution)/shard_map/ppermute | solution.py:713
  714.9 22.6 %collective-permute-start.10 = (bf16[1,3,2,256,512]{4,3,2,1,0:T(8,128)(2,1)}, bf16[1,3,2,256,512]{4,3,2,1,0:T(8,128)(2,1)}, u32[]{:S(2)}, u32[]{:S(2)}) collective-permute-start(bf16[1,3,2,256,512]{4,3,2,1,0:T(8,128)(2,1)} %load.20.refs_6_.refs_4_.refs_2_), channel_id=1, source_target_pairs={{2,0},{5,7},{4,2},{3,5},{6,4},{1,3},{10,8},{13,15},{12,10},{11,13}... | collective-permute-start | bytes 4718600 | tf_op jit(solution)/shard_map/ppermute | solution.py:713
  716.2 30.1 %collective-permute-start.27 = (bf16[1,3,2,256,512]{4,3,2,1,0:T(8,128)(2,1)}, bf16[1,3,2,256,512]{4,3,2,1,0:T(8,128)(2,1)}, u32[]{:S(2)}, u32[]{:S(2)}) collective-permute-start(bf16[1,3,2,256,512]{4,3,2,1,0:T(8,128)(2,1)} %load.11.refs_2_), channel_id=1, source_target_pairs={{0,1},{7,6},{2,3},{5,4},{4,5},{3,2},{8,9},{15,14},{10,11},{13,12},... | collective-permute-start | bytes 4718600 | tf_op jit(solution)/shard_map/ppermute | solution.py:715
  737.6 22.6 %collective-permute-start.11 = (bf16[1,3,2,256,512]{4,3,2,1,0:T(8,128)(2,1)}, bf16[1,3,2,256,512]{4,3,2,1,0:T(8,128)(2,1)}, u32[]{:S(2)}, u32[]{:S(2)}) collective-permute-start(bf16[1,3,2,256,512]{4,3,2,1,0:T(8,128)(2,1)} %load.21.refs_6_.refs_4_.refs_2_), channel_id=1, source_target_pairs={{2,0},{5,7},{4,2},{3,5},{6,4},{1,3},{10,8},{13,15},{12,10},{11,13}... | collective-permute-start | bytes 4718600 | tf_op jit(solution)/shard_map/ppermute | solution.py:713
  738.9 22.6 %collective-permute-start.26 = (bf16[1,3,2,256,512]{4,3,2,1,0:T(8,128)(2,1)}, bf16[1,3,2,256,512]{4,3,2,1,0:T(8,128)(2,1)}, u32[]{:S(2)}, u32[]{:S(2)}) collective-permute-start(bf16[1,3,2,256,512]{4,3,2,1,0:T(8,128)(2,1)} %load.12.refs_4_.refs_2_), channel_id=1, source_target_pairs={{0,1},{7,6},{2,3},{5,4},{4,5},{3,2},{8,9},{15,14},{10,11},{13,12},... | collective-permute-start | bytes 4718600 | tf_op jit(solution)/shard_map/ppermute | solution.py:715
  741.4 22.7 %collective-permute-start.25 = (bf16[1,3,2,256,512]{4,3,2,1,0:T(8,128)(2,1)}, bf16[1,3,2,256,512]{4,3,2,1,0:T(8,128)(2,1)}, u32[]{:S(2)}, u32[]{:S(2)}) collective-permute-start(bf16[1,3,2,256,512]{4,3,2,1,0:T(8,128)(2,1)} %load.13.refs_6_.refs_4_.refs_2_), channel_id=1, source_target_pairs={{0,1},{7,6},{2,3},{5,4},{4,5},{3,2},{8,9},{15,14},{10,11},{13,12},... | collective-permute-start | bytes 4718600 | tf_op jit(solution)/shard_map/ppermute | solution.py:715
  743.9 22.6 %collective-permute-start.24 = (bf16[1,3,2,256,512]{4,3,2,1,0:T(8,128)(2,1)}, bf16[1,3,2,256,512]{4,3,2,1,0:T(8,128)(2,1)}, u32[]{:S(2)}, u32[]{:S(2)}) collective-permute-start(bf16[1,3,2,256,512]{4,3,2,1,0:T(8,128)(2,1)} %load.14.refs_6_.refs_4_.refs_2_), channel_id=1, source_target_pairs={{0,1},{7,6},{2,3},{5,4},{4,5},{3,2},{8,9},{15,14},{10,11},{13,12},... | collective-permute-start | bytes 4718600 | tf_op jit(solution)/shard_map/ppermute | solution.py:715
  746.3 22.6 %collective-permute-start.23 = (bf16[1,3,2,256,512]{4,3,2,1,0:T(8,128)(2,1)}, bf16[1,3,2,256,512]{4,3,2,1,0:T(8,128)(2,1)}, u32[]{:S(2)}, u32[]{:S(2)}) collective-permute-start(bf16[1,3,2,256,512]{4,3,2,1,0:T(8,128)(2,1)} %load.15.refs_6_.refs_4_.refs_2_), channel_id=1, source_target_pairs={{0,1},{7,6},{2,3},{5,4},{4,5},{3,2},{8,9},{15,14},{10,11},{13,12},... | collective-permute-start | bytes 4718600 | tf_op jit(solution)/shard_map/ppermute | solution.py:715
  760.3 22.6 %collective-permute-start.13 = (bf16[1,3,2,256,512]{4,3,2,1,0:T(8,128)(2,1)}, bf16[1,3,2,256,512]{4,3,2,1,0:T(8,128)(2,1)}, u32[]{:S(2)}, u32[]{:S(2)}) collective-permute-start(bf16[1,3,2,256,512]{4,3,2,1,0:T(8,128)(2,1)} %collective-permute-done.11.refs_6_.refs_4_.refs_2_), channel_id=1, source_target_pairs={{2,0},{5,7},{4,2},{3,5},{10,8},{13,15},{12,10},{11,13},{18,16},{21... | collective-permute-start | bytes 4718600 | tf_op jit(solution)/shard_map/ppermute | solution.py:713
  761.6 22.6 %collective-permute-start.22 = (bf16[1,3,2,256,512]{4,3,2,1,0:T(8,128)(2,1)}, bf16[1,3,2,256,512]{4,3,2,1,0:T(8,128)(2,1)}, u32[]{:S(2)}, u32[]{:S(2)}) collective-permute-start(bf16[1,3,2,256,512]{4,3,2,1,0:T(8,128)(2,1)} %load.16.refs_6_.refs_4_.refs_2_), channel_id=1, source_target_pairs={{0,1},{7,6},{2,3},{5,4},{4,5},{3,2},{8,9},{15,14},{10,11},{13,12},... | collective-permute-start | bytes 4718600 | tf_op jit(solution)/shard_map/ppermute | solution.py:715
  764.1 22.6 %collective-permute-start.21 = (bf16[1,3,2,256,512]{4,3,2,1,0:T(8,128)(2,1)}, bf16[1,3,2,256,512]{4,3,2,1,0:T(8,128)(2,1)}, u32[]{:S(2)}, u32[]{:S(2)}) collective-permute-start(bf16[1,3,2,256,512]{4,3,2,1,0:T(8,128)(2,1)} %load.17.refs_6_.refs_4_.refs_2_), channel_id=1, source_target_pairs={{0,1},{7,6},{2,3},{5,4},{4,5},{3,2},{8,9},{15,14},{10,11},{13,12},... | collective-permute-start | bytes 4718600 | tf_op jit(solution)/shard_map/ppermute | solution.py:715
  766.5 22.5 %collective-permute-start.20 = (bf16[1,3,2,256,512]{4,3,2,1,0:T(8,128)(2,1)}, bf16[1,3,2,256,512]{4,3,2,1,0:T(8,128)(2,1)}, u32[]{:S(2)}, u32[]{:S(2)}) collective-permute-start(bf16[1,3,2,256,512]{4,3,2,1,0:T(8,128)(2,1)} %load.18.refs_6_.refs_4_.refs_2_), channel_id=1, source_target_pairs={{0,1},{7,6},{2,3},{5,4},{4,5},{3,2},{8,9},{15,14},{10,11},{13,12},... | collective-permute-start | bytes 4718600 | tf_op jit(solution)/shard_map/ppermute | solution.py:715
  768.9 22.6 %collective-permute-start.19 = (bf16[1,3,2,256,512]{4,3,2,1,0:T(8,128)(2,1)}, bf16[1,3,2,256,512]{4,3,2,1,0:T(8,128)(2,1)}, u32[]{:S(2)}, u32[]{:S(2)}) collective-permute-start(bf16[1,3,2,256,512]{4,3,2,1,0:T(8,128)(2,1)} %load.19.refs_6_.refs_4_.refs_2_), channel_id=1, source_target_pairs={{0,1},{7,6},{2,3},{5,4},{4,5},{3,2},{8,9},{15,14},{10,11},{13,12},... | collective-permute-start | bytes 4718600 | tf_op jit(solution)/shard_map/ppermute | solution.py:715
  782.9 22.6 %collective-permute-start.15 = (bf16[1,3,2,256,512]{4,3,2,1,0:T(8,128)(2,1)}, bf16[1,3,2,256,512]{4,3,2,1,0:T(8,128)(2,1)}, u32[]{:S(2)}, u32[]{:S(2)}) collective-permute-start(bf16[1,3,2,256,512]{4,3,2,1,0:T(8,128)(2,1)} %collective-permute-done.13.refs_6_.refs_4_), channel_id=1, source_target_pairs={{2,0},{5,7},{10,8},{13,15},{18,16},{21,23},{26,24},{29,31}} | collective-permute-start | bytes 4718600 | tf_op jit(solution)/shard_map/ppermute | solution.py:713
  784.2 178.3 %collective-permute-start.18 = (bf16[1,3,2,256,512]{4,3,2,1,0:T(8,128)(2,1)}, bf16[1,3,2,256,512]{4,3,2,1,0:T(8,128)(2,1)}, u32[]{:S(2)}, u32[]{:S(2)}) collective-permute-start(bf16[1,3,2,256,512]{4,3,2,1,0:T(8,128)(2,1)} %load.20.refs_6_.refs_4_.refs_2_), channel_id=1, source_target_pairs={{0,1},{7,6},{2,3},{5,4},{4,5},{3,2},{8,9},{15,14},{10,11},{13,12},... | collective-permute-start | bytes 4718600 | tf_op jit(solution)/shard_map/ppermute | solution.py:715
  786.6 189.8 %collective-permute-start.17 = (bf16[1,3,2,256,512]{4,3,2,1,0:T(8,128)(2,1)}, bf16[1,3,2,256,512]{4,3,2,1,0:T(8,128)(2,1)}, u32[]{:S(2)}, u32[]{:S(2)}) collective-permute-start(bf16[1,3,2,256,512]{4,3,2,1,0:T(8,128)(2,1)} %load.21.refs_6_.refs_4_.refs_2_), channel_id=1, source_target_pairs={{0,1},{7,6},{2,3},{5,4},{4,5},{3,2},{8,9},{15,14},{10,11},{13,12},... | collective-permute-start | bytes 4718600 | tf_op jit(solution)/shard_map/ppermute | solution.py:715
  789.1 201.4 %collective-permute-start.12 = (bf16[1,3,2,256,512]{4,3,2,1,0:T(8,128)(2,1)}, bf16[1,3,2,256,512]{4,3,2,1,0:T(8,128)(2,1)}, u32[]{:S(2)}, u32[]{:S(2)}) collective-permute-start(bf16[1,3,2,256,512]{4,3,2,1,0:T(8,128)(2,1)} %collective-permute-done.11.refs_6_.refs_4_.refs_2_), channel_id=1, source_target_pairs={{0,1},{7,6},{2,3},{5,4},{4,5},{3,2},{8,9},{15,14},{10,11},{13,12},... | collective-permute-start | bytes 4718600 | tf_op jit(solution)/shard_map/ppermute | solution.py:715
  791.5 213.0 %collective-permute-start.14 = (bf16[1,3,2,256,512]{4,3,2,1,0:T(8,128)(2,1)}, bf16[1,3,2,256,512]{4,3,2,1,0:T(8,128)(2,1)}, u32[]{:S(2)}, u32[]{:S(2)}) collective-permute-start(bf16[1,3,2,256,512]{4,3,2,1,0:T(8,128)(2,1)} %collective-permute-done.13.refs_6_.refs_4_), channel_id=1, source_target_pairs={{0,1},{7,6},{2,3},{5,4},{8,9},{15,14},{10,11},{13,12},{16,17},{23,... | collective-permute-start | bytes 4718600 | tf_op jit(solution)/shard_map/ppermute | solution.py:715
  805.5 213.0 %collective-permute-start.16 = (bf16[1,3,2,256,512]{4,3,2,1,0:T(8,128)(2,1)}, bf16[1,3,2,256,512]{4,3,2,1,0:T(8,128)(2,1)}, u32[]{:S(2)}, u32[]{:S(2)}) collective-permute-start(bf16[1,3,2,256,512]{4,3,2,1,0:T(8,128)(2,1)} %collective-permute-done.15.refs_6_), channel_id=1, source_target_pairs={{0,1},{7,6},{8,9},{15,14},{16,17},{23,22},{24,25},{31,30}} | collective-permute-start | bytes 4718600 | tf_op jit(solution)/shard_map/ppermute | solution.py:715

commit v4 on v3

--- a/solution.py
+++ b/solution.py
@@ -12,7 +12,8 @@
 CHIPS = 4
 PARTS = 8
 NS = 2 * PARTS
-WHOLE = 2
+KEPT = PARTS - 2
+WHOLE = 6
 LAG = 3
 SLOTS = 4
 F32, BF16 = jnp.float32, jnp.bfloat16
@@ -33,9 +34,9 @@
 def gradients_kernel(
     sizes,
     x_ref, dy_ref, wg_ref, wu_ref, wd_ref,
-    g_ref, own_ref, pair_ref, chain_ref, ssq_ref, h_ref,
+    g_ref, own_ref, pair_ref, chain_ref, ssq_ref, h_ref, dgu_ref,
     a, at, up, upt, acc, wgu, wd, hid, dgu, gb, st, out, ssq,
-    w_sem, io_sem, pair_send, own_sem, pair_recv, ld_sem, chain_send, chain_recv, keep_sem, pass_send, pass_recv, mate_send, mate_recv, ssq_send, ssq_recv,
+    w_sem, io_sem, dgu_sem, pair_send, own_sem, pair_recv, ld_sem, chain_send, chain_recv, keep_sem, pass_send, pass_recv, mate_send, mate_recv, ssq_send, ssq_recv,
 ):
     T, D, FS, RT, RD = sizes
     UNITS = 3 * NS
@@ -50,22 +51,34 @@
         pl.semaphore_signal(barrier, inc=1, device_id={"dp": (dp + k) % (2 * CHIPS)}, device_id_type=MESH)
 
     def weight_copies(w):
-        layer = jnp.where((w >= PARTS) & (w < 2 * PARTS), 1, 0)
-        columns = pl.ds(pl.multiple_of((w % PARTS) * FS, FS), FS)
+        phase = w // PARTS
+        layer = jnp.where((phase == 1) | (phase == 2), 1, 0)
+        part = jnp.where(phase == 2, w + KEPT, w) % PARTS
+        columns = pl.ds(pl.multiple_of(part * FS, FS), FS)
         slot = w % 2
-        return (
+        both = (
             pltpu.make_async_copy(wg_ref.at[layer, :, columns], wgu.at[slot, :, pl.ds(0, FS)], w_sem.at[slot, 0]),
             pltpu.make_async_copy(wu_ref.at[layer, :, columns], wgu.at[slot, :, pl.ds(FS, FS)], w_sem.at[slot, 1]),
-            pltpu.make_async_copy(wd_ref.at[layer, columns, :], wd.at[slot], w_sem.at[slot, 2]),
         )
+        return both, pltpu.make_async_copy(wd_ref.at[layer, columns, :], wd.at[slot], w_sem.at[slot, 2]), phase != 2
 
     def fetch(w):
-        for copy in weight_copies(w):
+        both, down, needed = weight_copies(w)
+        for copy in both:
             copy.start()
 
+        @pl.when(needed)
+        def _():
+            down.start()
+
     def fetched(w):
-        for copy in weight_copies(w):
+        both, down, needed = weight_copies(w)
+        for copy in both:
             copy.wait()
+
+        @pl.when(needed)
+        def _():
+            down.wait()
 
     def rows_of(r, size):
         return pl.ds(pl.multiple_of(r * size, size), size)
@@ -79,7 +92,7 @@
     load_x = pltpu.make_async_copy(x_ref.at[0], a, io_sem.at[0])
     load_x.start()
     fetch(0)
-    load_again = pltpu.make_async_copy(x_ref.at[0], dgu, io_sem.at[1])
+    load_again = pltpu.make_async_copy(x_ref.at[0], dgu.at[0], io_sem.at[1])
     load_again.start()
     load_dy = pltpu.make_async_copy(dy_ref.at[0], up, io_sem.at[2])
     load_dy.start()
@@ -110,15 +123,14 @@
     load_again.wait()
 
     def close_forward(rows):
-        h = dgu[rows, :].astype(F32) + acc[rows, :].astype(BF16).astype(F32)
+        h = dgu[0, rows, :].astype(F32) + acc[rows, :].astype(BF16).astype(F32)
         h = h.astype(BF16)
-        dgu[rows, :] = h
+        dgu[0, rows, :] = h
         wide = h.astype(F32)
         a[rows, :] = (wide * inverse_size(wide)).astype(BF16)
-        acc[rows, :] = jnp.zeros((RD, D), F32)
 
     over_rows(T, RD, close_forward)
-    save_h = pltpu.make_async_copy(dgu, h_ref, io_sem.at[0])
+    save_h = pltpu.make_async_copy(dgu.at[0], h_ref, io_sem.at[0])
     save_h.start()
 
     def turn(source, target):
@@ -135,16 +147,16 @@
 
     reload_x = pltpu.make_async_copy(x_ref.at[0], a, io_sem.at[1])
 
+    load_h = pltpu.make_async_copy(h_ref, dgu.at[0], io_sem.at[0])
+
     def cross_layers():
-        load_h = pltpu.make_async_copy(h_ref, dgu, io_sem.at[0])
-        load_h.start()
         reload_x.wait()
         over_rows(T, RD, norm_in_place)
         turn(a, at)
         load_h.wait()
 
         def tile(rows):
-            wide = dgu[rows, :].astype(F32)
+            wide = dgu[0, rows, :].astype(F32)
             scale = inverse_size(wide)
             da = acc[rows, :].astype(BF16).astype(F32)
             along = jnp.sum(da * wide, -1, keepdims=True) * (1.0 / D)
@@ -222,14 +234,19 @@
     def inside(n):
         return (n >= 0) & (n < UNITS)
 
+    def unit(k):
+        return jnp.where(k < 3 * PARTS, k, jnp.where(k < 3 * PARTS + PARTS, -1, k - PARTS))
+
     def start_tick(k):
-        @pl.when(inside(k - 2))
-        def _():
-            own_copy(k - 2).wait()
-            pair_copy(k - 2).wait_recv()
+        newest = unit(k - 2)
+
+        @pl.when(inside(newest))
+        def _():
+            own_copy(newest).wait()
+            pair_copy(newest).wait_recv()
 
         for way in ways:
-            n = k - 2 - LAG * way.place
+            n = unit(k - 2 - LAG * way.place)
 
             @pl.when(inside(n))
             def _(way=way, n=n):
@@ -245,7 +262,7 @@
     def finish_tick(k):
         for way in ways:
             d = way.d
-            n = k - 2 - LAG * way.place
+            n = unit(k - 2 - LAG * way.place)
 
             @pl.when(inside(n))
             def _(way=way, d=d, n=n):
@@ -284,7 +301,7 @@
                     ssq[...] += jnp.sum((total * total).reshape(quarter // 8, 8, FS), 0)
 
         for way in ways:
-            n = k - 3 - LAG * (2 * last - way.place)
+            n = unit(k - 3 - LAG * (2 * last - way.place))
 
             @pl.when(inside(n))
             def _(way=way, n=n):
@@ -304,22 +321,25 @@
                 def _():
                     way.share(n).start()
 
-    def backward(t):
-        w = PARTS + t
-        slot = w % 2
-
-        @pl.when(t == PARTS)
-        def _():
-            cross_layers()
-
+    def dgu_copy(t):
+        return pltpu.make_async_copy(dgu.at[t % 2], dgu_ref.at[t], dgu_sem.at[t % 2])
+
+    def backward(t, tick, w, early):
+        slot, half_slot = w % 2, t % 2
         fetched(w)
 
-        @pl.when(t < NS - 1)
+        @pl.when(w < 4 * PARTS - 1)
         def _():
             fetch(w + 1)
 
+        if early:
+
+            @pl.when((t >= 2) & (t < PARTS))
+            def _():
+                dgu_copy(t - 2).wait()
+
         def hidden_half(k):
-            start_tick(3 * t + k)
+            start_tick(tick + k)
 
             def tile(r):
                 rows = rows_of(k * (T // RT // 2) + r, RT)
@@ -329,17 +349,19 @@
                 s = jax.nn.sigmoid(gate)
                 silu = gate * s
                 hid[rows, :] = (silu * lift).astype(BF16)
-                dgu[rows, :FS] = (dh * lift * (s + silu * (1.0 - s))).astype(BF16)
-                dgu[rows, FS:] = (dh * silu).astype(BF16)
+                dgu[half_slot, rows, :FS] = (dh * lift * (s + silu * (1.0 - s))).astype(BF16)
+                dgu[half_slot, rows, FS:] = (dh * silu).astype(BF16)
 
             repeat(T // RT // 2, tile)
-            finish_tick(3 * t + k)
+            finish_tick(tick + k)
 
         repeat(2, hidden_half)
 
-        @pl.when(t == PARTS - 1)
-        def _():
-            reload_x.start()
+        if early:
+
+            @pl.when(t < KEPT)
+            def _():
+                dgu_copy(t).start()
 
         @pl.when(t >= 2)
         def _():
@@ -348,7 +370,7 @@
 
         def down_half(k):
             rows = half_of(jnp.where(k == 0, 1 - c, c))
-            gb[t % 2, 0, rows, :] = dot(upt[rows, :], hid[...]).astype(BF16)
+            gb[half_slot, 0, rows, :] = dot(upt[rows, :], hid[...]).astype(BF16)
 
             @pl.when(k == 0)
             def _():
@@ -363,12 +385,12 @@
         def both_half(k):
             @pl.when(k == 1)
             def _():
-                start_tick(3 * t + 2)
+                start_tick(tick + 2)
 
             rows = half_of(jnp.where(k == 0, 1 - c, c))
-            both = dot(at[rows, :], dgu[...]).astype(BF16)
-            gb[t % 2, 1, rows, :] = both[:, :FS]
-            gb[t % 2, 2, rows, :] = both[:, FS:]
+            both = dot(at[rows, :], dgu[half_slot]).astype(BF16)
+            gb[half_slot, 1, rows, :] = both[:, :FS]
+            gb[half_slot, 2, rows, :] = both[:, FS:]
 
             @pl.when(k == 0)
             def _():
@@ -379,22 +401,53 @@
             def _():
                 own_copy(3 * t + 1).start()
                 own_copy(3 * t + 2).start()
-                finish_tick(3 * t + 2)
+                finish_tick(tick + 2)
 
         repeat(2, both_half)
 
-        @pl.when(t < PARTS)
-        def _():
-            def tile(rows):
-                acc[rows, :] += dot_nt(dgu[rows, :], wgu[slot])
-
-            over_rows(T, RT, tile)
-
-    repeat(NS, backward)
+    def dgu_load(s):
+        return pltpu.make_async_copy(dgu_ref.at[s + KEPT - PARTS], dgu.at[s % 2], dgu_sem.at[s % 2])
+
+    def sum_for_a(s):
+        w = 2 * PARTS + s
+        fetched(w)
+        fetch(w + 1)
+
+        @pl.when(s >= PARTS - KEPT)
+        def _():
+            dgu_load(s).wait()
+
+        @pl.when((s >= 1) & (s < PARTS - 1))
+        def _():
+            dgu_load(s + 1).start()
+
+        @pl.when(s == PARTS - 1)
+        def _():
+            load_h.start()
+
+        start_tick(3 * PARTS + s)
+
+        def tile(rows):
+            acc[rows, :] = jnp.where(s > 0, acc[rows, :], 0.0) + dot_nt(dgu[s % 2, rows, :], wgu[w % 2])
+
+        over_rows(T, RT, tile)
+        finish_tick(3 * PARTS + s)
+
+    def slice_of(i):
+        @pl.when(i == PARTS)
+        def _():
+            reload_x.start()
+            repeat(PARTS, sum_for_a)
+            cross_layers()
+
+        later = i >= PARTS
+        backward(i, jnp.where(later, 3 * i + PARTS, 3 * i), jnp.where(later, i + 2 * PARTS, i + PARTS), True)
+
+    repeat(NS, slice_of)
 
     def drain(k):
-        start_tick(UNITS + k)
-        finish_tick(UNITS + k)
+        start_tick(UNITS + PARTS + k)
+        finish_tick(UNITS + PARTS + k)
 
     ticks = max(UNITS + 2 + LAG * last + 1, 3 * (WHOLE + last - 1) + 2 + LAG * 2 * last + 1)
     repeat(ticks - UNITS, drain)
@@ -469,9 +522,10 @@
             jax.ShapeDtypeStruct((2, NS, 3, D // 4, FS), BF16),
             jax.ShapeDtypeStruct((4, 8, FS), F32),
             jax.ShapeDtypeStruct((T, D), BF16),
+            jax.ShapeDtypeStruct((KEPT, T, 2 * FS), BF16),
         ),
         in_specs=[anywhere] * 5,
-        out_specs=(anywhere,) * 6,
+        out_specs=(anywhere,) * 7,
         scratch_shapes=[
             pltpu.VMEM((T, D), BF16),
             pltpu.VMEM((D, T), BF16),
@@ -481,13 +535,14 @@
             pltpu.VMEM((2, D, 2 * FS), BF16),
             pltpu.VMEM((2, FS, D), BF16),
             pltpu.VMEM((T, FS), BF16),
-            pltpu.VMEM((T, 2 * FS), BF16),
+            pltpu.VMEM((2, T, 2 * FS), BF16),
             pltpu.VMEM((2, 3, D, FS), BF16),
             pltpu.VMEM((2, 3, D // 4, FS), BF16),
             pltpu.VMEM((2, SLOTS, D // 4, FS), BF16),
             pltpu.VMEM((8, FS), F32),
             dma((2, 3)),
             dma((3,)),
+            dma((2,)),
             dma((2, 3)),
             dma((2, 3)),
             dma((NS, 3)),
@@ -507,7 +562,7 @@
     )(x, dy, w_gate, w_up, w_down)
 
 
-SUBS, DEEP = 4, 6
+SUBS, DEEP = 2, 4
 
 
 def adamw_kernel(count, work, n_in, aliased, *refs):
@@ -529,9 +584,8 @@
     dp = lax.axis_index("dp")
     z, c = dp // 2, dp % 2
     total = SUBS * len(work)
-    alone = 4 * work[0][0] + work[0][1]
-    rest = 4 * work[-1][0] + 4 - len(work)
-    run = all(4 * i + b == alone + at for at, (i, b, _) in enumerate(work))
+    numbers = [4 * i + b for i, b, _ in work]
+    cut = next((k for k in range(1, len(work)) if numbers[k] != numbers[k - 1] + 1), len(work))
 
     def here(k, source):
         return pltpu.make_async_copy(source, gv.at[k], g_sem.at[k])
@@ -555,7 +609,7 @@
 
     def blocks(n):
         k, sub = n // SUBS, n % SUBS
-        at = alone + k if run else jnp.where(k == 0, alone, rest + k)
+        at = numbers[0] + k if cut == len(work) else jnp.where(k < cut, numbers[0] + k, numbers[cut] - cut + k)
         i, b = at // 4, at % 4
         layer, hidden, q = 1 - i // PARTS, i % PARTS, b % 2 * 2 + b // 2
         across = (layer, pl.ds(pl.multiple_of(q * quarter + sub * few, few), few), pl.ds(pl.multiple_of(hidden * FS, FS), FS))
@@ -688,8 +742,9 @@
     place = jnp.where(c == 0, z, last - z)
     stages = NS - WHOLE
     ready = [(i, b, (None,) * CHIPS) for i in range(WHOLE) for b in range(4)]
-    first = min(5, 2 * WHOLE)
-    extra = 4 * WHOLE - 2 * first
+    first = min(6, 2 * WHOLE)
+    spare = 4 * WHOLE - 2 * first
+    more = [spare // (stages - 2) + (s < spare % (stages - 2)) for s in range(stages - 2)] + [0] * 2
     back, index, results = [], {}, None
 
     def units(u):
@@ -714,7 +769,7 @@
         if pending is not None:
             back.append(lax.ppermute(*pending))
             pending = None
-        many = first if s < 2 else 1 if s - 2 < extra else 0
+        many = first if s < 2 else more[s - 2]
         listed, ready = ready[:many], ready[many:]
         if s >= 2:
             listed = listed + units(s - 2)
@@ -729,7 +784,7 @@
 
 def solution(mesh):
     def step(x, dy, *arrays):
-        g, *_, ssq, _ = gradients(x, dy, *arrays[:3])
+        g, *_, ssq, _, _ = gradients(x, dy, *arrays[:3])
         return tuple(finish(g, ssq, arrays))
 
     return jax.shard_map(

time: 1030 us -> 985 us (0.956)
  waiting for transfers between devices: 266 us -> 191 us
  Pallas kernels: 711 us -> 753 us
  starting transfers between devices: 52.4 us -> 37.4 us
    ppermute x14 -> x10, waiting for transfers between devices: 266 us -> 191 us  [finish(): newest = lax.ppermute(sent, 'dp', moves)]
    pallas_call x1, Pallas kernels: 486 us -> 538 us  [gradients(): pl.pallas_call(functools.partial(gradients_kernel, (T, D, FS, RT, RD)), o...]
    pallas_call x16 -> x12, Pallas kernels: 224 us -> 214 us  [adamw(): pl.pallas_call(functools.partial(adamw_kernel, float(g.size), listed, len...]
    ppermute x14 -> x10, starting transfers between devices: 34.4 us -> 24.5 us  [finish(): back.append(lax.ppermute(*pending))]
  transfers between devices with their start and end apart: 28 -> 20, of which waited for: 14 -> 10; matrix products, arithmetic and copies ran while one was open for 0% -> 0% of each run, Pallas kernels for 20% -> 20%
where the time goes in v4:
time: 985 us; the launch traced here: 984 us
  Pallas kernels  753 us (76%)
  waiting for transfers between devices  191 us (19%)
  starting transfers between devices  37.4 us (4%)
    pallas_call x1, Pallas kernels, gradients(): pl.pallas_call(functools.partial(gradients_kernel, (T, D, FS, RT, RD)), o...  538 us
    pallas_call x12, Pallas kernels, adamw(): pl.pallas_call(functools.partial(adamw_kernel, float(g.size), listed, len...  214 us
    ppermute x10, waiting for transfers between devices, finish(): newest = lax.ppermute(sent, 'dp', moves)  191 us
    ppermute x10, starting transfers between devices, finish(): back.append(lax.ppermute(*pending))  24.5 us
  transfers between devices with their start and end apart: 20, of which 10 were waited for; matrix products, arithmetic and copies ran while one was open for 0% of the time, Pallas kernels for 20%

profile of v4, /device:TPU:0, one launch (start us, length us, event | category | flops | bytes accessed | tf_op | source)
XLA Modules:
  0.0 983.8 jit_solution(2688433826423898070)
XLA Ops:
  0.7 538.2 %gradients.1 = (bf16[16,3,4,256,512]{4,3,2,1,0:T(8,128)(2,1)}, bf16[16,3,512,512]{3,2,1,0:T(8,128)(2,1)}, bf16[16,3,512,512]{3,2,1,0:T(8,128)(2,1)}, bf16[2,16,3...) custom-call(bf16[1,2048,1024]{2,1,0:T(8,128)(2,1)} %x_ref.1, ...), custom_call_target="tpu_custom_call" | custom-call | tf_op jit(solution)/shard_map/gradients/pallas_call | solution.py:516
  538.9 1.5 constant_dynamic-slice_fusion
  540.4 1.3 collective-permute-start
  541.7 21.1 %collective-permute-done._ = bf16[1,3,2,256,512]{4,3,2,1,0:T(8,128)(2,1)} collective-permute-done((bf16[1,3,2,256,512]{4,3,2,1,0:T(8,128)(2,1)S(1)}, bf16[1,3,2,256,512]{4,3,2,1,0:T(8,128)(2,1)}, u32[]{:S(2)}, u32[]{:S(2)}) %collective-permute-start) | collective-permute-done | bytes 1572896 | tf_op jit(solution)/shard_map/ppermute | solution.py:768
  562.8 0.1 load.7.refs_2_
  562.9 1.3 collective-permute-start.1
  564.2 21.3 %collective-permute-done.1._ = bf16[1,3,2,256,512]{4,3,2,1,0:T(8,128)(2,1)} collective-permute-done((bf16[1,3,2,256,512]{4,3,2,1,0:T(8,128)(2,1)}, bf16[1,3,2,256,512]{4,3,2,1,0:T(8,128)(2,1)}, u32[]{:S(2)}, u32[]{:S(2)}) %collective-permute-start.1) | collective-permute-done | bytes 1572896 | tf_op jit(solution)/shard_map/ppermute | solution.py:768
  585.5 0.1 load.8.refs_4_.refs_2_
  585.6 1.3 collective-permute-start.2
  586.9 21.3 %collective-permute-done.2._ = bf16[1,3,2,256,512]{4,3,2,1,0:T(8,128)(2,1)} collective-permute-done((bf16[1,3,2,256,512]{4,3,2,1,0:T(8,128)(2,1)}, bf16[1,3,2,256,512]{4,3,2,1,0:T(8,128)(2,1)}, u32[]{:S(2)}, u32[]{:S(2)}) %collective-permute-start.2) | collective-permute-done | bytes 1572896 | tf_op jit(solution)/shard_map/ppermute | solution.py:768
  608.2 0.1 load.9.refs_6_.refs_4_.refs_2_
  608.3 1.3 collective-permute-start.3
  609.6 21.3 %collective-permute-done.3._ = bf16[1,3,2,256,512]{4,3,2,1,0:T(8,128)(2,1)} collective-permute-done((bf16[1,3,2,256,512]{4,3,2,1,0:T(8,128)(2,1)}, bf16[1,3,2,256,512]{4,3,2,1,0:T(8,128)(2,1)}, u32[]{:S(2)}, u32[]{:S(2)}) %collective-permute-start.3) | collective-permute-done | bytes 1572896 | tf_op jit(solution)/shard_map/ppermute | solution.py:768
  630.9 0.1 load.10.refs_6_.refs_4_.refs_2_
  630.9 1.3 collective-permute-start.4
  632.2 21.3 %collective-permute-done.4._ = bf16[1,3,2,256,512]{4,3,2,1,0:T(8,128)(2,1)} collective-permute-done((bf16[1,3,2,256,512]{4,3,2,1,0:T(8,128)(2,1)}, bf16[1,3,2,256,512]{4,3,2,1,0:T(8,128)(2,1)}, u32[]{:S(2)}, u32[]{:S(2)}) %collective-permute-start.4) | collective-permute-done | bytes 1572896 | tf_op jit(solution)/shard_map/ppermute | solution.py:768
  653.6 0.1 load.11.refs_6_.refs_4_.refs_2_
  653.6 1.3 collective-permute-start.5
  654.9 21.3 %collective-permute-done.5._ = bf16[1,3,2,256,512]{4,3,2,1,0:T(8,128)(2,1)} collective-permute-done((bf16[1,3,2,256,512]{4,3,2,1,0:T(8,128)(2,1)}, bf16[1,3,2,256,512]{4,3,2,1,0:T(8,128)(2,1)}, u32[]{:S(2)}, u32[]{:S(2)}) %collective-permute-start.5) | collective-permute-done | bytes 1572896 | tf_op jit(solution)/shard_map/ppermute | solution.py:768
  676.3 0.1 load.12.refs_6_.refs_4_.refs_2_
  676.3 1.3 collective-permute-start.6
  677.6 21.3 %collective-permute-done.6._ = bf16[1,3,2,256,512]{4,3,2,1,0:T(8,128)(2,1)} collective-permute-done((bf16[1,3,2,256,512]{4,3,2,1,0:T(8,128)(2,1)}, bf16[1,3,2,256,512]{4,3,2,1,0:T(8,128)(2,1)}, u32[]{:S(2)}, u32[]{:S(2)}) %collective-permute-start.6) | collective-permute-done | bytes 1572896 | tf_op jit(solution)/shard_map/ppermute | solution.py:768
  699.0 0.1 load.13.refs_6_.refs_4_.refs_2_
  699.0 1.3 collective-permute-start.7
  700.3 2.4 collective-permute-start.19
  702.8 18.9 %collective-permute-done.7.refs_6_.refs_4_.refs_2_ = bf16[1,3,2,256,512]{4,3,2,1,0:T(8,128)(2,1)} collective-permute-done((bf16[1,3,2,256,512]{4,3,2,1,0:T(8,128)(2,1)}, bf16[1,3,2,256,512]{4,3,2,1,0:T(8,128)(2,1)}, u32[]{:S(2)}, u32[]{:S(2)}) %collective-permute-start.7) | collective-permute-done | bytes 1572896 | tf_op jit(solution)/shard_map/ppermute | solution.py:768
  721.6 1.3 collective-permute-start.9
  722.9 2.5 collective-permute-start.18
  725.4 2.4 collective-permute-start.17
  727.9 2.4 collective-permute-start.16
  730.3 0.0 collective-permute-done.19.refs_3_
  730.3 2.5 collective-permute-start.15
  732.8 11.5 %collective-permute-done.9.refs_6_.refs_4_ = bf16[1,3,2,256,512]{4,3,2,1,0:T(8,128)(2,1)} collective-permute-done((bf16[1,3,2,256,512]{4,3,2,1,0:T(8,128)(2,1)}, bf16[1,3,2,256,512]{4,3,2,1,0:T(8,128)(2,1)}, u32[]{:S(2)}, u32[]{:S(2)}) %collective-permute-start.9) | collective-permute-done | bytes 1572896 | tf_op jit(solution)/shard_map/ppermute | solution.py:768
  744.3 1.3 collective-permute-start.11
  745.5 0.0 collective-permute-done.18.refs_5_.refs_3_
  745.6 2.4 collective-permute-start.14
  748.0 0.0 collective-permute-done.17.refs_7_.refs_5_.refs_3_
  748.0 2.4 collective-permute-start.13
  750.4 0.0 collective-permute-done.16.refs_7_.refs_5_.refs_3_
  750.4 2.4 collective-permute-start.8
  752.9 0.0 collective-permute-done.15.refs_7_.refs_5_.refs_3_
  752.9 2.4 collective-permute-start.10
  755.3 11.6 %collective-permute-done.11.refs_6_ = bf16[1,3,2,256,512]{4,3,2,1,0:T(8,128)(2,1)} collective-permute-done((bf16[1,3,2,256,512]{4,3,2,1,0:T(8,128)(2,1)}, bf16[1,3,2,256,512]{4,3,2,1,0:T(8,128)(2,1)}, u32[]{:S(2)}, u32[]{:S(2)}) %collective-permute-start.11) | collective-permute-done | bytes 1572896 | tf_op jit(solution)/shard_map/ppermute | solution.py:768
  766.9 2.4 collective-permute-start.12
  769.3 19.8 %adamw.12 = (bf16[2,1024,4096]{2,1,0:T(8,128)(2,1)}, bf16[2,1024,4096]{2,1,0:T(8,128)(2,1)}, bf16[2,4096,1024]{2,1,0:T(8,128)(2,1)}, f32[2,1024,4096]{2,1,0:T(8,...) custom-call(f32[4,8,512]{2,1,0:T(8,128)} %get-tuple-element.110.refs, ...), custom_call_target="tpu_custom_call" | custom-call | flops 37748736 | bytes 51904512 | tf_op jit(solution)/shard_map/adamw/pallas_call | solution.py:684
  789.1 19.8 %adamw.13 = (bf16[2,1024,4096]{2,1,0:T(8,128)(2,1)}, bf16[2,1024,4096]{2,1,0:T(8,128)(2,1)}, bf16[2,4096,1024]{2,1,0:T(8,128)(2,1)}, f32[2,1024,4096]{2,1,0:T(8,...) custom-call(f32[4,8,512]{2,1,0:T(8,128)} %get-tuple-element.110.refs, ...), custom_call_target="tpu_custom_call", output_to_operand_aliasing={{0}: (11, {}), {1}: (12, {}), {2}: (13, {}), {3}: (14, {}),... | custom-call | flops 37748736 | bytes 51904512 | tf_op jit(solution)/shard_map/adamw/pallas_call | solution.py:684
  808.9 19.7 %adamw.14 = (bf16[2,1024,4096]{2,1,0:T(8,128)(2,1)}, bf16[2,1024,4096]{2,1,0:T(8,128)(2,1)}, bf16[2,4096,1024]{2,1,0:T(8,128)(2,1)}, f32[2,1024,4096]{2,1,0:T(8,...) custom-call(f32[4,8,512]{2,1,0:T(8,128)} %get-tuple-element.110.refs, ...), custom_call_target="tpu_custom_call", output_to_operand_aliasing={{0}: (13, {}), {1}: (14, {}), {2}: (15, {}), {3}: (16, {}),... | custom-call | flops 37748736 | bytes 51904512 | tf_op jit(solution)/shard_map/adamw/pallas_call | solution.py:684
  828.7 19.7 %adamw.15 = (bf16[2,1024,4096]{2,1,0:T(8,128)(2,1)}, bf16[2,1024,4096]{2,1,0:T(8,128)(2,1)}, bf16[2,4096,1024]{2,1,0:T(8,128)(2,1)}, f32[2,1024,4096]{2,1,0:T(8,...) custom-call(f32[4,8,512]{2,1,0:T(8,128)} %get-tuple-element.110.refs, ...), custom_call_target="tpu_custom_call", output_to_operand_aliasing={{0}: (15, {}), {1}: (16, {}), {2}: (17, {}), {3}: (18, {}),... | custom-call | flops 37748736 | bytes 51904512 | tf_op jit(solution)/shard_map/adamw/pallas_call | solution.py:684
  848.4 19.8 %adamw.16 = (bf16[2,1024,4096]{2,1,0:T(8,128)(2,1)}, bf16[2,1024,4096]{2,1,0:T(8,128)(2,1)}, bf16[2,4096,1024]{2,1,0:T(8,128)(2,1)}, f32[2,1024,4096]{2,1,0:T(8,...) custom-call(f32[4,8,512]{2,1,0:T(8,128)} %get-tuple-element.110.refs, ...), custom_call_target="tpu_custom_call", output_to_operand_aliasing={{0}: (17, {}), {1}: (18, {}), {2}: (19, {}), {3}: (20, {}),... | custom-call | flops 37748736 | bytes 51904512 | tf_op jit(solution)/shard_map/adamw/pallas_call | solution.py:684
  868.2 19.9 %adamw.17 = (bf16[2,1024,4096]{2,1,0:T(8,128)(2,1)}, bf16[2,1024,4096]{2,1,0:T(8,128)(2,1)}, bf16[2,4096,1024]{2,1,0:T(8,128)(2,1)}, f32[2,1024,4096]{2,1,0:T(8,...) custom-call(f32[4,8,512]{2,1,0:T(8,128)} %get-tuple-element.110.refs, ...), custom_call_target="tpu_custom_call", output_to_operand_aliasing={{0}: (17, {}), {1}: (18, {}), {2}: (19, {}), {3}: (20, {}),... | custom-call | flops 37748736 | bytes 51904512 | tf_op jit(solution)/shard_map/adamw/pallas_call | solution.py:684
  888.1 16.5 %adamw.18 = (bf16[2,1024,4096]{2,1,0:T(8,128)(2,1)}, bf16[2,1024,4096]{2,1,0:T(8,128)(2,1)}, bf16[2,4096,1024]{2,1,0:T(8,128)(2,1)}, f32[2,1024,4096]{2,1,0:T(8,...) custom-call(f32[4,8,512]{2,1,0:T(8,128)} %get-tuple-element.110.refs, ...), custom_call_target="tpu_custom_call", output_to_operand_aliasing={{0}: (17, {}), {1}: (18, {}), {2}: (19, {}), {3}: (20, {}),... | custom-call | flops 31457280 | bytes 43253760 | tf_op jit(solution)/shard_map/adamw/pallas_call | solution.py:684
  904.7 0.0 collective-permute-done.14.refs_7_.refs_5_.refs_3_
  904.7 16.5 %adamw.19 = (bf16[2,1024,4096]{2,1,0:T(8,128)(2,1)}, bf16[2,1024,4096]{2,1,0:T(8,128)(2,1)}, bf16[2,4096,1024]{2,1,0:T(8,128)(2,1)}, f32[2,1024,4096]{2,1,0:T(8,...) custom-call(f32[4,8,512]{2,1,0:T(8,128)} %get-tuple-element.110.refs, ...), custom_call_target="tpu_custom_call", output_to_operand_aliasing={{0}: (17, {}), {1}: (18, {}), {2}: (19, {}), {3}: (20, {}),... | custom-call | flops 31457280 | bytes 43253760 | tf_op jit(solution)/shard_map/adamw/pallas_call | solution.py:684
  921.2 0.0 collective-permute-done.13.refs_7_.refs_5_.refs_3_
  921.2 16.5 %adamw.20 = (bf16[2,1024,4096]{2,1,0:T(8,128)(2,1)}, bf16[2,1024,4096]{2,1,0:T(8,128)(2,1)}, bf16[2,4096,1024]{2,1,0:T(8,128)(2,1)}, f32[2,1024,4096]{2,1,0:T(8,...) custom-call(f32[4,8,512]{2,1,0:T(8,128)} %get-tuple-element.110.refs, ...), custom_call_target="tpu_custom_call", output_to_operand_aliasing={{0}: (17, {}), {1}: (18, {}), {2}: (19, {}), {3}: (20, {}),... | custom-call | flops 31457280 | bytes 43253760 | tf_op jit(solution)/shard_map/adamw/pallas_call | solution.py:684
  937.8 0.0 collective-permute-done.8.refs_7_.refs_5_.refs_3_
  937.8 16.5 %adamw.21 = (bf16[2,1024,4096]{2,1,0:T(8,128)(2,1)}, bf16[2,1024,4096]{2,1,0:T(8,128)(2,1)}, bf16[2,4096,1024]{2,1,0:T(8,128)(2,1)}, f32[2,1024,4096]{2,1,0:T(8,...) custom-call(f32[4,8,512]{2,1,0:T(8,128)} %get-tuple-element.110.refs, ...), custom_call_target="tpu_custom_call", output_to_operand_aliasing={{0}: (17, {}), {1}: (18, {}), {2}: (19, {}), {3}: (20, {}),... | custom-call | flops 31457280 | bytes 43253760 | tf_op jit(solution)/shard_map/adamw/pallas_call | solution.py:684
  954.3 0.0 collective-permute-done.10.refs_7_.refs_5_
  954.3 14.6 %adamw.22 = (bf16[2,1024,4096]{2,1,0:T(8,128)(2,1)}, bf16[2,1024,4096]{2,1,0:T(8,128)(2,1)}, bf16[2,4096,1024]{2,1,0:T(8,128)(2,1)}, f32[2,1024,4096]{2,1,0:T(8,...) custom-call(f32[4,8,512]{2,1,0:T(8,128)} %get-tuple-element.110.refs, ...), custom_call_target="tpu_custom_call", output_to_operand_aliasing={{0}: (17, {}), {1}: (18, {}), {2}: (19, {}), {3}: (20, {}),... | custom-call | flops 25165824 | bytes 34603008 | tf_op jit(solution)/shard_map/adamw/pallas_call | solution.py:684
  969.0 0.0 collective-permute-done.12.refs_7_
  969.0 14.6 %adamw.23 = (bf16[2,1024,4096]{2,1,0:T(8,128)(2,1)}, bf16[2,1024,4096]{2,1,0:T(8,128)(2,1)}, bf16[2,4096,1024]{2,1,0:T(8,128)(2,1)}, f32[2,1024,4096]{2,1,0:T(8,...) custom-call(f32[4,8,512]{2,1,0:T(8,128)} %get-tuple-element.110.refs, ...), custom_call_target="tpu_custom_call", output_to_operand_aliasing={{0}: (17, {}), {1}: (18, {}), {2}: (19, {}), {3}: (20, {}),... | custom-call | flops 25165824 | bytes 34603008 | tf_op jit(solution)/shard_map/adamw/pallas_call | solution.py:684
Async XLA Ops:
  540.4 22.4 %collective-permute-start = (bf16[1,3,2,256,512]{4,3,2,1,0:T(8,128)(2,1)S(1)}, bf16[1,3,2,256,512]{4,3,2,1,0:T(8,128)(2,1)}, u32[]{:S(2)}, u32[]{:S(2)}) collective-permute-start(bf16[1,3,2,256,512]{4,3,2,1,0:T(8,128)(2,1)S(1)} %constant_dynamic-slice_fusion), channel_id=1, source_target_pairs={{2,0},{5,7},{4,2},{3,5},{6,4},{1,3},{10,8},{13,15},{12,10},{11,13}... | collective-permute-start | bytes 4718600 | tf_op jit(solution)/shard_map/ppermute | solution.py:768
  562.9 22.6 %collective-permute-start.1 = (bf16[1,3,2,256,512]{4,3,2,1,0:T(8,128)(2,1)}, bf16[1,3,2,256,512]{4,3,2,1,0:T(8,128)(2,1)}, u32[]{:S(2)}, u32[]{:S(2)}) collective-permute-start(bf16[1,3,2,256,512]{4,3,2,1,0:T(8,128)(2,1)} %load.7.refs_2_), channel_id=1, source_target_pairs={{2,0},{5,7},{4,2},{3,5},{6,4},{1,3},{10,8},{13,15},{12,10},{11,13}... | collective-permute-start | bytes 4718600 | tf_op jit(solution)/shard_map/ppermute | solution.py:768
  585.6 22.6 %collective-permute-start.2 = (bf16[1,3,2,256,512]{4,3,2,1,0:T(8,128)(2,1)}, bf16[1,3,2,256,512]{4,3,2,1,0:T(8,128)(2,1)}, u32[]{:S(2)}, u32[]{:S(2)}) collective-permute-start(bf16[1,3,2,256,512]{4,3,2,1,0:T(8,128)(2,1)} %load.8.refs_4_.refs_2_), channel_id=1, source_target_pairs={{2,0},{5,7},{4,2},{3,5},{6,4},{1,3},{10,8},{13,15},{12,10},{11,13}... | collective-permute-start | bytes 4718600 | tf_op jit(solution)/shard_map/ppermute | solution.py:768
  608.3 22.6 %collective-permute-start.3 = (bf16[1,3,2,256,512]{4,3,2,1,0:T(8,128)(2,1)}, bf16[1,3,2,256,512]{4,3,2,1,0:T(8,128)(2,1)}, u32[]{:S(2)}, u32[]{:S(2)}) collective-permute-start(bf16[1,3,2,256,512]{4,3,2,1,0:T(8,128)(2,1)} %load.9.refs_6_.refs_4_.refs_2_), channel_id=1, source_target_pairs={{2,0},{5,7},{4,2},{3,5},{6,4},{1,3},{10,8},{13,15},{12,10},{11,13}... | collective-permute-start | bytes 4718600 | tf_op jit(solution)/shard_map/ppermute | solution.py:768
  630.9 22.6 %collective-permute-start.4 = (bf16[1,3,2,256,512]{4,3,2,1,0:T(8,128)(2,1)}, bf16[1,3,2,256,512]{4,3,2,1,0:T(8,128)(2,1)}, u32[]{:S(2)}, u32[]{:S(2)}) collective-permute-start(bf16[1,3,2,256,512]{4,3,2,1,0:T(8,128)(2,1)} %load.10.refs_6_.refs_4_.refs_2_), channel_id=1, source_target_pairs={{2,0},{5,7},{4,2},{3,5},{6,4},{1,3},{10,8},{13,15},{12,10},{11,13}... | collective-permute-start | bytes 4718600 | tf_op jit(solution)/shard_map/ppermute | solution.py:768
  653.6 22.6 %collective-permute-start.5 = (bf16[1,3,2,256,512]{4,3,2,1,0:T(8,128)(2,1)}, bf16[1,3,2,256,512]{4,3,2,1,0:T(8,128)(2,1)}, u32[]{:S(2)}, u32[]{:S(2)}) collective-permute-start(bf16[1,3,2,256,512]{4,3,2,1,0:T(8,128)(2,1)} %load.11.refs_6_.refs_4_.refs_2_), channel_id=1, source_target_pairs={{2,0},{5,7},{4,2},{3,5},{6,4},{1,3},{10,8},{13,15},{12,10},{11,13}... | collective-permute-start | bytes 4718600 | tf_op jit(solution)/shard_map/ppermute | solution.py:768
  676.3 22.6 %collective-permute-start.6 = (bf16[1,3,2,256,512]{4,3,2,1,0:T(8,128)(2,1)}, bf16[1,3,2,256,512]{4,3,2,1,0:T(8,128)(2,1)}, u32[]{:S(2)}, u32[]{:S(2)}) collective-permute-start(bf16[1,3,2,256,512]{4,3,2,1,0:T(8,128)(2,1)} %load.12.refs_6_.refs_4_.refs_2_), channel_id=1, source_target_pairs={{2,0},{5,7},{4,2},{3,5},{6,4},{1,3},{10,8},{13,15},{12,10},{11,13}... | collective-permute-start | bytes 4718600 | tf_op jit(solution)/shard_map/ppermute | solution.py:768
  699.0 22.6 %collective-permute-start.7 = (bf16[1,3,2,256,512]{4,3,2,1,0:T(8,128)(2,1)}, bf16[1,3,2,256,512]{4,3,2,1,0:T(8,128)(2,1)}, u32[]{:S(2)}, u32[]{:S(2)}) collective-permute-start(bf16[1,3,2,256,512]{4,3,2,1,0:T(8,128)(2,1)} %load.13.refs_6_.refs_4_.refs_2_), channel_id=1, source_target_pairs={{2,0},{5,7},{4,2},{3,5},{6,4},{1,3},{10,8},{13,15},{12,10},{11,13}... | collective-permute-start | bytes 4718600 | tf_op jit(solution)/shard_map/ppermute | solution.py:768
  700.3 30.0 %collective-permute-start.19 = (bf16[1,3,2,256,512]{4,3,2,1,0:T(8,128)(2,1)}, bf16[1,3,2,256,512]{4,3,2,1,0:T(8,128)(2,1)}, u32[]{:S(2)}, u32[]{:S(2)}) collective-permute-start(bf16[1,3,2,256,512]{4,3,2,1,0:T(8,128)(2,1)} %load.7.refs_2_), channel_id=1, source_target_pairs={{0,1},{7,6},{2,3},{5,4},{4,5},{3,2},{8,9},{15,14},{10,11},{13,12},... | collective-permute-start | bytes 4718600 | tf_op jit(solution)/shard_map/ppermute | solution.py:770
  721.6 22.6 %collective-permute-start.9 = (bf16[1,3,2,256,512]{4,3,2,1,0:T(8,128)(2,1)}, bf16[1,3,2,256,512]{4,3,2,1,0:T(8,128)(2,1)}, u32[]{:S(2)}, u32[]{:S(2)}) collective-permute-start(bf16[1,3,2,256,512]{4,3,2,1,0:T(8,128)(2,1)} %collective-permute-done.7.refs_6_.refs_4_.refs_2_), channel_id=1, source_target_pairs={{2,0},{5,7},{4,2},{3,5},{10,8},{13,15},{12,10},{11,13},{18,16},{21... | collective-permute-start | bytes 4718600 | tf_op jit(solution)/shard_map/ppermute | solution.py:768
  722.9 22.6 %collective-permute-start.18 = (bf16[1,3,2,256,512]{4,3,2,1,0:T(8,128)(2,1)}, bf16[1,3,2,256,512]{4,3,2,1,0:T(8,128)(2,1)}, u32[]{:S(2)}, u32[]{:S(2)}) collective-permute-start(bf16[1,3,2,256,512]{4,3,2,1,0:T(8,128)(2,1)} %load.8.refs_4_.refs_2_), channel_id=1, source_target_pairs={{0,1},{7,6},{2,3},{5,4},{4,5},{3,2},{8,9},{15,14},{10,11},{13,12},... | collective-permute-start | bytes 4718600 | tf_op jit(solution)/shard_map/ppermute | solution.py:770
  725.4 22.6 %collective-permute-start.17 = (bf16[1,3,2,256,512]{4,3,2,1,0:T(8,128)(2,1)}, bf16[1,3,2,256,512]{4,3,2,1,0:T(8,128)(2,1)}, u32[]{:S(2)}, u32[]{:S(2)}) collective-permute-start(bf16[1,3,2,256,512]{4,3,2,1,0:T(8,128)(2,1)} %load.9.refs_6_.refs_4_.refs_2_), channel_id=1, source_target_pairs={{0,1},{7,6},{2,3},{5,4},{4,5},{3,2},{8,9},{15,14},{10,11},{13,12},... | collective-permute-start | bytes 4718600 | tf_op jit(solution)/shard_map/ppermute | solution.py:770
  727.9 22.6 %collective-permute-start.16 = (bf16[1,3,2,256,512]{4,3,2,1,0:T(8,128)(2,1)}, bf16[1,3,2,256,512]{4,3,2,1,0:T(8,128)(2,1)}, u32[]{:S(2)}, u32[]{:S(2)}) collective-permute-start(bf16[1,3,2,256,512]{4,3,2,1,0:T(8,128)(2,1)} %load.10.refs_6_.refs_4_.refs_2_), channel_id=1, source_target_pairs={{0,1},{7,6},{2,3},{5,4},{4,5},{3,2},{8,9},{15,14},{10,11},{13,12},... | collective-permute-start | bytes 4718600 | tf_op jit(solution)/shard_map/ppermute | solution.py:770
  730.3 22.5 %collective-permute-start.15 = (bf16[1,3,2,256,512]{4,3,2,1,0:T(8,128)(2,1)}, bf16[1,3,2,256,512]{4,3,2,1,0:T(8,128)(2,1)}, u32[]{:S(2)}, u32[]{:S(2)}) collective-permute-start(bf16[1,3,2,256,512]{4,3,2,1,0:T(8,128)(2,1)} %load.11.refs_6_.refs_4_.refs_2_), channel_id=1, source_target_pairs={{0,1},{7,6},{2,3},{5,4},{4,5},{3,2},{8,9},{15,14},{10,11},{13,12},... | collective-permute-start | bytes 4718600 | tf_op jit(solution)/shard_map/ppermute | solution.py:770
  744.3 22.6 %collective-permute-start.11 = (bf16[1,3,2,256,512]{4,3,2,1,0:T(8,128)(2,1)}, bf16[1,3,2,256,512]{4,3,2,1,0:T(8,128)(2,1)}, u32[]{:S(2)}, u32[]{:S(2)}) collective-permute-start(bf16[1,3,2,256,512]{4,3,2,1,0:T(8,128)(2,1)} %collective-permute-done.9.refs_6_.refs_4_), channel_id=1, source_target_pairs={{2,0},{5,7},{10,8},{13,15},{18,16},{21,23},{26,24},{29,31}} | collective-permute-start | bytes 4718600 | tf_op jit(solution)/shard_map/ppermute | solution.py:768
  745.6 159.1 %collective-permute-start.14 = (bf16[1,3,2,256,512]{4,3,2,1,0:T(8,128)(2,1)}, bf16[1,3,2,256,512]{4,3,2,1,0:T(8,128)(2,1)}, u32[]{:S(2)}, u32[]{:S(2)}) collective-permute-start(bf16[1,3,2,256,512]{4,3,2,1,0:T(8,128)(2,1)} %load.12.refs_6_.refs_4_.refs_2_), channel_id=1, source_target_pairs={{0,1},{7,6},{2,3},{5,4},{4,5},{3,2},{8,9},{15,14},{10,11},{13,12},... | collective-permute-start | bytes 4718600 | tf_op jit(solution)/shard_map/ppermute | solution.py:770
  748.0 173.2 %collective-permute-start.13 = (bf16[1,3,2,256,512]{4,3,2,1,0:T(8,128)(2,1)}, bf16[1,3,2,256,512]{4,3,2,1,0:T(8,128)(2,1)}, u32[]{:S(2)}, u32[]{:S(2)}) collective-permute-start(bf16[1,3,2,256,512]{4,3,2,1,0:T(8,128)(2,1)} %load.13.refs_6_.refs_4_.refs_2_), channel_id=1, source_target_pairs={{0,1},{7,6},{2,3},{5,4},{4,5},{3,2},{8,9},{15,14},{10,11},{13,12},... | collective-permute-start | bytes 4718600 | tf_op jit(solution)/shard_map/ppermute | solution.py:770
  750.4 187.3 %collective-permute-start.8 = (bf16[1,3,2,256,512]{4,3,2,1,0:T(8,128)(2,1)}, bf16[1,3,2,256,512]{4,3,2,1,0:T(8,128)(2,1)}, u32[]{:S(2)}, u32[]{:S(2)}) collective-permute-start(bf16[1,3,2,256,512]{4,3,2,1,0:T(8,128)(2,1)} %collective-permute-done.7.refs_6_.refs_4_.refs_2_), channel_id=1, source_target_pairs={{0,1},{7,6},{2,3},{5,4},{4,5},{3,2},{8,9},{15,14},{10,11},{13,12},... | collective-permute-start | bytes 4718600 | tf_op jit(solution)/shard_map/ppermute | solution.py:770
  752.9 201.5 %collective-permute-start.10 = (bf16[1,3,2,256,512]{4,3,2,1,0:T(8,128)(2,1)}, bf16[1,3,2,256,512]{4,3,2,1,0:T(8,128)(2,1)}, u32[]{:S(2)}, u32[]{:S(2)}) collective-permute-start(bf16[1,3,2,256,512]{4,3,2,1,0:T(8,128)(2,1)} %collective-permute-done.9.refs_6_.refs_4_), channel_id=1, source_target_pairs={{0,1},{7,6},{2,3},{5,4},{8,9},{15,14},{10,11},{13,12},{16,17},{23,... | collective-permute-start | bytes 4718600 | tf_op jit(solution)/shard_map/ppermute | solution.py:770
  766.9 202.1 %collective-permute-start.12 = (bf16[1,3,2,256,512]{4,3,2,1,0:T(8,128)(2,1)}, bf16[1,3,2,256,512]{4,3,2,1,0:T(8,128)(2,1)}, u32[]{:S(2)}, u32[]{:S(2)}) collective-permute-start(bf16[1,3,2,256,512]{4,3,2,1,0:T(8,128)(2,1)} %collective-permute-done.11.refs_6_), channel_id=1, source_target_pairs={{0,1},{7,6},{8,9},{15,14},{16,17},{23,22},{24,25},{31,30}} | collective-permute-start | bytes 4718600 | tf_op jit(solution)/shard_map/ppermute | solution.py:770

commit v5 on v4

--- a/solution.py
+++ b/solution.py
@@ -16,6 +16,7 @@
 WHOLE = 6
 LAG = 3
 SLOTS = 4
+FOLD = 128
 F32, BF16 = jnp.float32, jnp.bfloat16
 
 
@@ -34,11 +35,11 @@
 def gradients_kernel(
     sizes,
     x_ref, dy_ref, wg_ref, wu_ref, wd_ref,
-    g_ref, own_ref, pair_ref, chain_ref, ssq_ref, h_ref, dgu_ref,
-    a, at, up, upt, acc, wgu, wd, hid, dgu, gb, st, out, ssq,
+    g_ref, own_ref, pair_ref, chain_ref, ssq_ref, sent_ref, h_ref, dgu_ref,
+    a, at, up, upt, acc, wgu, wd, hid, dgu, gb, st, out, ssq, folded,
     w_sem, io_sem, dgu_sem, pair_send, own_sem, pair_recv, ld_sem, chain_send, chain_recv, keep_sem, pass_send, pass_recv, mate_send, mate_recv, ssq_send, ssq_recv,
 ):
-    T, D, FS, RT, RD = sizes
+    T, D, FS, RF, RT, RD = sizes
     UNITS = 3 * NS
     half, quarter = D // 2, D // 4
     dp = lax.axis_index("dp")
@@ -116,55 +117,51 @@
             hidden = (gate * jax.nn.sigmoid(gate) * lift).astype(BF16)
             acc[rows, :] = jnp.where(j > 0, acc[rows, :], 0.0) + dot(hidden, wd[slot])
 
-        over_rows(T, RT, tile)
+        over_rows(T, RF, tile)
 
     repeat(PARTS, forward)
 
     load_again.wait()
+    load_dy.wait()
 
     def close_forward(rows):
         h = dgu[0, rows, :].astype(F32) + acc[rows, :].astype(BF16).astype(F32)
         h = h.astype(BF16)
         dgu[0, rows, :] = h
         wide = h.astype(F32)
-        a[rows, :] = (wide * inverse_size(wide)).astype(BF16)
+        normed = (wide * inverse_size(wide)).astype(BF16)
+        a[rows, :] = normed
+        at[:, rows] = normed.T
+        upt[:, rows] = up[rows, :].T
 
     over_rows(T, RD, close_forward)
     save_h = pltpu.make_async_copy(dgu.at[0], h_ref, io_sem.at[0])
     save_h.start()
-
-    def turn(source, target):
-        def tile(rows):
-            target[:, rows] = source[rows, :].T
-
-        over_rows(T, RD, tile)
-
-    load_dy.wait()
-    turn(a, at)
-    turn(up, upt)
+    pl.semaphore_wait(barrier, 2 * CHIPS - 1)
     save_h.wait()
-    pl.semaphore_wait(barrier, 2 * CHIPS - 1)
 
     reload_x = pltpu.make_async_copy(x_ref.at[0], a, io_sem.at[1])
-
     load_h = pltpu.make_async_copy(h_ref, dgu.at[0], io_sem.at[0])
 
     def cross_layers():
         reload_x.wait()
-        over_rows(T, RD, norm_in_place)
-        turn(a, at)
         load_h.wait()
 
         def tile(rows):
+            wide = a[rows, :].astype(F32)
+            normed = (wide * inverse_size(wide)).astype(BF16)
+            a[rows, :] = normed
+            at[:, rows] = normed.T
             wide = dgu[0, rows, :].astype(F32)
             scale = inverse_size(wide)
             da = acc[rows, :].astype(BF16).astype(F32)
             along = jnp.sum(da * wide, -1, keepdims=True) * (1.0 / D)
             dh = (scale * da - wide * (scale * scale * scale * along)).astype(BF16)
-            up[rows, :] = (up[rows, :].astype(F32) + dh.astype(F32)).astype(BF16)
+            new = (up[rows, :].astype(F32) + dh.astype(F32)).astype(BF16)
+            up[rows, :] = new
+            upt[:, rows] = new.T
 
         over_rows(T, RD, tile)
-        turn(up, upt)
 
     def half_of(core):
         return pl.ds(pl.multiple_of(core * half, half), half)
@@ -452,37 +449,24 @@
     ticks = max(UNITS + 2 + LAG * last + 1, 3 * (WHOLE + last - 1) + 2 + LAG * 2 * last + 1)
     repeat(ticks - UNITS, drain)
 
-    for at_end in range(2):
-        for core in range(2):
-            slot = 2 * at_end + core
-            holder = 2 * last * at_end + core
-
-            def to(k, slot=slot):
-                return pltpu.make_async_remote_copy(
-                    src_ref=ssq, dst_ref=ssq_ref.at[slot], send_sem=ssq_send.at[k], recv_sem=ssq_recv.at[slot],
-                    device_id={"dp": (dp + k) % (2 * CHIPS)}, device_id_type=MESH,
-                )
-
-            local = pltpu.make_async_copy(ssq, ssq_ref.at[slot], io_sem.at[0])
-
-            @pl.when(dp == holder)
-            def _(to=to, local=local):
-                local.start()
-                for k in range(1, 2 * CHIPS):
-                    to(k).start()
-                local.wait()
-                for k in range(1, 2 * CHIPS):
-                    to(k).wait_send()
+    folded[...] = sum(ssq[:, k * FOLD : (k + 1) * FOLD] for k in range(FS // FOLD))
+
+    def squares(k, slot):
+        return pltpu.make_async_remote_copy(
+            src_ref=folded, dst_ref=ssq_ref.at[slot], send_sem=ssq_send.at[k], recv_sem=ssq_recv.at[slot],
+            device_id={"dp": (dp + k) % (2 * CHIPS)}, device_id_type=MESH,
+        )
+
+    def holder(slot):
+        return 2 * last * (slot // 2) + slot % 2
 
     for slot in range(4):
-        holder = 2 * last * (slot // 2) + slot % 2
-
-        @pl.when(dp != holder)
+
+        @pl.when(dp == holder(slot))
         def _(slot=slot):
-            pltpu.make_async_remote_copy(
-                src_ref=ssq, dst_ref=ssq_ref.at[slot], send_sem=ssq_send.at[0], recv_sem=ssq_recv.at[slot],
-                device_id={"dp": dp}, device_id_type=MESH,
-            ).wait_recv()
+            pltpu.make_async_copy(folded, ssq_ref.at[slot], io_sem.at[0]).start()
+            for k in range(1, 2 * CHIPS):
+                squares(k, slot).start()
 
     for p in range(3):
         pair_copy(3 * (NS - 2) + p).wait_send()
@@ -505,27 +489,55 @@
 
         repeat(UNITS, close)
 
+    first = WHOLE + jnp.where(c == 0, z, last - z) - 1
+    loads, stores = [], []
+    for p in range(3):
+        for core in range(2):
+            staged = wgu.at[p % 2, pl.ds(p // 2 * half + core * quarter, quarter), pl.ds(0, FS)]
+            loads.append(pltpu.make_async_copy(g_ref.at[first, p, 2 * c + core], staged, w_sem.at[core, p]))
+            stores.append(pltpu.make_async_copy(staged, sent_ref.at[0, p, core], w_sem.at[core, p]))
+    for load in loads:
+        load.start()
+    for load, store in zip(loads, stores, strict=True):
+        load.wait()
+        store.start()
+    for store in stores:
+        store.wait()
+
+    for slot in range(4):
+
+        @pl.when(dp == holder(slot))
+        def _(slot=slot):
+            pltpu.make_async_copy(folded, ssq_ref.at[slot], io_sem.at[0]).wait()
+            for k in range(1, 2 * CHIPS):
+                squares(k, slot).wait_send()
+
+        @pl.when(dp != holder(slot))
+        def _(slot=slot):
+            squares(0, slot).wait_recv()
+
 
 def gradients(x, dy, w_gate, w_up, w_down):
     _, T, D = x.shape
     F = w_gate.shape[2]
     FS = F // PARTS
-    RT, RD = min(512, T // 2), min(256, T)
+    RF, RT, RD = min(1024, T), min(512, T // 2), min(256, T)
     anywhere = pl.BlockSpec(memory_space=pl.ANY)
     dma = pltpu.SemaphoreType.DMA
     return pl.pallas_call(
-        functools.partial(gradients_kernel, (T, D, FS, RT, RD)),
+        functools.partial(gradients_kernel, (T, D, FS, RF, RT, RD)),
         out_shape=(
             jax.ShapeDtypeStruct((NS, 3, 4, D // 4, FS), BF16),
             jax.ShapeDtypeStruct((NS, 3, D // 2, FS), BF16),
             jax.ShapeDtypeStruct((NS, 3, D // 2, FS), BF16),
             jax.ShapeDtypeStruct((2, NS, 3, D // 4, FS), BF16),
-            jax.ShapeDtypeStruct((4, 8, FS), F32),
+            jax.ShapeDtypeStruct((4, 8, FOLD), F32),
+            jax.ShapeDtypeStruct((1, 3, 2, D // 4, FS), BF16),
             jax.ShapeDtypeStruct((T, D), BF16),
             jax.ShapeDtypeStruct((KEPT, T, 2 * FS), BF16),
         ),
         in_specs=[anywhere] * 5,
-        out_specs=(anywhere,) * 7,
+        out_specs=(anywhere,) * 8,
         scratch_shapes=[
             pltpu.VMEM((T, D), BF16),
             pltpu.VMEM((D, T), BF16),
@@ -540,6 +552,7 @@
             pltpu.VMEM((2, 3, D // 4, FS), BF16),
             pltpu.VMEM((2, SLOTS, D // 4, FS), BF16),
             pltpu.VMEM((8, FS), F32),
+            pltpu.VMEM((8, FOLD), F32),
             dma((2, 3)),
             dma((3,)),
             dma((2,)),
@@ -562,7 +575,7 @@
     )(x, dy, w_gate, w_up, w_down)
 
 
-SUBS, DEEP = 2, 4
+SUBS, DEEP = 4, 6
 
 
 def adamw_kernel(count, work, n_in, aliased, *refs):
@@ -578,7 +591,7 @@
     take(9 if aliased else 0)
     results = take(9)
     bufs, outs = take(9), take(9)
-    gv, g_sem, in_sem, out_sem = take(4)
+    gv, squares, g_sem, in_sem, out_sem, squares_sem = take(6)
     quarter, FS = gv.shape[2:]
     few, part = quarter // SUBS, FS // SUBS
     dp = lax.axis_index("dp")
@@ -619,8 +632,8 @@
     def copies(n, inward):
         slot, where = n % DEEP, blocks(n)
         if inward:
-            return [pltpu.make_async_copy(arrays[k].at[where[k % 3]], bufs[k].at[slot], in_sem.at[slot, k]) for k in range(9)]
-        return [pltpu.make_async_copy(outs[k].at[slot], results[k].at[where[k % 3]], out_sem.at[slot, k]) for k in range(9)]
+            return [pltpu.make_async_copy(arrays[k].at[where[k % 3]], bufs[k].at[slot], in_sem.at[slot]) for k in range(9)]
+        return [pltpu.make_async_copy(outs[k].at[slot], results[k].at[where[k % 3]], out_sem.at[slot]) for k in range(9)]
 
     def start(n, inward):
         for copy in copies(n, inward):
@@ -630,12 +643,15 @@
         for copy in copies(n, inward):
             copy.wait()
 
+    load_squares = pltpu.make_async_copy(ssq_ref, squares, squares_sem)
+    load_squares.start()
     fetch(0)
     for n in range(min(DEEP - 1, total)):
         start(n, True)
     for k in range(1, len(work)):
         fetch(k)
-    factor = jnp.minimum(1.0, 0.5 * lax.rsqrt(jnp.sum(ssq_ref[...]) / count + 1e-30))
+    load_squares.wait()
+    factor = jnp.minimum(1.0, 0.5 * lax.rsqrt(jnp.sum(squares[...]) / count + 1e-30))
 
     def piece(n, _):
         k, sub, slot = n // SUBS, n % SUBS, n % DEEP
@@ -683,7 +699,7 @@
     bufs = [pltpu.VMEM(shapes[k % 3], a.dtype) for k, a in enumerate(arrays)]
     return pl.pallas_call(
         functools.partial(adamw_kernel, float(g.size), listed, len(back), bool(results)),
-        in_specs=[pl.BlockSpec(memory_space=pltpu.VMEM)] + [anywhere] * (len(ins) - 1),
+        in_specs=[anywhere] * len(ins),
         out_specs=[anywhere] * 9,
         out_shape=[jax.ShapeDtypeStruct(a.shape, a.dtype) for a in arrays],
         input_output_aliases={len(ins) - 9 + k: k for k in range(9)} if results else {},
@@ -691,9 +707,11 @@
             *bufs,
             *bufs,
             pltpu.VMEM((len(listed), 3, quarter, FS), BF16),
+            pltpu.VMEM(ssq.shape, F32),
             pltpu.SemaphoreType.DMA((len(listed),)),
-            pltpu.SemaphoreType.DMA((DEEP, 9)),
-            pltpu.SemaphoreType.DMA((DEEP, 9)),
+            pltpu.SemaphoreType.DMA((DEEP,)),
+            pltpu.SemaphoreType.DMA((DEEP,)),
+            pltpu.SemaphoreType.DMA,
         ],
         compiler_params=pltpu.CompilerParams(vmem_limit_bytes=66_000_000),
         cost_estimate=pl.CostEstimate(flops=16 * size, bytes_accessed=22 * size, transcendentals=size),
@@ -734,12 +752,8 @@
     )(g, came)
 
 
-def finish(g, ssq, arrays):
-    _, _, _, quarter, FS = g.shape
+def finish(g, ssq, sent, arrays):
     last = CHIPS - 1
-    dp = lax.axis_index("dp")
-    z, c = dp // 2, dp % 2
-    place = jnp.where(c == 0, z, last - z)
     stages = NS - WHOLE
     ready = [(i, b, (None,) * CHIPS) for i in range(WHOLE) for b in range(4)]
     first = min(6, 2 * WHOLE)
@@ -760,7 +774,6 @@
     def device(place, core):
         return 2 * (place if core == 0 else last - place) + core
 
-    sent = lax.dynamic_slice(g, (WHOLE + place - 1, jnp.int32(0), 2 * c, jnp.int32(0), jnp.int32(0)), (1, 3, 2, quarter, FS))
     pending = None
     for s in range(stages + 2):
         if s < stages:
@@ -784,8 +797,8 @@
 
 def solution(mesh):
     def step(x, dy, *arrays):
-        g, *_, ssq, _, _ = gradients(x, dy, *arrays[:3])
-        return tuple(finish(g, ssq, arrays))
+        g, *_, ssq, sent, _, _ = gradients(x, dy, *arrays[:3])
+        return tuple(finish(g, ssq, sent, arrays))
 
     return jax.shard_map(
         step,

time: 985 us -> 972 us (0.987)
  Pallas kernels: 753 us -> 740 us
where the time goes in v5:
time: 972 us; the launch traced here: 970 us
  Pallas kernels  740 us (76%)
  waiting for transfers between devices  191 us (20%)
  starting transfers between devices  37.4 us (4%)
    pallas_call x1, Pallas kernels, gradients(): pl.pallas_call(functools.partial(gradients_kernel, (T, D, FS, RF, RT, RD)...  534 us
    pallas_call x12, Pallas kernels, adamw(): pl.pallas_call(functools.partial(adamw_kernel, float(g.size), listed, len...  206 us
    ppermute x10, waiting for transfers between devices, finish(): newest = lax.ppermute(sent, 'dp', moves)  191 us
    ppermute x10, starting transfers between devices, finish(): back.append(lax.ppermute(*pending))  24.5 us
  transfers between devices with their start and end apart: 20, of which 10 were waited for; matrix products, arithmetic and copies ran while one was open for 0% of the time, Pallas kernels for 20%

profile of v5, /device:TPU:0, one launch (start us, length us, event | category | flops | bytes accessed | tf_op | source)
XLA Modules:
  0.0 969.8 jit_solution(3431868293136024368)
XLA Ops:
  0.6 534.1 %gradients.1 = (bf16[16,3,4,256,512]{4,3,2,1,0:T(8,128)(2,1)}, bf16[16,3,512,512]{3,2,1,0:T(8,128)(2,1)}, bf16[16,3,512,512]{3,2,1,0:T(8,128)(2,1)}, bf16[2,16,3...) custom-call(bf16[1,2048,1024]{2,1,0:T(8,128)(2,1)} %x_ref.1, ...), custom_call_target="tpu_custom_call" | custom-call | tf_op jit(solution)/shard_map/gradients/pallas_call | solution.py:527
  534.8 1.3 collective-permute-start
  536.1 21.3 %collective-permute-done._ = bf16[1,3,2,256,512]{4,3,2,1,0:T(8,128)(2,1)} collective-permute-done((bf16[1,3,2,256,512]{4,3,2,1,0:T(8,128)(2,1)}, bf16[1,3,2,256,512]{4,3,2,1,0:T(8,128)(2,1)}, u32[]{:S(2)}, u32[]{:S(2)}) %collective-permute-start) | collective-permute-done | bytes 1572896 | tf_op jit(solution)/shard_map/ppermute | solution.py:781
  557.4 0.1 load.7.refs_2_
  557.5 1.3 collective-permute-start.1
  558.8 21.3 %collective-permute-done.1._ = bf16[1,3,2,256,512]{4,3,2,1,0:T(8,128)(2,1)} collective-permute-done((bf16[1,3,2,256,512]{4,3,2,1,0:T(8,128)(2,1)}, bf16[1,3,2,256,512]{4,3,2,1,0:T(8,128)(2,1)}, u32[]{:S(2)}, u32[]{:S(2)}) %collective-permute-start.1) | collective-permute-done | bytes 1572896 | tf_op jit(solution)/shard_map/ppermute | solution.py:781
  580.1 0.1 load.8.refs_4_.refs_2_
  580.2 1.3 collective-permute-start.2
  581.5 21.3 %collective-permute-done.2._ = bf16[1,3,2,256,512]{4,3,2,1,0:T(8,128)(2,1)} collective-permute-done((bf16[1,3,2,256,512]{4,3,2,1,0:T(8,128)(2,1)}, bf16[1,3,2,256,512]{4,3,2,1,0:T(8,128)(2,1)}, u32[]{:S(2)}, u32[]{:S(2)}) %collective-permute-start.2) | collective-permute-done | bytes 1572896 | tf_op jit(solution)/shard_map/ppermute | solution.py:781
  602.8 0.1 load.9.refs_6_.refs_4_.refs_2_
  602.8 1.3 collective-permute-start.3
  604.1 21.3 %collective-permute-done.3._ = bf16[1,3,2,256,512]{4,3,2,1,0:T(8,128)(2,1)} collective-permute-done((bf16[1,3,2,256,512]{4,3,2,1,0:T(8,128)(2,1)}, bf16[1,3,2,256,512]{4,3,2,1,0:T(8,128)(2,1)}, u32[]{:S(2)}, u32[]{:S(2)}) %collective-permute-start.3) | collective-permute-done | bytes 1572896 | tf_op jit(solution)/shard_map/ppermute | solution.py:781
  625.5 0.1 load.10.refs_6_.refs_4_.refs_2_
  625.5 1.3 collective-permute-start.4
  626.8 21.3 %collective-permute-done.4._ = bf16[1,3,2,256,512]{4,3,2,1,0:T(8,128)(2,1)} collective-permute-done((bf16[1,3,2,256,512]{4,3,2,1,0:T(8,128)(2,1)}, bf16[1,3,2,256,512]{4,3,2,1,0:T(8,128)(2,1)}, u32[]{:S(2)}, u32[]{:S(2)}) %collective-permute-start.4) | collective-permute-done | bytes 1572896 | tf_op jit(solution)/shard_map/ppermute | solution.py:781
  648.2 0.1 load.11.refs_6_.refs_4_.refs_2_
  648.2 1.3 collective-permute-start.5
  649.5 21.3 %collective-permute-done.5._ = bf16[1,3,2,256,512]{4,3,2,1,0:T(8,128)(2,1)} collective-permute-done((bf16[1,3,2,256,512]{4,3,2,1,0:T(8,128)(2,1)}, bf16[1,3,2,256,512]{4,3,2,1,0:T(8,128)(2,1)}, u32[]{:S(2)}, u32[]{:S(2)}) %collective-permute-start.5) | collective-permute-done | bytes 1572896 | tf_op jit(solution)/shard_map/ppermute | solution.py:781
  670.9 0.1 load.12.refs_6_.refs_4_.refs_2_
  670.9 1.3 collective-permute-start.6
  672.2 21.3 %collective-permute-done.6._ = bf16[1,3,2,256,512]{4,3,2,1,0:T(8,128)(2,1)} collective-permute-done((bf16[1,3,2,256,512]{4,3,2,1,0:T(8,128)(2,1)}, bf16[1,3,2,256,512]{4,3,2,1,0:T(8,128)(2,1)}, u32[]{:S(2)}, u32[]{:S(2)}) %collective-permute-start.6) | collective-permute-done | bytes 1572896 | tf_op jit(solution)/shard_map/ppermute | solution.py:781
  693.5 0.1 load.13.refs_6_.refs_4_.refs_2_
  693.6 1.3 collective-permute-start.7
  694.9 2.4 collective-permute-start.19
  697.3 18.9 %collective-permute-done.7.refs_6_.refs_4_.refs_2_ = bf16[1,3,2,256,512]{4,3,2,1,0:T(8,128)(2,1)} collective-permute-done((bf16[1,3,2,256,512]{4,3,2,1,0:T(8,128)(2,1)}, bf16[1,3,2,256,512]{4,3,2,1,0:T(8,128)(2,1)}, u32[]{:S(2)}, u32[]{:S(2)}) %collective-permute-start.7) | collective-permute-done | bytes 1572896 | tf_op jit(solution)/shard_map/ppermute | solution.py:781
  716.2 1.3 collective-permute-start.9
  717.5 2.5 collective-permute-start.18
  720.0 2.4 collective-permute-start.17
  722.5 2.4 collective-permute-start.16
  724.9 0.0 collective-permute-done.19.refs_3_
  724.9 2.5 collective-permute-start.15
  727.4 11.5 %collective-permute-done.9.refs_6_.refs_4_ = bf16[1,3,2,256,512]{4,3,2,1,0:T(8,128)(2,1)} collective-permute-done((bf16[1,3,2,256,512]{4,3,2,1,0:T(8,128)(2,1)}, bf16[1,3,2,256,512]{4,3,2,1,0:T(8,128)(2,1)}, u32[]{:S(2)}, u32[]{:S(2)}) %collective-permute-start.9) | collective-permute-done | bytes 1572896 | tf_op jit(solution)/shard_map/ppermute | solution.py:781
  738.8 1.3 collective-permute-start.11
  740.1 0.0 collective-permute-done.18.refs_5_.refs_3_
  740.1 2.4 collective-permute-start.14
  742.6 0.0 collective-permute-done.17.refs_7_.refs_5_.refs_3_
  742.6 2.4 collective-permute-start.13
  745.0 0.0 collective-permute-done.16.refs_7_.refs_5_.refs_3_
  745.0 2.4 collective-permute-start.8
  747.4 0.0 collective-permute-done.15.refs_7_.refs_5_.refs_3_
  747.5 2.4 collective-permute-start.10
  749.9 11.6 %collective-permute-done.11.refs_6_ = bf16[1,3,2,256,512]{4,3,2,1,0:T(8,128)(2,1)} collective-permute-done((bf16[1,3,2,256,512]{4,3,2,1,0:T(8,128)(2,1)}, bf16[1,3,2,256,512]{4,3,2,1,0:T(8,128)(2,1)}, u32[]{:S(2)}, u32[]{:S(2)}) %collective-permute-start.11) | collective-permute-done | bytes 1572896 | tf_op jit(solution)/shard_map/ppermute | solution.py:781
  761.5 2.4 collective-permute-start.12
  763.9 18.7 %adamw.12 = (bf16[2,1024,4096]{2,1,0:T(8,128)(2,1)}, bf16[2,1024,4096]{2,1,0:T(8,128)(2,1)}, bf16[2,4096,1024]{2,1,0:T(8,128)(2,1)}, f32[2,1024,4096]{2,1,0:T(8,...) custom-call(f32[4,8,128]{2,1,0:T(8,128)} %get-tuple-element.111.refs, ...), custom_call_target="tpu_custom_call" | custom-call | flops 37748736 | bytes 51904512 | tf_op jit(solution)/shard_map/adamw/pallas_call | solution.py:700
  782.6 18.5 %adamw.13 = (bf16[2,1024,4096]{2,1,0:T(8,128)(2,1)}, bf16[2,1024,4096]{2,1,0:T(8,128)(2,1)}, bf16[2,4096,1024]{2,1,0:T(8,128)(2,1)}, f32[2,1024,4096]{2,1,0:T(8,...) custom-call(f32[4,8,128]{2,1,0:T(8,128)} %get-tuple-element.111.refs, ...), custom_call_target="tpu_custom_call", output_to_operand_aliasing={{0}: (11, {}), {1}: (12, {}), {2}: (13, {}), {3}: (14, {}),... | custom-call | flops 37748736 | bytes 51904512 | tf_op jit(solution)/shard_map/adamw/pallas_call | solution.py:700
  801.1 18.7 %adamw.14 = (bf16[2,1024,4096]{2,1,0:T(8,128)(2,1)}, bf16[2,1024,4096]{2,1,0:T(8,128)(2,1)}, bf16[2,4096,1024]{2,1,0:T(8,128)(2,1)}, f32[2,1024,4096]{2,1,0:T(8,...) custom-call(f32[4,8,128]{2,1,0:T(8,128)} %get-tuple-element.111.refs, ...), custom_call_target="tpu_custom_call", output_to_operand_aliasing={{0}: (13, {}), {1}: (14, {}), {2}: (15, {}), {3}: (16, {}),... | custom-call | flops 37748736 | bytes 51904512 | tf_op jit(solution)/shard_map/adamw/pallas_call | solution.py:700
  819.8 18.7 %adamw.15 = (bf16[2,1024,4096]{2,1,0:T(8,128)(2,1)}, bf16[2,1024,4096]{2,1,0:T(8,128)(2,1)}, bf16[2,4096,1024]{2,1,0:T(8,128)(2,1)}, f32[2,1024,4096]{2,1,0:T(8,...) custom-call(f32[4,8,128]{2,1,0:T(8,128)} %get-tuple-element.111.refs, ...), custom_call_target="tpu_custom_call", output_to_operand_aliasing={{0}: (15, {}), {1}: (16, {}), {2}: (17, {}), {3}: (18, {}),... | custom-call | flops 37748736 | bytes 51904512 | tf_op jit(solution)/shard_map/adamw/pallas_call | solution.py:700
  838.6 19.0 %adamw.16 = (bf16[2,1024,4096]{2,1,0:T(8,128)(2,1)}, bf16[2,1024,4096]{2,1,0:T(8,128)(2,1)}, bf16[2,4096,1024]{2,1,0:T(8,128)(2,1)}, f32[2,1024,4096]{2,1,0:T(8,...) custom-call(f32[4,8,128]{2,1,0:T(8,128)} %get-tuple-element.111.refs, ...), custom_call_target="tpu_custom_call", output_to_operand_aliasing={{0}: (17, {}), {1}: (18, {}), {2}: (19, {}), {3}: (20, {}),... | custom-call | flops 37748736 | bytes 51904512 | tf_op jit(solution)/shard_map/adamw/pallas_call | solution.py:700
  857.6 18.8 %adamw.17 = (bf16[2,1024,4096]{2,1,0:T(8,128)(2,1)}, bf16[2,1024,4096]{2,1,0:T(8,128)(2,1)}, bf16[2,4096,1024]{2,1,0:T(8,128)(2,1)}, f32[2,1024,4096]{2,1,0:T(8,...) custom-call(f32[4,8,128]{2,1,0:T(8,128)} %get-tuple-element.111.refs, ...), custom_call_target="tpu_custom_call", output_to_operand_aliasing={{0}: (17, {}), {1}: (18, {}), {2}: (19, {}), {3}: (20, {}),... | custom-call | flops 37748736 | bytes 51904512 | tf_op jit(solution)/shard_map/adamw/pallas_call | solution.py:700
  876.4 16.9 %adamw.18 = (bf16[2,1024,4096]{2,1,0:T(8,128)(2,1)}, bf16[2,1024,4096]{2,1,0:T(8,128)(2,1)}, bf16[2,4096,1024]{2,1,0:T(8,128)(2,1)}, f32[2,1024,4096]{2,1,0:T(8,...) custom-call(f32[4,8,128]{2,1,0:T(8,128)} %get-tuple-element.111.refs, ...), custom_call_target="tpu_custom_call", output_to_operand_aliasing={{0}: (17, {}), {1}: (18, {}), {2}: (19, {}), {3}: (20, {}),... | custom-call | flops 31457280 | bytes 43253760 | tf_op jit(solution)/shard_map/adamw/pallas_call | solution.py:700
  893.3 0.0 collective-permute-done.14.refs_7_.refs_5_.refs_3_
  893.3 16.5 %adamw.19 = (bf16[2,1024,4096]{2,1,0:T(8,128)(2,1)}, bf16[2,1024,4096]{2,1,0:T(8,128)(2,1)}, bf16[2,4096,1024]{2,1,0:T(8,128)(2,1)}, f32[2,1024,4096]{2,1,0:T(8,...) custom-call(f32[4,8,128]{2,1,0:T(8,128)} %get-tuple-element.111.refs, ...), custom_call_target="tpu_custom_call", output_to_operand_aliasing={{0}: (17, {}), {1}: (18, {}), {2}: (19, {}), {3}: (20, {}),... | custom-call | flops 31457280 | bytes 43253760 | tf_op jit(solution)/shard_map/adamw/pallas_call | solution.py:700
  909.8 0.0 collective-permute-done.13.refs_7_.refs_5_.refs_3_
  909.8 16.3 %adamw.20 = (bf16[2,1024,4096]{2,1,0:T(8,128)(2,1)}, bf16[2,1024,4096]{2,1,0:T(8,128)(2,1)}, bf16[2,4096,1024]{2,1,0:T(8,128)(2,1)}, f32[2,1024,4096]{2,1,0:T(8,...) custom-call(f32[4,8,128]{2,1,0:T(8,128)} %get-tuple-element.111.refs, ...), custom_call_target="tpu_custom_call", output_to_operand_aliasing={{0}: (17, {}), {1}: (18, {}), {2}: (19, {}), {3}: (20, {}),... | custom-call | flops 31457280 | bytes 43253760 | tf_op jit(solution)/shard_map/adamw/pallas_call | solution.py:700
  926.0 0.0 collective-permute-done.8.refs_7_.refs_5_.refs_3_
  926.1 16.3 %adamw.21 = (bf16[2,1024,4096]{2,1,0:T(8,128)(2,1)}, bf16[2,1024,4096]{2,1,0:T(8,128)(2,1)}, bf16[2,4096,1024]{2,1,0:T(8,128)(2,1)}, f32[2,1024,4096]{2,1,0:T(8,...) custom-call(f32[4,8,128]{2,1,0:T(8,128)} %get-tuple-element.111.refs, ...), custom_call_target="tpu_custom_call", output_to_operand_aliasing={{0}: (17, {}), {1}: (18, {}), {2}: (19, {}), {3}: (20, {}),... | custom-call | flops 31457280 | bytes 43253760 | tf_op jit(solution)/shard_map/adamw/pallas_call | solution.py:700
  942.3 0.0 collective-permute-done.10.refs_7_.refs_5_
  942.3 13.7 %adamw.22 = (bf16[2,1024,4096]{2,1,0:T(8,128)(2,1)}, bf16[2,1024,4096]{2,1,0:T(8,128)(2,1)}, bf16[2,4096,1024]{2,1,0:T(8,128)(2,1)}, f32[2,1024,4096]{2,1,0:T(8,...) custom-call(f32[4,8,128]{2,1,0:T(8,128)} %get-tuple-element.111.refs, ...), custom_call_target="tpu_custom_call", output_to_operand_aliasing={{0}: (17, {}), {1}: (18, {}), {2}: (19, {}), {3}: (20, {}),... | custom-call | flops 25165824 | bytes 34603008 | tf_op jit(solution)/shard_map/adamw/pallas_call | solution.py:700
  956.0 0.0 collective-permute-done.12.refs_7_
  956.0 13.7 %adamw.23 = (bf16[2,1024,4096]{2,1,0:T(8,128)(2,1)}, bf16[2,1024,4096]{2,1,0:T(8,128)(2,1)}, bf16[2,4096,1024]{2,1,0:T(8,128)(2,1)}, f32[2,1024,4096]{2,1,0:T(8,...) custom-call(f32[4,8,128]{2,1,0:T(8,128)} %get-tuple-element.111.refs, ...), custom_call_target="tpu_custom_call", output_to_operand_aliasing={{0}: (17, {}), {1}: (18, {}), {2}: (19, {}), {3}: (20, {}),... | custom-call | flops 25165824 | bytes 34603008 | tf_op jit(solution)/shard_map/adamw/pallas_call | solution.py:700
Async XLA Ops:
  534.8 22.6 %collective-permute-start = (bf16[1,3,2,256,512]{4,3,2,1,0:T(8,128)(2,1)}, bf16[1,3,2,256,512]{4,3,2,1,0:T(8,128)(2,1)}, u32[]{:S(2)}, u32[]{:S(2)}) collective-permute-start(bf16[1,3,2,256,512]{4,3,2,1,0:T(8,128)(2,1)} %get-tuple-element.113), channel_id=1, source_target_pairs={{2,0},{5,7},{4,2},{3,5},{6,4},{1,3},{10,8},{13,15},{12,10},{11,13}... | collective-permute-start | bytes 4718600 | tf_op jit(solution)/shard_map/ppermute | solution.py:781
  557.5 22.6 %collective-permute-start.1 = (bf16[1,3,2,256,512]{4,3,2,1,0:T(8,128)(2,1)}, bf16[1,3,2,256,512]{4,3,2,1,0:T(8,128)(2,1)}, u32[]{:S(2)}, u32[]{:S(2)}) collective-permute-start(bf16[1,3,2,256,512]{4,3,2,1,0:T(8,128)(2,1)} %load.7.refs_2_), channel_id=1, source_target_pairs={{2,0},{5,7},{4,2},{3,5},{6,4},{1,3},{10,8},{13,15},{12,10},{11,13}... | collective-permute-start | bytes 4718600 | tf_op jit(solution)/shard_map/ppermute | solution.py:781
  580.2 22.6 %collective-permute-start.2 = (bf16[1,3,2,256,512]{4,3,2,1,0:T(8,128)(2,1)}, bf16[1,3,2,256,512]{4,3,2,1,0:T(8,128)(2,1)}, u32[]{:S(2)}, u32[]{:S(2)}) collective-permute-start(bf16[1,3,2,256,512]{4,3,2,1,0:T(8,128)(2,1)} %load.8.refs_4_.refs_2_), channel_id=1, source_target_pairs={{2,0},{5,7},{4,2},{3,5},{6,4},{1,3},{10,8},{13,15},{12,10},{11,13}... | collective-permute-start | bytes 4718600 | tf_op jit(solution)/shard_map/ppermute | solution.py:781
  602.8 22.6 %collective-permute-start.3 = (bf16[1,3,2,256,512]{4,3,2,1,0:T(8,128)(2,1)}, bf16[1,3,2,256,512]{4,3,2,1,0:T(8,128)(2,1)}, u32[]{:S(2)}, u32[]{:S(2)}) collective-permute-start(bf16[1,3,2,256,512]{4,3,2,1,0:T(8,128)(2,1)} %load.9.refs_6_.refs_4_.refs_2_), channel_id=1, source_target_pairs={{2,0},{5,7},{4,2},{3,5},{6,4},{1,3},{10,8},{13,15},{12,10},{11,13}... | collective-permute-start | bytes 4718600 | tf_op jit(solution)/shard_map/ppermute | solution.py:781
  625.5 22.6 %collective-permute-start.4 = (bf16[1,3,2,256,512]{4,3,2,1,0:T(8,128)(2,1)}, bf16[1,3,2,256,512]{4,3,2,1,0:T(8,128)(2,1)}, u32[]{:S(2)}, u32[]{:S(2)}) collective-permute-start(bf16[1,3,2,256,512]{4,3,2,1,0:T(8,128)(2,1)} %load.10.refs_6_.refs_4_.refs_2_), channel_id=1, source_target_pairs={{2,0},{5,7},{4,2},{3,5},{6,4},{1,3},{10,8},{13,15},{12,10},{11,13}... | collective-permute-start | bytes 4718600 | tf_op jit(solution)/shard_map/ppermute | solution.py:781
  648.2 22.6 %collective-permute-start.5 = (bf16[1,3,2,256,512]{4,3,2,1,0:T(8,128)(2,1)}, bf16[1,3,2,256,512]{4,3,2,1,0:T(8,128)(2,1)}, u32[]{:S(2)}, u32[]{:S(2)}) collective-permute-start(bf16[1,3,2,256,512]{4,3,2,1,0:T(8,128)(2,1)} %load.11.refs_6_.refs_4_.refs_2_), channel_id=1, source_target_pairs={{2,0},{5,7},{4,2},{3,5},{6,4},{1,3},{10,8},{13,15},{12,10},{11,13}... | collective-permute-start | bytes 4718600 | tf_op jit(solution)/shard_map/ppermute | solution.py:781
  670.9 22.6 %collective-permute-start.6 = (bf16[1,3,2,256,512]{4,3,2,1,0:T(8,128)(2,1)}, bf16[1,3,2,256,512]{4,3,2,1,0:T(8,128)(2,1)}, u32[]{:S(2)}, u32[]{:S(2)}) collective-permute-start(bf16[1,3,2,256,512]{4,3,2,1,0:T(8,128)(2,1)} %load.12.refs_6_.refs_4_.refs_2_), channel_id=1, source_target_pairs={{2,0},{5,7},{4,2},{3,5},{6,4},{1,3},{10,8},{13,15},{12,10},{11,13}... | collective-permute-start | bytes 4718600 | tf_op jit(solution)/shard_map/ppermute | solution.py:781
  693.6 22.6 %collective-permute-start.7 = (bf16[1,3,2,256,512]{4,3,2,1,0:T(8,128)(2,1)}, bf16[1,3,2,256,512]{4,3,2,1,0:T(8,128)(2,1)}, u32[]{:S(2)}, u32[]{:S(2)}) collective-permute-start(bf16[1,3,2,256,512]{4,3,2,1,0:T(8,128)(2,1)} %load.13.refs_6_.refs_4_.refs_2_), channel_id=1, source_target_pairs={{2,0},{5,7},{4,2},{3,5},{6,4},{1,3},{10,8},{13,15},{12,10},{11,13}... | collective-permute-start | bytes 4718600 | tf_op jit(solution)/shard_map/ppermute | solution.py:781
  694.9 30.0 %collective-permute-start.19 = (bf16[1,3,2,256,512]{4,3,2,1,0:T(8,128)(2,1)}, bf16[1,3,2,256,512]{4,3,2,1,0:T(8,128)(2,1)}, u32[]{:S(2)}, u32[]{:S(2)}) collective-permute-start(bf16[1,3,2,256,512]{4,3,2,1,0:T(8,128)(2,1)} %load.7.refs_2_), channel_id=1, source_target_pairs={{0,1},{7,6},{2,3},{5,4},{4,5},{3,2},{8,9},{15,14},{10,11},{13,12},... | collective-permute-start | bytes 4718600 | tf_op jit(solution)/shard_map/ppermute | solution.py:783
  716.2 22.6 %collective-permute-start.9 = (bf16[1,3,2,256,512]{4,3,2,1,0:T(8,128)(2,1)}, bf16[1,3,2,256,512]{4,3,2,1,0:T(8,128)(2,1)}, u32[]{:S(2)}, u32[]{:S(2)}) collective-permute-start(bf16[1,3,2,256,512]{4,3,2,1,0:T(8,128)(2,1)} %collective-permute-done.7.refs_6_.refs_4_.refs_2_), channel_id=1, source_target_pairs={{2,0},{5,7},{4,2},{3,5},{10,8},{13,15},{12,10},{11,13},{18,16},{21... | collective-permute-start | bytes 4718600 | tf_op jit(solution)/shard_map/ppermute | solution.py:781
  717.5 22.6 %collective-permute-start.18 = (bf16[1,3,2,256,512]{4,3,2,1,0:T(8,128)(2,1)}, bf16[1,3,2,256,512]{4,3,2,1,0:T(8,128)(2,1)}, u32[]{:S(2)}, u32[]{:S(2)}) collective-permute-start(bf16[1,3,2,256,512]{4,3,2,1,0:T(8,128)(2,1)} %load.8.refs_4_.refs_2_), channel_id=1, source_target_pairs={{0,1},{7,6},{2,3},{5,4},{4,5},{3,2},{8,9},{15,14},{10,11},{13,12},... | collective-permute-start | bytes 4718600 | tf_op jit(solution)/shard_map/ppermute | solution.py:783
  720.0 22.6 %collective-permute-start.17 = (bf16[1,3,2,256,512]{4,3,2,1,0:T(8,128)(2,1)}, bf16[1,3,2,256,512]{4,3,2,1,0:T(8,128)(2,1)}, u32[]{:S(2)}, u32[]{:S(2)}) collective-permute-start(bf16[1,3,2,256,512]{4,3,2,1,0:T(8,128)(2,1)} %load.9.refs_6_.refs_4_.refs_2_), channel_id=1, source_target_pairs={{0,1},{7,6},{2,3},{5,4},{4,5},{3,2},{8,9},{15,14},{10,11},{13,12},... | collective-permute-start | bytes 4718600 | tf_op jit(solution)/shard_map/ppermute | solution.py:783
  722.5 22.6 %collective-permute-start.16 = (bf16[1,3,2,256,512]{4,3,2,1,0:T(8,128)(2,1)}, bf16[1,3,2,256,512]{4,3,2,1,0:T(8,128)(2,1)}, u32[]{:S(2)}, u32[]{:S(2)}) collective-permute-start(bf16[1,3,2,256,512]{4,3,2,1,0:T(8,128)(2,1)} %load.10.refs_6_.refs_4_.refs_2_), channel_id=1, source_target_pairs={{0,1},{7,6},{2,3},{5,4},{4,5},{3,2},{8,9},{15,14},{10,11},{13,12},... | collective-permute-start | bytes 4718600 | tf_op jit(solution)/shard_map/ppermute | solution.py:783
  724.9 22.5 %collective-permute-start.15 = (bf16[1,3,2,256,512]{4,3,2,1,0:T(8,128)(2,1)}, bf16[1,3,2,256,512]{4,3,2,1,0:T(8,128)(2,1)}, u32[]{:S(2)}, u32[]{:S(2)}) collective-permute-start(bf16[1,3,2,256,512]{4,3,2,1,0:T(8,128)(2,1)} %load.11.refs_6_.refs_4_.refs_2_), channel_id=1, source_target_pairs={{0,1},{7,6},{2,3},{5,4},{4,5},{3,2},{8,9},{15,14},{10,11},{13,12},... | collective-permute-start | bytes 4718600 | tf_op jit(solution)/shard_map/ppermute | solution.py:783
  738.8 22.6 %collective-permute-start.11 = (bf16[1,3,2,256,512]{4,3,2,1,0:T(8,128)(2,1)}, bf16[1,3,2,256,512]{4,3,2,1,0:T(8,128)(2,1)}, u32[]{:S(2)}, u32[]{:S(2)}) collective-permute-start(bf16[1,3,2,256,512]{4,3,2,1,0:T(8,128)(2,1)} %collective-permute-done.9.refs_6_.refs_4_), channel_id=1, source_target_pairs={{2,0},{5,7},{10,8},{13,15},{18,16},{21,23},{26,24},{29,31}} | collective-permute-start | bytes 4718600 | tf_op jit(solution)/shard_map/ppermute | solution.py:781
  740.1 153.1 %collective-permute-start.14 = (bf16[1,3,2,256,512]{4,3,2,1,0:T(8,128)(2,1)}, bf16[1,3,2,256,512]{4,3,2,1,0:T(8,128)(2,1)}, u32[]{:S(2)}, u32[]{:S(2)}) collective-permute-start(bf16[1,3,2,256,512]{4,3,2,1,0:T(8,128)(2,1)} %load.12.refs_6_.refs_4_.refs_2_), channel_id=1, source_target_pairs={{0,1},{7,6},{2,3},{5,4},{4,5},{3,2},{8,9},{15,14},{10,11},{13,12},... | collective-permute-start | bytes 4718600 | tf_op jit(solution)/shard_map/ppermute | solution.py:783
  742.6 167.2 %collective-permute-start.13 = (bf16[1,3,2,256,512]{4,3,2,1,0:T(8,128)(2,1)}, bf16[1,3,2,256,512]{4,3,2,1,0:T(8,128)(2,1)}, u32[]{:S(2)}, u32[]{:S(2)}) collective-permute-start(bf16[1,3,2,256,512]{4,3,2,1,0:T(8,128)(2,1)} %load.13.refs_6_.refs_4_.refs_2_), channel_id=1, source_target_pairs={{0,1},{7,6},{2,3},{5,4},{4,5},{3,2},{8,9},{15,14},{10,11},{13,12},... | collective-permute-start | bytes 4718600 | tf_op jit(solution)/shard_map/ppermute | solution.py:783
  745.0 181.0 %collective-permute-start.8 = (bf16[1,3,2,256,512]{4,3,2,1,0:T(8,128)(2,1)}, bf16[1,3,2,256,512]{4,3,2,1,0:T(8,128)(2,1)}, u32[]{:S(2)}, u32[]{:S(2)}) collective-permute-start(bf16[1,3,2,256,512]{4,3,2,1,0:T(8,128)(2,1)} %collective-permute-done.7.refs_6_.refs_4_.refs_2_), channel_id=1, source_target_pairs={{0,1},{7,6},{2,3},{5,4},{4,5},{3,2},{8,9},{15,14},{10,11},{13,12},... | collective-permute-start | bytes 4718600 | tf_op jit(solution)/shard_map/ppermute | solution.py:783
  747.5 194.9 %collective-permute-start.10 = (bf16[1,3,2,256,512]{4,3,2,1,0:T(8,128)(2,1)}, bf16[1,3,2,256,512]{4,3,2,1,0:T(8,128)(2,1)}, u32[]{:S(2)}, u32[]{:S(2)}) collective-permute-start(bf16[1,3,2,256,512]{4,3,2,1,0:T(8,128)(2,1)} %collective-permute-done.9.refs_6_.refs_4_), channel_id=1, source_target_pairs={{0,1},{7,6},{2,3},{5,4},{8,9},{15,14},{10,11},{13,12},{16,17},{23,... | collective-permute-start | bytes 4718600 | tf_op jit(solution)/shard_map/ppermute | solution.py:783
  761.5 194.5 %collective-permute-start.12 = (bf16[1,3,2,256,512]{4,3,2,1,0:T(8,128)(2,1)}, bf16[1,3,2,256,512]{4,3,2,1,0:T(8,128)(2,1)}, u32[]{:S(2)}, u32[]{:S(2)}) collective-permute-start(bf16[1,3,2,256,512]{4,3,2,1,0:T(8,128)(2,1)} %collective-permute-done.11.refs_6_), channel_id=1, source_target_pairs={{0,1},{7,6},{8,9},{15,14},{16,17},{23,22},{24,25},{31,30}} | collective-permute-start | bytes 4718600 | tf_op jit(solution)/shard_map/ppermute | solution.py:783

commit v6 on v5

--- a/solution.py
+++ b/solution.py
@@ -13,7 +13,8 @@
 PARTS = 8
 NS = 2 * PARTS
 KEPT = PARTS - 2
-WHOLE = 6
+WHOLE = 5
+LATE = WHOLE + 1
 LAG = 3
 SLOTS = 4
 FOLD = 128
@@ -306,16 +307,33 @@
                 def _():
                     way.keep(n).wait()
 
-                @pl.when((way.place < last) & way.holds(n))
+                on_time = n // 3 != LATE
+
+                @pl.when((way.place < last) & way.holds(n) & on_time)
                 def _():
                     way.spread(n).wait_recv()
 
-                @pl.when(way.passes(n))
+                @pl.when(way.passes(n) & on_time)
                 def _():
                     way.spread(n).start()
 
-                @pl.when(way.holds(n))
-                def _():
+                @pl.when(way.holds(n) & ((way.place == last) | on_time))
+                def _():
+                    way.share(n).start()
+
+            m = k - (UNITS + PARTS + 2) - LAG * (last - way.place)
+
+            @pl.when((m >= 0) & (m < 3) & (way.place >= last - 1))
+            def _(way=way, m=m):
+                n = 3 * LATE + m
+
+                @pl.when(way.place == last)
+                def _():
+                    way.spread(n).start()
+
+                @pl.when(way.place < last)
+                def _():
+                    way.spread(n).wait_recv()
                     way.share(n).start()
 
     def dgu_copy(t):
@@ -521,7 +539,7 @@
     _, T, D = x.shape
     F = w_gate.shape[2]
     FS = F // PARTS
-    RF, RT, RD = min(1024, T), min(512, T // 2), min(256, T)
+    RF, RT, RD = min(1024, T), min(1024, T // 2), min(256, T)
     anywhere = pl.BlockSpec(memory_space=pl.ANY)
     dma = pltpu.SemaphoreType.DMA
     return pl.pallas_call(

time: 972 us -> 987 us (1.015)
  waiting for transfers between devices: 191 us -> 210 us
    ppermute x10 -> x11, waiting for transfers between devices: 191 us -> 210 us  [finish(): newest = lax.ppermute(sent, 'dp', moves)]
    pallas_call x1, Pallas kernels: 534 us -> 522 us  [gradients(): pl.pallas_call(functools.partial(gradients_kernel, (T, D, FS, RF, RT, RD)...]
    pallas_call x12 -> x13, Pallas kernels: 206 us -> 211 us  [adamw(): pl.pallas_call(functools.partial(adamw_kernel, float(g.size), listed, len...]
    ppermute x10 -> x11, starting transfers between devices: 24.5 us -> 27 us  [finish(): back.append(lax.ppermute(*pending))]
  transfers between devices with their start and end apart: 20 -> 22, of which waited for: 10 -> 11; matrix products, arithmetic and copies ran while one was open for 0% -> 0% of each run, Pallas kernels for 20% -> 20%
where the time goes in v6:
time: 987 us; the launch traced here: 985 us
  Pallas kernels  733 us (74%)
  waiting for transfers between devices  210 us (21%)
  starting transfers between devices  41.2 us (4%)
    pallas_call x1, Pallas kernels, gradients(): pl.pallas_call(functools.partial(gradients_kernel, (T, D, FS, RF, RT, RD)...  522 us
    pallas_call x13, Pallas kernels, adamw(): pl.pallas_call(functools.partial(adamw_kernel, float(g.size), listed, len...  211 us
    ppermute x11, waiting for transfers between devices, finish(): newest = lax.ppermute(sent, 'dp', moves)  210 us
    ppermute x11, starting transfers between devices, finish(): back.append(lax.ppermute(*pending))  27 us
  transfers between devices with their start and end apart: 22, of which 11 were waited for; matrix products, arithmetic and copies ran while one was open for 0% of the time, Pallas kernels for 20%

profile of v6, /device:TPU:0, one launch (start us, length us, event | category | flops | bytes accessed | tf_op | source)
XLA Modules:
  0.0 985.4 jit_solution(3811832221103419548)
XLA Ops:
  0.6 522.0 %gradients.1 = (bf16[16,3,4,256,512]{4,3,2,1,0:T(8,128)(2,1)}, bf16[16,3,512,512]{3,2,1,0:T(8,128)(2,1)}, bf16[16,3,512,512]{3,2,1,0:T(8,128)(2,1)}, bf16[2,16,3...) custom-call(bf16[1,2048,1024]{2,1,0:T(8,128)(2,1)} %x_ref.1, ...), custom_call_target="tpu_custom_call" | custom-call | tf_op jit(solution)/shard_map/gradients/pallas_call | solution.py:545
  522.6 1.3 collective-permute-start
  523.9 21.3 %collective-permute-done._ = bf16[1,3,2,256,512]{4,3,2,1,0:T(8,128)(2,1)} collective-permute-done((bf16[1,3,2,256,512]{4,3,2,1,0:T(8,128)(2,1)}, bf16[1,3,2,256,512]{4,3,2,1,0:T(8,128)(2,1)}, u32[]{:S(2)}, u32[]{:S(2)}) %collective-permute-start) | collective-permute-done | bytes 1572896 | tf_op jit(solution)/shard_map/ppermute | solution.py:799
  545.3 0.1 load.8.refs_2_
  545.3 1.3 collective-permute-start.1
  546.6 21.3 %collective-permute-done.1._ = bf16[1,3,2,256,512]{4,3,2,1,0:T(8,128)(2,1)} collective-permute-done((bf16[1,3,2,256,512]{4,3,2,1,0:T(8,128)(2,1)}, bf16[1,3,2,256,512]{4,3,2,1,0:T(8,128)(2,1)}, u32[]{:S(2)}, u32[]{:S(2)}) %collective-permute-start.1) | collective-permute-done | bytes 1572896 | tf_op jit(solution)/shard_map/ppermute | solution.py:799
  567.9 0.1 load.9.refs_4_.refs_2_
  568.0 1.3 collective-permute-start.2
  569.3 21.3 %collective-permute-done.2._ = bf16[1,3,2,256,512]{4,3,2,1,0:T(8,128)(2,1)} collective-permute-done((bf16[1,3,2,256,512]{4,3,2,1,0:T(8,128)(2,1)}, bf16[1,3,2,256,512]{4,3,2,1,0:T(8,128)(2,1)}, u32[]{:S(2)}, u32[]{:S(2)}) %collective-permute-start.2) | collective-permute-done | bytes 1572896 | tf_op jit(solution)/shard_map/ppermute | solution.py:799
  590.6 0.1 load.10.refs_6_.refs_4_.refs_2_
  590.7 1.3 collective-permute-start.3
  592.0 21.3 %collective-permute-done.3._ = bf16[1,3,2,256,512]{4,3,2,1,0:T(8,128)(2,1)} collective-permute-done((bf16[1,3,2,256,512]{4,3,2,1,0:T(8,128)(2,1)}, bf16[1,3,2,256,512]{4,3,2,1,0:T(8,128)(2,1)}, u32[]{:S(2)}, u32[]{:S(2)}) %collective-permute-start.3) | collective-permute-done | bytes 1572896 | tf_op jit(solution)/shard_map/ppermute | solution.py:799
  613.3 0.1 load.11.refs_6_.refs_4_.refs_2_
  613.4 1.3 collective-permute-start.4
  614.7 21.3 %collective-permute-done.4._ = bf16[1,3,2,256,512]{4,3,2,1,0:T(8,128)(2,1)} collective-permute-done((bf16[1,3,2,256,512]{4,3,2,1,0:T(8,128)(2,1)}, bf16[1,3,2,256,512]{4,3,2,1,0:T(8,128)(2,1)}, u32[]{:S(2)}, u32[]{:S(2)}) %collective-permute-start.4) | collective-permute-done | bytes 1572896 | tf_op jit(solution)/shard_map/ppermute | solution.py:799
  636.0 0.1 load.12.refs_6_.refs_4_.refs_2_
  636.1 1.3 collective-permute-start.5
  637.4 21.3 %collective-permute-done.5._ = bf16[1,3,2,256,512]{4,3,2,1,0:T(8,128)(2,1)} collective-permute-done((bf16[1,3,2,256,512]{4,3,2,1,0:T(8,128)(2,1)}, bf16[1,3,2,256,512]{4,3,2,1,0:T(8,128)(2,1)}, u32[]{:S(2)}, u32[]{:S(2)}) %collective-permute-start.5) | collective-permute-done | bytes 1572896 | tf_op jit(solution)/shard_map/ppermute | solution.py:799
  658.7 0.1 load.13.refs_6_.refs_4_.refs_2_
  658.8 1.3 collective-permute-start.6
  660.1 21.3 %collective-permute-done.6._ = bf16[1,3,2,256,512]{4,3,2,1,0:T(8,128)(2,1)} collective-permute-done((bf16[1,3,2,256,512]{4,3,2,1,0:T(8,128)(2,1)}, bf16[1,3,2,256,512]{4,3,2,1,0:T(8,128)(2,1)}, u32[]{:S(2)}, u32[]{:S(2)}) %collective-permute-start.6) | collective-permute-done | bytes 1572896 | tf_op jit(solution)/shard_map/ppermute | solution.py:799
  681.4 0.1 load.14.refs_6_.refs_4_.refs_2_
  681.5 1.3 collective-permute-start.7
  682.8 21.3 %collective-permute-done.7._ = bf16[1,3,2,256,512]{4,3,2,1,0:T(8,128)(2,1)} collective-permute-done((bf16[1,3,2,256,512]{4,3,2,1,0:T(8,128)(2,1)}, bf16[1,3,2,256,512]{4,3,2,1,0:T(8,128)(2,1)}, u32[]{:S(2)}, u32[]{:S(2)}) %collective-permute-start.7) | collective-permute-done | bytes 1572896 | tf_op jit(solution)/shard_map/ppermute | solution.py:799
  704.1 0.1 load.15.refs_6_.refs_4_.refs_2_
  704.1 1.3 collective-permute-start.8
  705.4 2.5 collective-permute-start.21
  707.9 2.5 collective-permute-start.20
  710.4 16.4 %collective-permute-done.8.refs_6_.refs_4_.refs_2_ = bf16[1,3,2,256,512]{4,3,2,1,0:T(8,128)(2,1)} collective-permute-done((bf16[1,3,2,256,512]{4,3,2,1,0:T(8,128)(2,1)}, bf16[1,3,2,256,512]{4,3,2,1,0:T(8,128)(2,1)}, u32[]{:S(2)}, u32[]{:S(2)}) %collective-permute-start.8) | collective-permute-done | bytes 1572896 | tf_op jit(solution)/shard_map/ppermute | solution.py:799
  726.8 1.3 collective-permute-start.10
  728.1 2.5 collective-permute-start.19
  730.6 2.4 collective-permute-start.18
  733.0 0.0 collective-permute-done.21.refs_3_
  733.0 2.4 collective-permute-start.17
  735.5 0.0 collective-permute-done.20.refs_5_.refs_3_
  735.5 2.5 collective-permute-start.16
  737.9 11.5 %collective-permute-done.10.refs_6_.refs_4_ = bf16[1,3,2,256,512]{4,3,2,1,0:T(8,128)(2,1)} collective-permute-done((bf16[1,3,2,256,512]{4,3,2,1,0:T(8,128)(2,1)}, bf16[1,3,2,256,512]{4,3,2,1,0:T(8,128)(2,1)}, u32[]{:S(2)}, u32[]{:S(2)}) %collective-permute-start.10) | collective-permute-done | bytes 1572896 | tf_op jit(solution)/shard_map/ppermute | solution.py:799
  749.4 1.3 collective-permute-start.12
  750.7 0.0 collective-permute-done.19.refs_7_.refs_5_.refs_3_
  750.7 2.4 collective-permute-start.15
  753.1 0.0 collective-permute-done.18.refs_7_.refs_5_.refs_3_
  753.1 2.4 collective-permute-start.14
  755.6 0.0 collective-permute-done.17.refs_7_.refs_5_.refs_3_
  755.6 2.4 collective-permute-start.9
  758.0 0.0 collective-permute-done.16.refs_7_.refs_5_.refs_3_
  758.0 2.4 collective-permute-start.11
  760.5 11.5 %collective-permute-done.12.refs_6_ = bf16[1,3,2,256,512]{4,3,2,1,0:T(8,128)(2,1)} collective-permute-done((bf16[1,3,2,256,512]{4,3,2,1,0:T(8,128)(2,1)}, bf16[1,3,2,256,512]{4,3,2,1,0:T(8,128)(2,1)}, u32[]{:S(2)}, u32[]{:S(2)}) %collective-permute-start.12) | collective-permute-done | bytes 1572896 | tf_op jit(solution)/shard_map/ppermute | solution.py:799
  772.0 2.4 collective-permute-start.13
  774.4 19.2 %adamw.13 = (bf16[2,1024,4096]{2,1,0:T(8,128)(2,1)}, bf16[2,1024,4096]{2,1,0:T(8,128)(2,1)}, bf16[2,4096,1024]{2,1,0:T(8,128)(2,1)}, f32[2,1024,4096]{2,1,0:T(8,...) custom-call(f32[4,8,128]{2,1,0:T(8,128)} %get-tuple-element.120.refs, ...), custom_call_target="tpu_custom_call" | custom-call | flops 37748736 | bytes 51904512 | tf_op jit(solution)/shard_map/adamw/pallas_call | solution.py:718
  793.7 18.5 %adamw.14 = (bf16[2,1024,4096]{2,1,0:T(8,128)(2,1)}, bf16[2,1024,4096]{2,1,0:T(8,128)(2,1)}, bf16[2,4096,1024]{2,1,0:T(8,128)(2,1)}, f32[2,1024,4096]{2,1,0:T(8,...) custom-call(f32[4,8,128]{2,1,0:T(8,128)} %get-tuple-element.120.refs, ...), custom_call_target="tpu_custom_call", output_to_operand_aliasing={{0}: (11, {}), {1}: (12, {}), {2}: (13, {}), {3}: (14, {}),... | custom-call | flops 37748736 | bytes 51904512 | tf_op jit(solution)/shard_map/adamw/pallas_call | solution.py:718
  812.2 16.7 %adamw.15 = (bf16[2,1024,4096]{2,1,0:T(8,128)(2,1)}, bf16[2,1024,4096]{2,1,0:T(8,128)(2,1)}, bf16[2,4096,1024]{2,1,0:T(8,128)(2,1)}, f32[2,1024,4096]{2,1,0:T(8,...) custom-call(f32[4,8,128]{2,1,0:T(8,128)} %get-tuple-element.120.refs, ...), custom_call_target="tpu_custom_call", output_to_operand_aliasing={{0}: (13, {}), {1}: (14, {}), {2}: (15, {}), {3}: (16, {}),... | custom-call | flops 31457280 | bytes 43253760 | tf_op jit(solution)/shard_map/adamw/pallas_call | solution.py:718
  829.0 16.5 %adamw.16 = (bf16[2,1024,4096]{2,1,0:T(8,128)(2,1)}, bf16[2,1024,4096]{2,1,0:T(8,128)(2,1)}, bf16[2,4096,1024]{2,1,0:T(8,128)(2,1)}, f32[2,1024,4096]{2,1,0:T(8,...) custom-call(f32[4,8,128]{2,1,0:T(8,128)} %get-tuple-element.120.refs, ...), custom_call_target="tpu_custom_call", output_to_operand_aliasing={{0}: (15, {}), {1}: (16, {}), {2}: (17, {}), {3}: (18, {}),... | custom-call | flops 31457280 | bytes 43253760 | tf_op jit(solution)/shard_map/adamw/pallas_call | solution.py:718
  845.4 16.3 %adamw.17 = (bf16[2,1024,4096]{2,1,0:T(8,128)(2,1)}, bf16[2,1024,4096]{2,1,0:T(8,128)(2,1)}, bf16[2,4096,1024]{2,1,0:T(8,128)(2,1)}, f32[2,1024,4096]{2,1,0:T(8,...) custom-call(f32[4,8,128]{2,1,0:T(8,128)} %get-tuple-element.120.refs, ...), custom_call_target="tpu_custom_call", output_to_operand_aliasing={{0}: (17, {}), {1}: (18, {}), {2}: (19, {}), {3}: (20, {}),... | custom-call | flops 31457280 | bytes 43253760 | tf_op jit(solution)/shard_map/adamw/pallas_call | solution.py:718
  861.7 16.5 %adamw.18 = (bf16[2,1024,4096]{2,1,0:T(8,128)(2,1)}, bf16[2,1024,4096]{2,1,0:T(8,128)(2,1)}, bf16[2,4096,1024]{2,1,0:T(8,128)(2,1)}, f32[2,1024,4096]{2,1,0:T(8,...) custom-call(f32[4,8,128]{2,1,0:T(8,128)} %get-tuple-element.120.refs, ...), custom_call_target="tpu_custom_call", output_to_operand_aliasing={{0}: (17, {}), {1}: (18, {}), {2}: (19, {}), {3}: (20, {}),... | custom-call | flops 31457280 | bytes 43253760 | tf_op jit(solution)/shard_map/adamw/pallas_call | solution.py:718
  878.2 16.5 %adamw.19 = (bf16[2,1024,4096]{2,1,0:T(8,128)(2,1)}, bf16[2,1024,4096]{2,1,0:T(8,128)(2,1)}, bf16[2,4096,1024]{2,1,0:T(8,128)(2,1)}, f32[2,1024,4096]{2,1,0:T(8,...) custom-call(f32[4,8,128]{2,1,0:T(8,128)} %get-tuple-element.120.refs, ...), custom_call_target="tpu_custom_call", output_to_operand_aliasing={{0}: (17, {}), {1}: (18, {}), {2}: (19, {}), {3}: (20, {}),... | custom-call | flops 31457280 | bytes 43253760 | tf_op jit(solution)/shard_map/adamw/pallas_call | solution.py:718
  894.7 16.7 %adamw.20 = (bf16[2,1024,4096]{2,1,0:T(8,128)(2,1)}, bf16[2,1024,4096]{2,1,0:T(8,128)(2,1)}, bf16[2,4096,1024]{2,1,0:T(8,128)(2,1)}, f32[2,1024,4096]{2,1,0:T(8,...) custom-call(f32[4,8,128]{2,1,0:T(8,128)} %get-tuple-element.120.refs, ...), custom_call_target="tpu_custom_call", output_to_operand_aliasing={{0}: (17, {}), {1}: (18, {}), {2}: (19, {}), {3}: (20, {}),... | custom-call | flops 31457280 | bytes 43253760 | tf_op jit(solution)/shard_map/adamw/pallas_call | solution.py:718
  911.5 16.3 %adamw.21 = (bf16[2,1024,4096]{2,1,0:T(8,128)(2,1)}, bf16[2,1024,4096]{2,1,0:T(8,128)(2,1)}, bf16[2,4096,1024]{2,1,0:T(8,128)(2,1)}, f32[2,1024,4096]{2,1,0:T(8,...) custom-call(f32[4,8,128]{2,1,0:T(8,128)} %get-tuple-element.120.refs, ...), custom_call_target="tpu_custom_call", output_to_operand_aliasing={{0}: (17, {}), {1}: (18, {}), {2}: (19, {}), {3}: (20, {}),... | custom-call | flops 31457280 | bytes 43253760 | tf_op jit(solution)/shard_map/adamw/pallas_call | solution.py:718
  927.7 0.0 collective-permute-done.14.refs_7_.refs_5_.refs_3_
  927.8 16.3 %adamw.22 = (bf16[2,1024,4096]{2,1,0:T(8,128)(2,1)}, bf16[2,1024,4096]{2,1,0:T(8,128)(2,1)}, bf16[2,4096,1024]{2,1,0:T(8,128)(2,1)}, f32[2,1024,4096]{2,1,0:T(8,...) custom-call(f32[4,8,128]{2,1,0:T(8,128)} %get-tuple-element.120.refs, ...), custom_call_target="tpu_custom_call", output_to_operand_aliasing={{0}: (17, {}), {1}: (18, {}), {2}: (19, {}), {3}: (20, {}),... | custom-call | flops 31457280 | bytes 43253760 | tf_op jit(solution)/shard_map/adamw/pallas_call | solution.py:718
  944.1 13.8 %adamw.23 = (bf16[2,1024,4096]{2,1,0:T(8,128)(2,1)}, bf16[2,1024,4096]{2,1,0:T(8,128)(2,1)}, bf16[2,4096,1024]{2,1,0:T(8,128)(2,1)}, f32[2,1024,4096]{2,1,0:T(8,...) custom-call(f32[4,8,128]{2,1,0:T(8,128)} %get-tuple-element.120.refs, ...), custom_call_target="tpu_custom_call", output_to_operand_aliasing={{0}: (17, {}), {1}: (18, {}), {2}: (19, {}), {3}: (20, {}),... | custom-call | flops 25165824 | bytes 34603008 | tf_op jit(solution)/shard_map/adamw/pallas_call | solution.py:718
  957.8 0.0 collective-permute-done.11.refs_7_.refs_5_
  957.9 13.7 %adamw.24 = (bf16[2,1024,4096]{2,1,0:T(8,128)(2,1)}, bf16[2,1024,4096]{2,1,0:T(8,128)(2,1)}, bf16[2,4096,1024]{2,1,0:T(8,128)(2,1)}, f32[2,1024,4096]{2,1,0:T(8,...) custom-call(f32[4,8,128]{2,1,0:T(8,128)} %get-tuple-element.120.refs, ...), custom_call_target="tpu_custom_call", output_to_operand_aliasing={{0}: (17, {}), {1}: (18, {}), {2}: (19, {}), {3}: (20, {}),... | custom-call | flops 25165824 | bytes 34603008 | tf_op jit(solution)/shard_map/adamw/pallas_call | solution.py:718
  971.5 0.0 collective-permute-done.13.refs_7_
  971.5 13.7 %adamw.25 = (bf16[2,1024,4096]{2,1,0:T(8,128)(2,1)}, bf16[2,1024,4096]{2,1,0:T(8,128)(2,1)}, bf16[2,4096,1024]{2,1,0:T(8,128)(2,1)}, f32[2,1024,4096]{2,1,0:T(8,...) custom-call(f32[4,8,128]{2,1,0:T(8,128)} %get-tuple-element.120.refs, ...), custom_call_target="tpu_custom_call", output_to_operand_aliasing={{0}: (17, {}), {1}: (18, {}), {2}: (19, {}), {3}: (20, {}),... | custom-call | flops 25165824 | bytes 34603008 | tf_op jit(solution)/shard_map/adamw/pallas_call | solution.py:718
  (2 shorter events, 0.0 us)
Async XLA Ops:
  522.6 22.6 %collective-permute-start = (bf16[1,3,2,256,512]{4,3,2,1,0:T(8,128)(2,1)}, bf16[1,3,2,256,512]{4,3,2,1,0:T(8,128)(2,1)}, u32[]{:S(2)}, u32[]{:S(2)}) collective-permute-start(bf16[1,3,2,256,512]{4,3,2,1,0:T(8,128)(2,1)} %get-tuple-element.122), channel_id=1, source_target_pairs={{2,0},{5,7},{4,2},{3,5},{6,4},{1,3},{10,8},{13,15},{12,10},{11,13}... | collective-permute-start | bytes 4718600 | tf_op jit(solution)/shard_map/ppermute | solution.py:799
  545.3 22.6 %collective-permute-start.1 = (bf16[1,3,2,256,512]{4,3,2,1,0:T(8,128)(2,1)}, bf16[1,3,2,256,512]{4,3,2,1,0:T(8,128)(2,1)}, u32[]{:S(2)}, u32[]{:S(2)}) collective-permute-start(bf16[1,3,2,256,512]{4,3,2,1,0:T(8,128)(2,1)} %load.8.refs_2_), channel_id=1, source_target_pairs={{2,0},{5,7},{4,2},{3,5},{6,4},{1,3},{10,8},{13,15},{12,10},{11,13}... | collective-permute-start | bytes 4718600 | tf_op jit(solution)/shard_map/ppermute | solution.py:799
  568.0 22.6 %collective-permute-start.2 = (bf16[1,3,2,256,512]{4,3,2,1,0:T(8,128)(2,1)}, bf16[1,3,2,256,512]{4,3,2,1,0:T(8,128)(2,1)}, u32[]{:S(2)}, u32[]{:S(2)}) collective-permute-start(bf16[1,3,2,256,512]{4,3,2,1,0:T(8,128)(2,1)} %load.9.refs_4_.refs_2_), channel_id=1, source_target_pairs={{2,0},{5,7},{4,2},{3,5},{6,4},{1,3},{10,8},{13,15},{12,10},{11,13}... | collective-permute-start | bytes 4718600 | tf_op jit(solution)/shard_map/ppermute | solution.py:799
  590.7 22.6 %collective-permute-start.3 = (bf16[1,3,2,256,512]{4,3,2,1,0:T(8,128)(2,1)}, bf16[1,3,2,256,512]{4,3,2,1,0:T(8,128)(2,1)}, u32[]{:S(2)}, u32[]{:S(2)}) collective-permute-start(bf16[1,3,2,256,512]{4,3,2,1,0:T(8,128)(2,1)} %load.10.refs_6_.refs_4_.refs_2_), channel_id=1, source_target_pairs={{2,0},{5,7},{4,2},{3,5},{6,4},{1,3},{10,8},{13,15},{12,10},{11,13}... | collective-permute-start | bytes 4718600 | tf_op jit(solution)/shard_map/ppermute | solution.py:799
  613.4 22.6 %collective-permute-start.4 = (bf16[1,3,2,256,512]{4,3,2,1,0:T(8,128)(2,1)}, bf16[1,3,2,256,512]{4,3,2,1,0:T(8,128)(2,1)}, u32[]{:S(2)}, u32[]{:S(2)}) collective-permute-start(bf16[1,3,2,256,512]{4,3,2,1,0:T(8,128)(2,1)} %load.11.refs_6_.refs_4_.refs_2_), channel_id=1, source_target_pairs={{2,0},{5,7},{4,2},{3,5},{6,4},{1,3},{10,8},{13,15},{12,10},{11,13}... | collective-permute-start | bytes 4718600 | tf_op jit(solution)/shard_map/ppermute | solution.py:799
  636.1 22.6 %collective-permute-start.5 = (bf16[1,3,2,256,512]{4,3,2,1,0:T(8,128)(2,1)}, bf16[1,3,2,256,512]{4,3,2,1,0:T(8,128)(2,1)}, u32[]{:S(2)}, u32[]{:S(2)}) collective-permute-start(bf16[1,3,2,256,512]{4,3,2,1,0:T(8,128)(2,1)} %load.12.refs_6_.refs_4_.refs_2_), channel_id=1, source_target_pairs={{2,0},{5,7},{4,2},{3,5},{6,4},{1,3},{10,8},{13,15},{12,10},{11,13}... | collective-permute-start | bytes 4718600 | tf_op jit(solution)/shard_map/ppermute | solution.py:799
  658.8 22.6 %collective-permute-start.6 = (bf16[1,3,2,256,512]{4,3,2,1,0:T(8,128)(2,1)}, bf16[1,3,2,256,512]{4,3,2,1,0:T(8,128)(2,1)}, u32[]{:S(2)}, u32[]{:S(2)}) collective-permute-start(bf16[1,3,2,256,512]{4,3,2,1,0:T(8,128)(2,1)} %load.13.refs_6_.refs_4_.refs_2_), channel_id=1, source_target_pairs={{2,0},{5,7},{4,2},{3,5},{6,4},{1,3},{10,8},{13,15},{12,10},{11,13}... | collective-permute-start | bytes 4718600 | tf_op jit(solution)/shard_map/ppermute | solution.py:799
  681.5 22.6 %collective-permute-start.7 = (bf16[1,3,2,256,512]{4,3,2,1,0:T(8,128)(2,1)}, bf16[1,3,2,256,512]{4,3,2,1,0:T(8,128)(2,1)}, u32[]{:S(2)}, u32[]{:S(2)}) collective-permute-start(bf16[1,3,2,256,512]{4,3,2,1,0:T(8,128)(2,1)} %load.14.refs_6_.refs_4_.refs_2_), channel_id=1, source_target_pairs={{2,0},{5,7},{4,2},{3,5},{6,4},{1,3},{10,8},{13,15},{12,10},{11,13}... | collective-permute-start | bytes 4718600 | tf_op jit(solution)/shard_map/ppermute | solution.py:799
  704.1 22.6 %collective-permute-start.8 = (bf16[1,3,2,256,512]{4,3,2,1,0:T(8,128)(2,1)}, bf16[1,3,2,256,512]{4,3,2,1,0:T(8,128)(2,1)}, u32[]{:S(2)}, u32[]{:S(2)}) collective-permute-start(bf16[1,3,2,256,512]{4,3,2,1,0:T(8,128)(2,1)} %load.15.refs_6_.refs_4_.refs_2_), channel_id=1, source_target_pairs={{2,0},{5,7},{4,2},{3,5},{6,4},{1,3},{10,8},{13,15},{12,10},{11,13}... | collective-permute-start | bytes 4718600 | tf_op jit(solution)/shard_map/ppermute | solution.py:799
  705.4 27.6 %collective-permute-start.21 = (bf16[1,3,2,256,512]{4,3,2,1,0:T(8,128)(2,1)}, bf16[1,3,2,256,512]{4,3,2,1,0:T(8,128)(2,1)}, u32[]{:S(2)}, u32[]{:S(2)}) collective-permute-start(bf16[1,3,2,256,512]{4,3,2,1,0:T(8,128)(2,1)} %load.8.refs_2_), channel_id=1, source_target_pairs={{0,1},{7,6},{2,3},{5,4},{4,5},{3,2},{8,9},{15,14},{10,11},{13,12},... | collective-permute-start | bytes 4718600 | tf_op jit(solution)/shard_map/ppermute | solution.py:801
  707.9 27.6 %collective-permute-start.20 = (bf16[1,3,2,256,512]{4,3,2,1,0:T(8,128)(2,1)}, bf16[1,3,2,256,512]{4,3,2,1,0:T(8,128)(2,1)}, u32[]{:S(2)}, u32[]{:S(2)}) collective-permute-start(bf16[1,3,2,256,512]{4,3,2,1,0:T(8,128)(2,1)} %load.9.refs_4_.refs_2_), channel_id=1, source_target_pairs={{0,1},{7,6},{2,3},{5,4},{4,5},{3,2},{8,9},{15,14},{10,11},{13,12},... | collective-permute-start | bytes 4718600 | tf_op jit(solution)/shard_map/ppermute | solution.py:801
  726.8 22.6 %collective-permute-start.10 = (bf16[1,3,2,256,512]{4,3,2,1,0:T(8,128)(2,1)}, bf16[1,3,2,256,512]{4,3,2,1,0:T(8,128)(2,1)}, u32[]{:S(2)}, u32[]{:S(2)}) collective-permute-start(bf16[1,3,2,256,512]{4,3,2,1,0:T(8,128)(2,1)} %collective-permute-done.8.refs_6_.refs_4_.refs_2_), channel_id=1, source_target_pairs={{2,0},{5,7},{4,2},{3,5},{10,8},{13,15},{12,10},{11,13},{18,16},{21... | collective-permute-start | bytes 4718600 | tf_op jit(solution)/shard_map/ppermute | solution.py:799
  728.1 22.6 %collective-permute-start.19 = (bf16[1,3,2,256,512]{4,3,2,1,0:T(8,128)(2,1)}, bf16[1,3,2,256,512]{4,3,2,1,0:T(8,128)(2,1)}, u32[]{:S(2)}, u32[]{:S(2)}) collective-permute-start(bf16[1,3,2,256,512]{4,3,2,1,0:T(8,128)(2,1)} %load.10.refs_6_.refs_4_.refs_2_), channel_id=1, source_target_pairs={{0,1},{7,6},{2,3},{5,4},{4,5},{3,2},{8,9},{15,14},{10,11},{13,12},... | collective-permute-start | bytes 4718600 | tf_op jit(solution)/shard_map/ppermute | solution.py:801
  730.6 22.6 %collective-permute-start.18 = (bf16[1,3,2,256,512]{4,3,2,1,0:T(8,128)(2,1)}, bf16[1,3,2,256,512]{4,3,2,1,0:T(8,128)(2,1)}, u32[]{:S(2)}, u32[]{:S(2)}) collective-permute-start(bf16[1,3,2,256,512]{4,3,2,1,0:T(8,128)(2,1)} %load.11.refs_6_.refs_4_.refs_2_), channel_id=1, source_target_pairs={{0,1},{7,6},{2,3},{5,4},{4,5},{3,2},{8,9},{15,14},{10,11},{13,12},... | collective-permute-start | bytes 4718600 | tf_op jit(solution)/shard_map/ppermute | solution.py:801
  733.0 22.6 %collective-permute-start.17 = (bf16[1,3,2,256,512]{4,3,2,1,0:T(8,128)(2,1)}, bf16[1,3,2,256,512]{4,3,2,1,0:T(8,128)(2,1)}, u32[]{:S(2)}, u32[]{:S(2)}) collective-permute-start(bf16[1,3,2,256,512]{4,3,2,1,0:T(8,128)(2,1)} %load.12.refs_6_.refs_4_.refs_2_), channel_id=1, source_target_pairs={{0,1},{7,6},{2,3},{5,4},{4,5},{3,2},{8,9},{15,14},{10,11},{13,12},... | collective-permute-start | bytes 4718600 | tf_op jit(solution)/shard_map/ppermute | solution.py:801
  735.5 22.6 %collective-permute-start.16 = (bf16[1,3,2,256,512]{4,3,2,1,0:T(8,128)(2,1)}, bf16[1,3,2,256,512]{4,3,2,1,0:T(8,128)(2,1)}, u32[]{:S(2)}, u32[]{:S(2)}) collective-permute-start(bf16[1,3,2,256,512]{4,3,2,1,0:T(8,128)(2,1)} %load.13.refs_6_.refs_4_.refs_2_), channel_id=1, source_target_pairs={{0,1},{7,6},{2,3},{5,4},{4,5},{3,2},{8,9},{15,14},{10,11},{13,12},... | collective-permute-start | bytes 4718600 | tf_op jit(solution)/shard_map/ppermute | solution.py:801
  749.4 22.6 %collective-permute-start.12 = (bf16[1,3,2,256,512]{4,3,2,1,0:T(8,128)(2,1)}, bf16[1,3,2,256,512]{4,3,2,1,0:T(8,128)(2,1)}, u32[]{:S(2)}, u32[]{:S(2)}) collective-permute-start(bf16[1,3,2,256,512]{4,3,2,1,0:T(8,128)(2,1)} %collective-permute-done.10.refs_6_.refs_4_), channel_id=1, source_target_pairs={{2,0},{5,7},{10,8},{13,15},{18,16},{21,23},{26,24},{29,31}} | collective-permute-start | bytes 4718600 | tf_op jit(solution)/shard_map/ppermute | solution.py:799
  750.7 160.8 %collective-permute-start.15 = (bf16[1,3,2,256,512]{4,3,2,1,0:T(8,128)(2,1)}, bf16[1,3,2,256,512]{4,3,2,1,0:T(8,128)(2,1)}, u32[]{:S(2)}, u32[]{:S(2)}) collective-permute-start(bf16[1,3,2,256,512]{4,3,2,1,0:T(8,128)(2,1)} %load.14.refs_6_.refs_4_.refs_2_), channel_id=1, source_target_pairs={{0,1},{7,6},{2,3},{5,4},{4,5},{3,2},{8,9},{15,14},{10,11},{13,12},... | collective-permute-start | bytes 4718600 | tf_op jit(solution)/shard_map/ppermute | solution.py:801
  753.1 174.6 %collective-permute-start.14 = (bf16[1,3,2,256,512]{4,3,2,1,0:T(8,128)(2,1)}, bf16[1,3,2,256,512]{4,3,2,1,0:T(8,128)(2,1)}, u32[]{:S(2)}, u32[]{:S(2)}) collective-permute-start(bf16[1,3,2,256,512]{4,3,2,1,0:T(8,128)(2,1)} %load.15.refs_6_.refs_4_.refs_2_), channel_id=1, source_target_pairs={{0,1},{7,6},{2,3},{5,4},{4,5},{3,2},{8,9},{15,14},{10,11},{13,12},... | collective-permute-start | bytes 4718600 | tf_op jit(solution)/shard_map/ppermute | solution.py:801
  755.6 188.5 %collective-permute-start.9 = (bf16[1,3,2,256,512]{4,3,2,1,0:T(8,128)(2,1)}, bf16[1,3,2,256,512]{4,3,2,1,0:T(8,128)(2,1)}, u32[]{:S(2)}, u32[]{:S(2)}) collective-permute-start(bf16[1,3,2,256,512]{4,3,2,1,0:T(8,128)(2,1)} %collective-permute-done.8.refs_6_.refs_4_.refs_2_), channel_id=1, source_target_pairs={{0,1},{7,6},{2,3},{5,4},{4,5},{3,2},{8,9},{15,14},{10,11},{13,12},... | collective-permute-start | bytes 4718600 | tf_op jit(solution)/shard_map/ppermute | solution.py:801
  758.0 199.8 %collective-permute-start.11 = (bf16[1,3,2,256,512]{4,3,2,1,0:T(8,128)(2,1)}, bf16[1,3,2,256,512]{4,3,2,1,0:T(8,128)(2,1)}, u32[]{:S(2)}, u32[]{:S(2)}) collective-permute-start(bf16[1,3,2,256,512]{4,3,2,1,0:T(8,128)(2,1)} %collective-permute-done.10.refs_6_.refs_4_), channel_id=1, source_target_pairs={{0,1},{7,6},{2,3},{5,4},{8,9},{15,14},{10,11},{13,12},{16,17},{23,... | collective-permute-start | bytes 4718600 | tf_op jit(solution)/shard_map/ppermute | solution.py:801
  772.0 199.5 %collective-permute-start.13 = (bf16[1,3,2,256,512]{4,3,2,1,0:T(8,128)(2,1)}, bf16[1,3,2,256,512]{4,3,2,1,0:T(8,128)(2,1)}, u32[]{:S(2)}, u32[]{:S(2)}) collective-permute-start(bf16[1,3,2,256,512]{4,3,2,1,0:T(8,128)(2,1)} %collective-permute-done.12.refs_6_), channel_id=1, source_target_pairs={{0,1},{7,6},{8,9},{15,14},{16,17},{23,22},{24,25},{31,30}} | collective-permute-start | bytes 4718600 | tf_op jit(solution)/shard_map/ppermute | solution.py:801

commit v7 on v5

--- a/solution.py
+++ b/solution.py
@@ -218,7 +218,7 @@
             )
 
         def reaches(self, n, place):
-            return last - place <= WHOLE + last - 1 - n // 3
+            return (n // 3 < WHOLE) | ((n // 3 == WHOLE) & (place >= last - 1))
 
         def holds(self, n):
             return (self.place == last) | self.reaches(n, self.place)
@@ -489,7 +489,7 @@
 
         repeat(UNITS, close)
 
-    first = WHOLE + jnp.where(c == 0, z, last - z) - 1
+    first = WHOLE + jnp.where(c == 0, z, last - z) - 2
     loads, stores = [], []
     for p in range(3):
         for core in range(2):
@@ -754,15 +754,16 @@
 
 def finish(g, ssq, sent, arrays):
     last = CHIPS - 1
-    stages = NS - WHOLE
+    units_left = NS - WHOLE
+    stages = units_left + 1
     ready = [(i, b, (None,) * CHIPS) for i in range(WHOLE) for b in range(4)]
     first = min(6, 2 * WHOLE)
-    spare = 4 * WHOLE - 2 * first
-    more = [spare // (stages - 2) + (s < spare % (stages - 2)) for s in range(stages - 2)] + [0] * 2
+    spare = 4 * WHOLE - 3 * first
+    more = [spare // (stages - 3) + (s < spare % (stages - 3)) for s in range(stages - 3)] + [0] * 2
     back, index, results = [], {}, None
 
     def units(u):
-        came = tuple(index[u - p] if p < last and u >= p else None for p in range(CHIPS))
+        came = tuple(index[u - p + 1] if p < last and u - p + 1 >= 0 else None for p in range(CHIPS))
         return [(WHOLE + u, b, came) for b in range(4)]
 
     def update(results, listed):
@@ -777,18 +778,18 @@
     pending = None
     for s in range(stages + 2):
         if s < stages:
-            moves = [(device(p, core), device(p - 1, core)) for p in range(1, CHIPS) if s + p - 1 < stages for core in range(2)]
+            moves = [(device(p, core), device(p - 1, core)) for p in range(1, CHIPS) if 0 <= s + p - 2 < units_left for core in range(2)]
             newest = lax.ppermute(sent, "dp", moves)
         if pending is not None:
             back.append(lax.ppermute(*pending))
             pending = None
-        many = first if s < 2 else more[s - 2]
+        many = first if s < 3 else more[s - 3]
         listed, ready = ready[:many], ready[many:]
-        if s >= 2:
-            listed = listed + units(s - 2)
+        if s >= 3:
+            listed = listed + units(s - 3)
         results = update(results, listed)
         if s < stages:
-            sent = load(g, WHOLE + s + last, newest) if s + last < stages else newest
+            sent = load(g, WHOLE + s + last - 1, newest) if s + last - 1 < units_left else newest
             index[s] = (len(back), len(back) + 1)
             back.append(sent)
             pending = (sent, "dp", [(to, to + 1 - 2 * (to % 2)) for _, to in moves])

time: 972 us -> 989 us (1.017)
  waiting for transfers between devices: 191 us -> 209 us
    ppermute x10 -> x11, waiting for transfers between devices: 191 us -> 209 us  [finish(): newest = lax.ppermute(sent, 'dp', moves)]
    pallas_call x12 -> x13, Pallas kernels: 206 us -> 210 us  [adamw(): pl.pallas_call(functools.partial(adamw_kernel, float(g.size), listed, len...]
    ppermute x10 -> x11, starting transfers between devices: 24.5 us -> 26.4 us  [finish(): back.append(lax.ppermute(*pending))]
  transfers between devices with their start and end apart: 20 -> 22, of which waited for: 10 -> 10; matrix products, arithmetic and copies ran while one was open for 0% -> 0% of each run, Pallas kernels for 20% -> 20%
where the time goes in v7:
time: 989 us; the launch traced here: 988 us
  Pallas kernels  737 us (75%)
  waiting for transfers between devices  209 us (21%)
  starting transfers between devices  41.1 us (4%)
    pallas_call x1, Pallas kernels, gradients(): pl.pallas_call(functools.partial(gradients_kernel, (T, D, FS, RF, RT, RD)...  526 us
    pallas_call x13, Pallas kernels, adamw(): pl.pallas_call(functools.partial(adamw_kernel, float(g.size), listed, len...  210 us
    ppermute x11, waiting for transfers between devices, finish(): newest = lax.ppermute(sent, 'dp', moves)  209 us
    ppermute x11, starting transfers between devices, finish(): back.append(lax.ppermute(*pending))  26.4 us
  transfers between devices with their start and end apart: 22, of which 10 were waited for; matrix products, arithmetic and copies ran while one was open for 0% of the time, Pallas kernels for 20%

profile of v7, /device:TPU:0, one launch (start us, length us, event | category | flops | bytes accessed | tf_op | source)
XLA Modules:
  0.0 987.6 jit_solution(4135706022798493275)
XLA Ops:
  0.6 525.9 %gradients.1 = (bf16[16,3,4,256,512]{4,3,2,1,0:T(8,128)(2,1)}, bf16[16,3,512,512]{3,2,1,0:T(8,128)(2,1)}, bf16[16,3,512,512]{3,2,1,0:T(8,128)(2,1)}, bf16[2,16,3...) custom-call(bf16[1,2048,1024]{2,1,0:T(8,128)(2,1)} %x_ref.1, ...), custom_call_target="tpu_custom_call" | custom-call | tf_op jit(solution)/shard_map/gradients/pallas_call | solution.py:527
  526.5 1.8 collective-permute-start
  528.4 0.0 collective-permute-done._
  528.4 0.1 load.8.refs_2_
  528.4 1.3 collective-permute-start.1
  529.7 40.8 %collective-permute-done.1._ = bf16[1,3,2,256,512]{4,3,2,1,0:T(8,128)(2,1)} collective-permute-done((bf16[1,3,2,256,512]{4,3,2,1,0:T(8,128)(2,1)}, bf16[1,3,2,256,512]{4,3,2,1,0:T(8,128)(2,1)}, u32[]{:S(2)}, u32[]{:S(2)}) %collective-permute-start.1) | collective-permute-done | bytes 1572896 | tf_op jit(solution)/shard_map/ppermute | solution.py:782
  570.5 0.1 load.9.refs_4_.refs_2_
  570.5 1.3 collective-permute-start.2
  571.9 21.3 %collective-permute-done.2._ = bf16[1,3,2,256,512]{4,3,2,1,0:T(8,128)(2,1)} collective-permute-done((bf16[1,3,2,256,512]{4,3,2,1,0:T(8,128)(2,1)}, bf16[1,3,2,256,512]{4,3,2,1,0:T(8,128)(2,1)}, u32[]{:S(2)}, u32[]{:S(2)}) %collective-permute-start.2) | collective-permute-done | bytes 1572896 | tf_op jit(solution)/shard_map/ppermute | solution.py:782
  593.2 0.1 load.10.refs_6_.refs_4_.refs_2_
  593.2 1.3 collective-permute-start.3
  594.5 21.3 %collective-permute-done.3._ = bf16[1,3,2,256,512]{4,3,2,1,0:T(8,128)(2,1)} collective-permute-done((bf16[1,3,2,256,512]{4,3,2,1,0:T(8,128)(2,1)}, bf16[1,3,2,256,512]{4,3,2,1,0:T(8,128)(2,1)}, u32[]{:S(2)}, u32[]{:S(2)}) %collective-permute-start.3) | collective-permute-done | bytes 1572896 | tf_op jit(solution)/shard_map/ppermute | solution.py:782
  615.9 0.1 load.11.refs_6_.refs_4_.refs_2_
  615.9 1.3 collective-permute-start.4
  617.2 21.3 %collective-permute-done.4._ = bf16[1,3,2,256,512]{4,3,2,1,0:T(8,128)(2,1)} collective-permute-done((bf16[1,3,2,256,512]{4,3,2,1,0:T(8,128)(2,1)}, bf16[1,3,2,256,512]{4,3,2,1,0:T(8,128)(2,1)}, u32[]{:S(2)}, u32[]{:S(2)}) %collective-permute-start.4) | collective-permute-done | bytes 1572896 | tf_op jit(solution)/shard_map/ppermute | solution.py:782
  638.6 0.1 load.12.refs_6_.refs_4_.refs_2_
  638.6 1.3 collective-permute-start.5
  639.9 21.3 %collective-permute-done.5._ = bf16[1,3,2,256,512]{4,3,2,1,0:T(8,128)(2,1)} collective-permute-done((bf16[1,3,2,256,512]{4,3,2,1,0:T(8,128)(2,1)}, bf16[1,3,2,256,512]{4,3,2,1,0:T(8,128)(2,1)}, u32[]{:S(2)}, u32[]{:S(2)}) %collective-permute-start.5) | collective-permute-done | bytes 1572896 | tf_op jit(solution)/shard_map/ppermute | solution.py:782
  661.2 0.1 load.13.refs_6_.refs_4_.refs_2_
  661.3 1.3 collective-permute-start.6
  662.6 21.3 %collective-permute-done.6._ = bf16[1,3,2,256,512]{4,3,2,1,0:T(8,128)(2,1)} collective-permute-done((bf16[1,3,2,256,512]{4,3,2,1,0:T(8,128)(2,1)}, bf16[1,3,2,256,512]{4,3,2,1,0:T(8,128)(2,1)}, u32[]{:S(2)}, u32[]{:S(2)}) %collective-permute-start.6) | collective-permute-done | bytes 1572896 | tf_op jit(solution)/shard_map/ppermute | solution.py:782
  683.9 0.1 load.14.refs_6_.refs_4_.refs_2_
  684.0 1.3 collective-permute-start.7
  685.3 21.3 %collective-permute-done.7._ = bf16[1,3,2,256,512]{4,3,2,1,0:T(8,128)(2,1)} collective-permute-done((bf16[1,3,2,256,512]{4,3,2,1,0:T(8,128)(2,1)}, bf16[1,3,2,256,512]{4,3,2,1,0:T(8,128)(2,1)}, u32[]{:S(2)}, u32[]{:S(2)}) %collective-permute-start.7) | collective-permute-done | bytes 1572896 | tf_op jit(solution)/shard_map/ppermute | solution.py:782
  706.6 0.1 load.15.refs_6_.refs_4_.refs_2_
  706.7 1.3 collective-permute-start.8
  708.0 1.8 collective-permute-start.21
  709.8 2.5 collective-permute-start.20
  712.3 17.0 %collective-permute-done.8.refs_6_.refs_4_.refs_2_ = bf16[1,3,2,256,512]{4,3,2,1,0:T(8,128)(2,1)} collective-permute-done((bf16[1,3,2,256,512]{4,3,2,1,0:T(8,128)(2,1)}, bf16[1,3,2,256,512]{4,3,2,1,0:T(8,128)(2,1)}, u32[]{:S(2)}, u32[]{:S(2)}) %collective-permute-start.8) | collective-permute-done | bytes 1572896 | tf_op jit(solution)/shard_map/ppermute | solution.py:782
  729.3 1.3 collective-permute-start.10
  730.6 2.5 collective-permute-start.19
  733.1 2.4 collective-permute-start.18
  735.6 0.0 collective-permute-done.21.refs_3_
  735.6 2.4 collective-permute-start.17
  738.0 0.0 collective-permute-done.20.refs_5_.refs_3_
  738.0 2.5 collective-permute-start.16
  740.5 11.5 %collective-permute-done.10.refs_6_.refs_4_ = bf16[1,3,2,256,512]{4,3,2,1,0:T(8,128)(2,1)} collective-permute-done((bf16[1,3,2,256,512]{4,3,2,1,0:T(8,128)(2,1)}, bf16[1,3,2,256,512]{4,3,2,1,0:T(8,128)(2,1)}, u32[]{:S(2)}, u32[]{:S(2)}) %collective-permute-start.10) | collective-permute-done | bytes 1572896 | tf_op jit(solution)/shard_map/ppermute | solution.py:782
  751.9 1.3 collective-permute-start.12
  753.2 0.0 collective-permute-done.19.refs_7_.refs_5_.refs_3_
  753.2 2.4 collective-permute-start.15
  755.7 0.0 collective-permute-done.18.refs_7_.refs_5_.refs_3_
  755.7 2.4 collective-permute-start.14
  758.1 0.0 collective-permute-done.17.refs_7_.refs_5_.refs_3_
  758.1 2.4 collective-permute-start.9
  760.6 0.0 collective-permute-done.16.refs_7_.refs_5_.refs_3_
  760.6 2.4 collective-permute-start.11
  763.0 11.5 %collective-permute-done.12.refs_6_ = bf16[1,3,2,256,512]{4,3,2,1,0:T(8,128)(2,1)} collective-permute-done((bf16[1,3,2,256,512]{4,3,2,1,0:T(8,128)(2,1)}, bf16[1,3,2,256,512]{4,3,2,1,0:T(8,128)(2,1)}, u32[]{:S(2)}, u32[]{:S(2)}) %collective-permute-start.12) | collective-permute-done | bytes 1572896 | tf_op jit(solution)/shard_map/ppermute | solution.py:782
  774.5 2.4 collective-permute-start.13
  777.0 19.2 %adamw.13 = (bf16[2,1024,4096]{2,1,0:T(8,128)(2,1)}, bf16[2,1024,4096]{2,1,0:T(8,128)(2,1)}, bf16[2,4096,1024]{2,1,0:T(8,128)(2,1)}, f32[2,1024,4096]{2,1,0:T(8,...) custom-call(f32[4,8,128]{2,1,0:T(8,128)} %get-tuple-element.120.refs, ...), custom_call_target="tpu_custom_call" | custom-call | flops 37748736 | bytes 51904512 | tf_op jit(solution)/shard_map/adamw/pallas_call | solution.py:700
  796.2 18.5 %adamw.14 = (bf16[2,1024,4096]{2,1,0:T(8,128)(2,1)}, bf16[2,1024,4096]{2,1,0:T(8,128)(2,1)}, bf16[2,4096,1024]{2,1,0:T(8,128)(2,1)}, f32[2,1024,4096]{2,1,0:T(8,...) custom-call(f32[4,8,128]{2,1,0:T(8,128)} %get-tuple-element.120.refs, ...), custom_call_target="tpu_custom_call", output_to_operand_aliasing={{0}: (11, {}), {1}: (12, {}), {2}: (13, {}), {3}: (14, {}),... | custom-call | flops 37748736 | bytes 51904512 | tf_op jit(solution)/shard_map/adamw/pallas_call | solution.py:700
  814.7 19.1 %adamw.15 = (bf16[2,1024,4096]{2,1,0:T(8,128)(2,1)}, bf16[2,1024,4096]{2,1,0:T(8,128)(2,1)}, bf16[2,4096,1024]{2,1,0:T(8,128)(2,1)}, f32[2,1024,4096]{2,1,0:T(8,...) custom-call(f32[4,8,128]{2,1,0:T(8,128)} %get-tuple-element.120.refs, ...), custom_call_target="tpu_custom_call", output_to_operand_aliasing={{0}: (11, {}), {1}: (12, {}), {2}: (13, {}), {3}: (14, {}),... | custom-call | flops 37748736 | bytes 51904512 | tf_op jit(solution)/shard_map/adamw/pallas_call | solution.py:700
  833.8 16.8 %adamw.16 = (bf16[2,1024,4096]{2,1,0:T(8,128)(2,1)}, bf16[2,1024,4096]{2,1,0:T(8,128)(2,1)}, bf16[2,4096,1024]{2,1,0:T(8,128)(2,1)}, f32[2,1024,4096]{2,1,0:T(8,...) custom-call(f32[4,8,128]{2,1,0:T(8,128)} %get-tuple-element.120.refs, ...), custom_call_target="tpu_custom_call", output_to_operand_aliasing={{0}: (15, {}), {1}: (16, {}), {2}: (17, {}), {3}: (18, {}),... | custom-call | flops 31457280 | bytes 43253760 | tf_op jit(solution)/shard_map/adamw/pallas_call | solution.py:700
  850.6 16.3 %adamw.17 = (bf16[2,1024,4096]{2,1,0:T(8,128)(2,1)}, bf16[2,1024,4096]{2,1,0:T(8,128)(2,1)}, bf16[2,4096,1024]{2,1,0:T(8,128)(2,1)}, f32[2,1024,4096]{2,1,0:T(8,...) custom-call(f32[4,8,128]{2,1,0:T(8,128)} %get-tuple-element.120.refs, ...), custom_call_target="tpu_custom_call", output_to_operand_aliasing={{0}: (17, {}), {1}: (18, {}), {2}: (19, {}), {3}: (20, {}),... | custom-call | flops 31457280 | bytes 43253760 | tf_op jit(solution)/shard_map/adamw/pallas_call | solution.py:700
  866.9 16.5 %adamw.18 = (bf16[2,1024,4096]{2,1,0:T(8,128)(2,1)}, bf16[2,1024,4096]{2,1,0:T(8,128)(2,1)}, bf16[2,4096,1024]{2,1,0:T(8,128)(2,1)}, f32[2,1024,4096]{2,1,0:T(8,...) custom-call(f32[4,8,128]{2,1,0:T(8,128)} %get-tuple-element.120.refs, ...), custom_call_target="tpu_custom_call", output_to_operand_aliasing={{0}: (17, {}), {1}: (18, {}), {2}: (19, {}), {3}: (20, {}),... | custom-call | flops 31457280 | bytes 43253760 | tf_op jit(solution)/shard_map/adamw/pallas_call | solution.py:700
  883.4 16.5 %adamw.19 = (bf16[2,1024,4096]{2,1,0:T(8,128)(2,1)}, bf16[2,1024,4096]{2,1,0:T(8,128)(2,1)}, bf16[2,4096,1024]{2,1,0:T(8,128)(2,1)}, f32[2,1024,4096]{2,1,0:T(8,...) custom-call(f32[4,8,128]{2,1,0:T(8,128)} %get-tuple-element.120.refs, ...), custom_call_target="tpu_custom_call", output_to_operand_aliasing={{0}: (17, {}), {1}: (18, {}), {2}: (19, {}), {3}: (20, {}),... | custom-call | flops 31457280 | bytes 43253760 | tf_op jit(solution)/shard_map/adamw/pallas_call | solution.py:700
  899.9 16.3 %adamw.20 = (bf16[2,1024,4096]{2,1,0:T(8,128)(2,1)}, bf16[2,1024,4096]{2,1,0:T(8,128)(2,1)}, bf16[2,4096,1024]{2,1,0:T(8,128)(2,1)}, f32[2,1024,4096]{2,1,0:T(8,...) custom-call(f32[4,8,128]{2,1,0:T(8,128)} %get-tuple-element.120.refs, ...), custom_call_target="tpu_custom_call", output_to_operand_aliasing={{0}: (17, {}), {1}: (18, {}), {2}: (19, {}), {3}: (20, {}),... | custom-call | flops 31457280 | bytes 43253760 | tf_op jit(solution)/shard_map/adamw/pallas_call | solution.py:700
  916.2 16.3 %adamw.21 = (bf16[2,1024,4096]{2,1,0:T(8,128)(2,1)}, bf16[2,1024,4096]{2,1,0:T(8,128)(2,1)}, bf16[2,4096,1024]{2,1,0:T(8,128)(2,1)}, f32[2,1024,4096]{2,1,0:T(8,...) custom-call(f32[4,8,128]{2,1,0:T(8,128)} %get-tuple-element.120.refs, ...), custom_call_target="tpu_custom_call", output_to_operand_aliasing={{0}: (17, {}), {1}: (18, {}), {2}: (19, {}), {3}: (20, {}),... | custom-call | flops 31457280 | bytes 43253760 | tf_op jit(solution)/shard_map/adamw/pallas_call | solution.py:700
  932.5 0.0 collective-permute-done.14.refs_7_.refs_5_.refs_3_
  932.5 13.8 %adamw.22 = (bf16[2,1024,4096]{2,1,0:T(8,128)(2,1)}, bf16[2,1024,4096]{2,1,0:T(8,128)(2,1)}, bf16[2,4096,1024]{2,1,0:T(8,128)(2,1)}, f32[2,1024,4096]{2,1,0:T(8,...) custom-call(f32[4,8,128]{2,1,0:T(8,128)} %get-tuple-element.120.refs, ...), custom_call_target="tpu_custom_call", output_to_operand_aliasing={{0}: (17, {}), {1}: (18, {}), {2}: (19, {}), {3}: (20, {}),... | custom-call | flops 25165824 | bytes 34603008 | tf_op jit(solution)/shard_map/adamw/pallas_call | solution.py:700
  946.3 0.0 collective-permute-done.9.refs_7_.refs_5_.refs_3_
  946.3 13.8 %adamw.23 = (bf16[2,1024,4096]{2,1,0:T(8,128)(2,1)}, bf16[2,1024,4096]{2,1,0:T(8,128)(2,1)}, bf16[2,4096,1024]{2,1,0:T(8,128)(2,1)}, f32[2,1024,4096]{2,1,0:T(8,...) custom-call(f32[4,8,128]{2,1,0:T(8,128)} %get-tuple-element.120.refs, ...), custom_call_target="tpu_custom_call", output_to_operand_aliasing={{0}: (17, {}), {1}: (18, {}), {2}: (19, {}), {3}: (20, {}),... | custom-call | flops 25165824 | bytes 34603008 | tf_op jit(solution)/shard_map/adamw/pallas_call | solution.py:700
  960.1 0.0 collective-permute-done.11.refs_7_.refs_5_
  960.1 13.7 %adamw.24 = (bf16[2,1024,4096]{2,1,0:T(8,128)(2,1)}, bf16[2,1024,4096]{2,1,0:T(8,128)(2,1)}, bf16[2,4096,1024]{2,1,0:T(8,128)(2,1)}, f32[2,1024,4096]{2,1,0:T(8,...) custom-call(f32[4,8,128]{2,1,0:T(8,128)} %get-tuple-element.120.refs, ...), custom_call_target="tpu_custom_call", output_to_operand_aliasing={{0}: (17, {}), {1}: (18, {}), {2}: (19, {}), {3}: (20, {}),... | custom-call | flops 25165824 | bytes 34603008 | tf_op jit(solution)/shard_map/adamw/pallas_call | solution.py:700
  973.7 13.7 %adamw.25 = (bf16[2,1024,4096]{2,1,0:T(8,128)(2,1)}, bf16[2,1024,4096]{2,1,0:T(8,128)(2,1)}, bf16[2,4096,1024]{2,1,0:T(8,128)(2,1)}, f32[2,1024,4096]{2,1,0:T(8,...) custom-call(f32[4,8,128]{2,1,0:T(8,128)} %get-tuple-element.120.refs, ...), custom_call_target="tpu_custom_call", output_to_operand_aliasing={{0}: (17, {}), {1}: (18, {}), {2}: (19, {}), {3}: (20, {}),... | custom-call | flops 25165824 | bytes 34603008 | tf_op jit(solution)/shard_map/adamw/pallas_call | solution.py:700
  (2 shorter events, 0.0 us)
Async XLA Ops:
  526.5 1.8 collective-permute-start
  528.4 42.1 %collective-permute-start.1 = (bf16[1,3,2,256,512]{4,3,2,1,0:T(8,128)(2,1)}, bf16[1,3,2,256,512]{4,3,2,1,0:T(8,128)(2,1)}, u32[]{:S(2)}, u32[]{:S(2)}) collective-permute-start(bf16[1,3,2,256,512]{4,3,2,1,0:T(8,128)(2,1)} %load.8.refs_2_), channel_id=1, source_target_pairs={{2,0},{5,7},{4,2},{3,5},{6,4},{1,3},{10,8},{13,15},{12,10},{11,13}... | collective-permute-start | bytes 4718600 | tf_op jit(solution)/shard_map/ppermute | solution.py:782
  570.5 22.6 %collective-permute-start.2 = (bf16[1,3,2,256,512]{4,3,2,1,0:T(8,128)(2,1)}, bf16[1,3,2,256,512]{4,3,2,1,0:T(8,128)(2,1)}, u32[]{:S(2)}, u32[]{:S(2)}) collective-permute-start(bf16[1,3,2,256,512]{4,3,2,1,0:T(8,128)(2,1)} %load.9.refs_4_.refs_2_), channel_id=1, source_target_pairs={{2,0},{5,7},{4,2},{3,5},{6,4},{1,3},{10,8},{13,15},{12,10},{11,13}... | collective-permute-start | bytes 4718600 | tf_op jit(solution)/shard_map/ppermute | solution.py:782
  593.2 22.6 %collective-permute-start.3 = (bf16[1,3,2,256,512]{4,3,2,1,0:T(8,128)(2,1)}, bf16[1,3,2,256,512]{4,3,2,1,0:T(8,128)(2,1)}, u32[]{:S(2)}, u32[]{:S(2)}) collective-permute-start(bf16[1,3,2,256,512]{4,3,2,1,0:T(8,128)(2,1)} %load.10.refs_6_.refs_4_.refs_2_), channel_id=1, source_target_pairs={{2,0},{5,7},{4,2},{3,5},{6,4},{1,3},{10,8},{13,15},{12,10},{11,13}... | collective-permute-start | bytes 4718600 | tf_op jit(solution)/shard_map/ppermute | solution.py:782
  615.9 22.6 %collective-permute-start.4 = (bf16[1,3,2,256,512]{4,3,2,1,0:T(8,128)(2,1)}, bf16[1,3,2,256,512]{4,3,2,1,0:T(8,128)(2,1)}, u32[]{:S(2)}, u32[]{:S(2)}) collective-permute-start(bf16[1,3,2,256,512]{4,3,2,1,0:T(8,128)(2,1)} %load.11.refs_6_.refs_4_.refs_2_), channel_id=1, source_target_pairs={{2,0},{5,7},{4,2},{3,5},{6,4},{1,3},{10,8},{13,15},{12,10},{11,13}... | collective-permute-start | bytes 4718600 | tf_op jit(solution)/shard_map/ppermute | solution.py:782
  638.6 22.6 %collective-permute-start.5 = (bf16[1,3,2,256,512]{4,3,2,1,0:T(8,128)(2,1)}, bf16[1,3,2,256,512]{4,3,2,1,0:T(8,128)(2,1)}, u32[]{:S(2)}, u32[]{:S(2)}) collective-permute-start(bf16[1,3,2,256,512]{4,3,2,1,0:T(8,128)(2,1)} %load.12.refs_6_.refs_4_.refs_2_), channel_id=1, source_target_pairs={{2,0},{5,7},{4,2},{3,5},{6,4},{1,3},{10,8},{13,15},{12,10},{11,13}... | collective-permute-start | bytes 4718600 | tf_op jit(solution)/shard_map/ppermute | solution.py:782
  661.3 22.6 %collective-permute-start.6 = (bf16[1,3,2,256,512]{4,3,2,1,0:T(8,128)(2,1)}, bf16[1,3,2,256,512]{4,3,2,1,0:T(8,128)(2,1)}, u32[]{:S(2)}, u32[]{:S(2)}) collective-permute-start(bf16[1,3,2,256,512]{4,3,2,1,0:T(8,128)(2,1)} %load.13.refs_6_.refs_4_.refs_2_), channel_id=1, source_target_pairs={{2,0},{5,7},{4,2},{3,5},{6,4},{1,3},{10,8},{13,15},{12,10},{11,13}... | collective-permute-start | bytes 4718600 | tf_op jit(solution)/shard_map/ppermute | solution.py:782
  684.0 22.6 %collective-permute-start.7 = (bf16[1,3,2,256,512]{4,3,2,1,0:T(8,128)(2,1)}, bf16[1,3,2,256,512]{4,3,2,1,0:T(8,128)(2,1)}, u32[]{:S(2)}, u32[]{:S(2)}) collective-permute-start(bf16[1,3,2,256,512]{4,3,2,1,0:T(8,128)(2,1)} %load.14.refs_6_.refs_4_.refs_2_), channel_id=1, source_target_pairs={{2,0},{5,7},{4,2},{3,5},{6,4},{1,3},{10,8},{13,15},{12,10},{11,13}... | collective-permute-start | bytes 4718600 | tf_op jit(solution)/shard_map/ppermute | solution.py:782
  706.7 22.6 %collective-permute-start.8 = (bf16[1,3,2,256,512]{4,3,2,1,0:T(8,128)(2,1)}, bf16[1,3,2,256,512]{4,3,2,1,0:T(8,128)(2,1)}, u32[]{:S(2)}, u32[]{:S(2)}) collective-permute-start(bf16[1,3,2,256,512]{4,3,2,1,0:T(8,128)(2,1)} %load.15.refs_6_.refs_4_.refs_2_), channel_id=1, source_target_pairs={{2,0},{5,7},{4,2},{3,5},{6,4},{1,3},{10,8},{13,15},{12,10},{11,13}... | collective-permute-start | bytes 4718600 | tf_op jit(solution)/shard_map/ppermute | solution.py:782
  708.0 27.6 %collective-permute-start.21 = (bf16[1,3,2,256,512]{4,3,2,1,0:T(8,128)(2,1)}, bf16[1,3,2,256,512]{4,3,2,1,0:T(8,128)(2,1)}, u32[]{:S(2)}, u32[]{:S(2)}) collective-permute-start(bf16[1,3,2,256,512]{4,3,2,1,0:T(8,128)(2,1)} %load.8.refs_2_), channel_id=1, source_target_pairs={{2,3},{5,4},{4,5},{3,2},{10,11},{13,12},{12,13},{11,10},{18,19},{2... | collective-permute-start | bytes 4718600 | tf_op jit(solution)/shard_map/ppermute | solution.py:784
  709.8 28.2 %collective-permute-start.20 = (bf16[1,3,2,256,512]{4,3,2,1,0:T(8,128)(2,1)}, bf16[1,3,2,256,512]{4,3,2,1,0:T(8,128)(2,1)}, u32[]{:S(2)}, u32[]{:S(2)}) collective-permute-start(bf16[1,3,2,256,512]{4,3,2,1,0:T(8,128)(2,1)} %load.9.refs_4_.refs_2_), channel_id=1, source_target_pairs={{0,1},{7,6},{2,3},{5,4},{4,5},{3,2},{8,9},{15,14},{10,11},{13,12},... | collective-permute-start | bytes 4718600 | tf_op jit(solution)/shard_map/ppermute | solution.py:784
  729.3 22.6 %collective-permute-start.10 = (bf16[1,3,2,256,512]{4,3,2,1,0:T(8,128)(2,1)}, bf16[1,3,2,256,512]{4,3,2,1,0:T(8,128)(2,1)}, u32[]{:S(2)}, u32[]{:S(2)}) collective-permute-start(bf16[1,3,2,256,512]{4,3,2,1,0:T(8,128)(2,1)} %collective-permute-done.8.refs_6_.refs_4_.refs_2_), channel_id=1, source_target_pairs={{2,0},{5,7},{4,2},{3,5},{10,8},{13,15},{12,10},{11,13},{18,16},{21... | collective-permute-start | bytes 4718600 | tf_op jit(solution)/shard_map/ppermute | solution.py:782
  730.6 22.6 %collective-permute-start.19 = (bf16[1,3,2,256,512]{4,3,2,1,0:T(8,128)(2,1)}, bf16[1,3,2,256,512]{4,3,2,1,0:T(8,128)(2,1)}, u32[]{:S(2)}, u32[]{:S(2)}) collective-permute-start(bf16[1,3,2,256,512]{4,3,2,1,0:T(8,128)(2,1)} %load.10.refs_6_.refs_4_.refs_2_), channel_id=1, source_target_pairs={{0,1},{7,6},{2,3},{5,4},{4,5},{3,2},{8,9},{15,14},{10,11},{13,12},... | collective-permute-start | bytes 4718600 | tf_op jit(solution)/shard_map/ppermute | solution.py:784
  733.1 22.6 %collective-permute-start.18 = (bf16[1,3,2,256,512]{4,3,2,1,0:T(8,128)(2,1)}, bf16[1,3,2,256,512]{4,3,2,1,0:T(8,128)(2,1)}, u32[]{:S(2)}, u32[]{:S(2)}) collective-permute-start(bf16[1,3,2,256,512]{4,3,2,1,0:T(8,128)(2,1)} %load.11.refs_6_.refs_4_.refs_2_), channel_id=1, source_target_pairs={{0,1},{7,6},{2,3},{5,4},{4,5},{3,2},{8,9},{15,14},{10,11},{13,12},... | collective-permute-start | bytes 4718600 | tf_op jit(solution)/shard_map/ppermute | solution.py:784
  735.6 22.6 %collective-permute-start.17 = (bf16[1,3,2,256,512]{4,3,2,1,0:T(8,128)(2,1)}, bf16[1,3,2,256,512]{4,3,2,1,0:T(8,128)(2,1)}, u32[]{:S(2)}, u32[]{:S(2)}) collective-permute-start(bf16[1,3,2,256,512]{4,3,2,1,0:T(8,128)(2,1)} %load.12.refs_6_.refs_4_.refs_2_), channel_id=1, source_target_pairs={{0,1},{7,6},{2,3},{5,4},{4,5},{3,2},{8,9},{15,14},{10,11},{13,12},... | collective-permute-start | bytes 4718600 | tf_op jit(solution)/shard_map/ppermute | solution.py:784
  738.0 22.6 %collective-permute-start.16 = (bf16[1,3,2,256,512]{4,3,2,1,0:T(8,128)(2,1)}, bf16[1,3,2,256,512]{4,3,2,1,0:T(8,128)(2,1)}, u32[]{:S(2)}, u32[]{:S(2)}) collective-permute-start(bf16[1,3,2,256,512]{4,3,2,1,0:T(8,128)(2,1)} %load.13.refs_6_.refs_4_.refs_2_), channel_id=1, source_target_pairs={{0,1},{7,6},{2,3},{5,4},{4,5},{3,2},{8,9},{15,14},{10,11},{13,12},... | collective-permute-start | bytes 4718600 | tf_op jit(solution)/shard_map/ppermute | solution.py:784
  751.9 22.6 %collective-permute-start.12 = (bf16[1,3,2,256,512]{4,3,2,1,0:T(8,128)(2,1)}, bf16[1,3,2,256,512]{4,3,2,1,0:T(8,128)(2,1)}, u32[]{:S(2)}, u32[]{:S(2)}) collective-permute-start(bf16[1,3,2,256,512]{4,3,2,1,0:T(8,128)(2,1)} %collective-permute-done.10.refs_6_.refs_4_), channel_id=1, source_target_pairs={{2,0},{5,7},{10,8},{13,15},{18,16},{21,23},{26,24},{29,31}} | collective-permute-start | bytes 4718600 | tf_op jit(solution)/shard_map/ppermute | solution.py:782
  753.2 163.0 %collective-permute-start.15 = (bf16[1,3,2,256,512]{4,3,2,1,0:T(8,128)(2,1)}, bf16[1,3,2,256,512]{4,3,2,1,0:T(8,128)(2,1)}, u32[]{:S(2)}, u32[]{:S(2)}) collective-permute-start(bf16[1,3,2,256,512]{4,3,2,1,0:T(8,128)(2,1)} %load.14.refs_6_.refs_4_.refs_2_), channel_id=1, source_target_pairs={{0,1},{7,6},{2,3},{5,4},{4,5},{3,2},{8,9},{15,14},{10,11},{13,12},... | collective-permute-start | bytes 4718600 | tf_op jit(solution)/shard_map/ppermute | solution.py:784
  755.7 176.8 %collective-permute-start.14 = (bf16[1,3,2,256,512]{4,3,2,1,0:T(8,128)(2,1)}, bf16[1,3,2,256,512]{4,3,2,1,0:T(8,128)(2,1)}, u32[]{:S(2)}, u32[]{:S(2)}) collective-permute-start(bf16[1,3,2,256,512]{4,3,2,1,0:T(8,128)(2,1)} %load.15.refs_6_.refs_4_.refs_2_), channel_id=1, source_target_pairs={{0,1},{7,6},{2,3},{5,4},{4,5},{3,2},{8,9},{15,14},{10,11},{13,12},... | collective-permute-start | bytes 4718600 | tf_op jit(solution)/shard_map/ppermute | solution.py:784
  758.1 188.1 %collective-permute-start.9 = (bf16[1,3,2,256,512]{4,3,2,1,0:T(8,128)(2,1)}, bf16[1,3,2,256,512]{4,3,2,1,0:T(8,128)(2,1)}, u32[]{:S(2)}, u32[]{:S(2)}) collective-permute-start(bf16[1,3,2,256,512]{4,3,2,1,0:T(8,128)(2,1)} %collective-permute-done.8.refs_6_.refs_4_.refs_2_), channel_id=1, source_target_pairs={{0,1},{7,6},{2,3},{5,4},{4,5},{3,2},{8,9},{15,14},{10,11},{13,12},... | collective-permute-start | bytes 4718600 | tf_op jit(solution)/shard_map/ppermute | solution.py:784
  760.6 199.5 %collective-permute-start.11 = (bf16[1,3,2,256,512]{4,3,2,1,0:T(8,128)(2,1)}, bf16[1,3,2,256,512]{4,3,2,1,0:T(8,128)(2,1)}, u32[]{:S(2)}, u32[]{:S(2)}) collective-permute-start(bf16[1,3,2,256,512]{4,3,2,1,0:T(8,128)(2,1)} %collective-permute-done.10.refs_6_.refs_4_), channel_id=1, source_target_pairs={{0,1},{7,6},{2,3},{5,4},{8,9},{15,14},{10,11},{13,12},{16,17},{23,... | collective-permute-start | bytes 4718600 | tf_op jit(solution)/shard_map/ppermute | solution.py:784
  774.5 199.2 %collective-permute-start.13 = (bf16[1,3,2,256,512]{4,3,2,1,0:T(8,128)(2,1)}, bf16[1,3,2,256,512]{4,3,2,1,0:T(8,128)(2,1)}, u32[]{:S(2)}, u32[]{:S(2)}) collective-permute-start(bf16[1,3,2,256,512]{4,3,2,1,0:T(8,128)(2,1)} %collective-permute-done.12.refs_6_), channel_id=1, source_target_pairs={{0,1},{7,6},{8,9},{15,14},{16,17},{23,22},{24,25},{31,30}} | collective-permute-start | bytes 4718600 | tf_op jit(solution)/shard_map/ppermute | solution.py:784
